TPU v7x, 32 devices: a whole 2x2x4 slice. The times are simulated.
32 devices in a mesh: fsdp: 32 (over z, y, x, core).
Axes of the slice: x: 2, y: 2, z: 4, core: 2. Of those that a mesh axis runs over, the one named last changes fastest.
Arguments:
- language: bfloat16 [384, 20, 768], P('fsdp'), may hold values from -6 to 6
- vision: bfloat16 [384, 16, 768], P('fsdp'), may hold values from -6 to 6
- cross_project: bfloat16 [3, 768, 768], P(None, 'fsdp'), may hold values from -0.21875 to 0.21875
- cross_output: bfloat16 [768, 768], P('fsdp'), may hold values from -0.4375 to 0.4375
- cross_biases: bfloat16 [4, 768], P(None, 'fsdp'), may hold values from -3 to 3
- cross_gain: bfloat16 [768], P('fsdp'), may hold values from 0.099609375 to 1.8984375
- self_project: bfloat16 [2, 3, 768, 768], P(None, None, 'fsdp'), may hold values from -0.21875 to 0.21875
- self_output: bfloat16 [2, 768, 768], P(None, 'fsdp'), may hold values from -0.4375 to 0.4375
- self_biases: bfloat16 [2, 4, 768], P(None, None, 'fsdp'), may hold values from -3 to 3
- self_gain: bfloat16 [2, 768], P(None, 'fsdp'), may hold values from 0.099609375 to 1.8984375
- feed_up: bfloat16 [2, 768, 3072], P(None, 'fsdp'), may hold values from -0.21875 to 0.21875
- feed_up_bias: bfloat16 [2, 3072], P(None, 'fsdp'), may hold values from -3 to 3
- feed_down: bfloat16 [2, 3072, 768], P(None, 'fsdp'), may hold values from -0.109375 to 0.109375
- feed_biases: bfloat16 [2, 2, 768], P(None, None, 'fsdp'), may hold values from -3 to 3
- feed_gain: bfloat16 [2, 768], P(None, 'fsdp'), may hold values from 0.099609375 to 1.8984375
- language_cotangent: bfloat16 [384, 20, 768], P('fsdp'), may hold values from -6 to 6
- vision_cotangent: bfloat16 [384, 16, 768], P('fsdp'), may hold values from -6 to 6
- task_flags: int32 [384, 2], P('fsdp'), may hold values 0 or 1
Outputs:
- language_out: bfloat16 [384, 20, 768], P('fsdp')
- vision_out: bfloat16 [384, 16, 768], P('fsdp')
- language_grad: float32 [384, 20, 768], P('fsdp')
- vision_grad: float32 [384, 16, 768], P('fsdp')
- cross_project_grad: float32 [3, 768, 768], P(None, 'fsdp')
- cross_output_grad: float32 [768, 768], P('fsdp')
- cross_biases_grad: float32 [4, 768], P(None, 'fsdp')
- cross_gain_grad: float32 [768], P('fsdp')
- self_project_grad: float32 [2, 3, 768, 768], P(None, None, 'fsdp')
- self_output_grad: float32 [2, 768, 768], P(None, 'fsdp')
- self_biases_grad: float32 [2, 4, 768], P(None, None, 'fsdp')
- self_gain_grad: float32 [2, 768], P(None, 'fsdp')
- feed_up_grad: float32 [2, 768, 3072], P(None, 'fsdp')
- feed_up_bias_grad: float32 [2, 3072], P(None, 'fsdp')
- feed_down_grad: float32 [2, 3072, 768], P(None, 'fsdp')
- feed_biases_grad: float32 [2, 2, 768], P(None, None, 'fsdp')
- feed_gain_grad: float32 [2, 768], P(None, 'fsdp')
All inputs are finite; a program needn't handle non-finite values. No bound on the sum of `task_flags` on one device may be relied on, other than what follows from the above.
Results may differ from a plain program's by a relative error of at most 0.02.
Values may be sent and summed in bfloat16 or wider, within the bound.
A program may use at most 256 MiB of HBM per device.

v0:
```python
import jax
import jax.numpy as jnp
from jax import lax
from jax.sharding import PartitionSpec as P

HEAD = 64


epsilon = 1e-12
root_half = 0.7071067811865476
root_two_pi = 2.5066282746310002


def layer_norm(hidden, gain, shift):
    average = jnp.mean(hidden, axis=-1, keepdims=True)
    centred = hidden - average
    inverse = lax.rsqrt(jnp.mean(centred * centred, axis=-1, keepdims=True) + epsilon)
    normed = centred * inverse
    return (normed * gain + shift, normed, inverse)


def norm_back(upstream, normed, inverse, gain):
    scaled = upstream * gain
    centred = scaled - jnp.mean(scaled, axis=-1, keepdims=True)
    result = inverse * (centred - normed * jnp.mean(scaled * normed, axis=-1, keepdims=True))
    return (result, jnp.sum(upstream * normed, axis=0), jnp.sum(upstream, axis=0))


def weight_grad(left_rows, right_rows):
    return jnp.einsum("na,nb->ab", left_rows, right_rows, preferred_element_type=jnp.float32)


def row_grad(upstream, weight):
    return jnp.einsum("nb,ab->na", upstream, weight, preferred_element_type=jnp.float32)


def three_ways(block_of_rows, incoming_weight, biases):
    projected_rows = jnp.einsum(
        "vf,zfk->zvk", block_of_rows, incoming_weight, preferred_element_type=jnp.float32
    )
    query = (projected_rows[0] + biases[0]).astype(jnp.bfloat16)
    keys = projected_rows[1].astype(jnp.bfloat16)
    values = (projected_rows[2] + biases[1]).astype(jnp.bfloat16)
    return (query, keys, values)


def split_heads(block_of_rows, item_count):
    return block_of_rows.reshape(
        item_count, block_of_rows.shape[0] // item_count, block_of_rows.shape[1] // HEAD, HEAD
    )


def scores_of(query, keys, item_count):
    return jnp.einsum(
        "bqhd,bkhd->bhqk",
        split_heads(query, item_count),
        split_heads(keys, item_count),
        preferred_element_type=jnp.float32,
    ) * HEAD ** (-0.5)


def attend(query, keys, values, item_count):
    scores = scores_of(query, keys, item_count)
    highest = jnp.max(scores, axis=-1, keepdims=True)
    powers = jnp.exp(scores - highest)
    totals = jnp.sum(powers, axis=-1, keepdims=True)
    weights = (powers / totals).astype(jnp.bfloat16)
    context = jnp.einsum(
        "bhqk,bkhd->bqhd",
        weights,
        split_heads(values, item_count),
        preferred_element_type=jnp.float32,
    )
    return (context.reshape(query.shape).astype(jnp.bfloat16), highest + jnp.log(totals))


def attend_back(context_grad, query, keys, values, log_total, item_count):
    weights = jnp.exp(scores_of(query, keys, item_count) - log_total)
    upstream = split_heads(context_grad, item_count)
    gradient_weights = jnp.einsum(
        "bqhd,bkhd->bhqk",
        upstream,
        split_heads(values, item_count),
        preferred_element_type=jnp.float32,
    )
    values_grad = jnp.einsum(
        "bhqk,bqhd->bkhd",
        weights.astype(jnp.bfloat16),
        upstream,
        preferred_element_type=jnp.float32,
    )
    scores_grad = (
        weights * (gradient_weights - jnp.sum(weights * gradient_weights, axis=-1, keepdims=True))
    ).astype(jnp.bfloat16)
    query_grad = jnp.einsum(
        "bhqk,bkhd->bqhd",
        scores_grad,
        split_heads(keys, item_count),
        preferred_element_type=jnp.float32,
    ) * HEAD ** (-0.5)
    keys_grad = jnp.einsum(
        "bhqk,bqhd->bkhd",
        scores_grad,
        split_heads(query, item_count),
        preferred_element_type=jnp.float32,
    ) * HEAD ** (-0.5)
    return (
        query_grad.reshape(query.shape).astype(jnp.bfloat16),
        keys_grad.reshape(keys.shape).astype(jnp.bfloat16),
        values_grad.reshape(values.shape).astype(jnp.bfloat16),
    )


def project_back(block_of_rows, pieces, incoming_weight):
    stacked_pieces = jnp.stack(pieces)
    gradient_rows = jnp.einsum(
        "rzi,rti->zt", stacked_pieces, incoming_weight, preferred_element_type=jnp.float32
    )
    gradient_weights = jnp.einsum(
        "ti,gtx->gix", block_of_rows, stacked_pieces, preferred_element_type=jnp.float32
    )
    biases_grad = jnp.stack(
        [
            jnp.sum(pieces[0].astype(jnp.float32), axis=0),
            jnp.sum(pieces[2].astype(jnp.float32), axis=0),
        ]
    )
    return (gradient_rows, gradient_weights, biases_grad)


def gelu_of(prior_input):
    return prior_input * (lax.erf(prior_input * root_half) + 1.0) * 0.5


def gelu_slope(prior_input):
    return (lax.erf(prior_input * root_half) + 1.0) * 0.5 + prior_input * jnp.exp(
        -0.5 * prior_input * prior_input
    ) / root_two_pi


def to_front(terms, dims):
    return [jnp.moveaxis(term, where, 0) for term, where in zip(terms, dims)]


def to_place(shards, dims):
    return tuple((jnp.moveaxis(shard, 0, where) for shard, where in zip(shards, dims)))


def per_device(
    language,
    vision,
    cross_project,
    cross_output,
    cross_biases,
    cross_gain,
    self_project,
    self_output,
    self_biases,
    self_gain,
    feed_up,
    feed_up_bias,
    feed_down,
    feed_biases,
    feed_gain,
    language_cotangent,
    vision_cotangent,
    task_flags,
):
    item_count = language.shape[0]
    model_width = language.shape[2]
    streams = (language.reshape(-1, model_width), vision.reshape(-1, model_width))
    cotangents = (language_cotangent, vision_cotangent)
    cross_dims = (1, 0, 1, 0)
    self_dims = (2, 1, 2, 1)
    feed_dims = (1, 1, 1, 2, 1)
    cross_full = (
        lax.all_gather(cross_project, "fsdp", axis=1, tiled=True),
        lax.all_gather(cross_output, "fsdp", axis=0, tiled=True),
        lax.all_gather(cross_biases, "fsdp", axis=1, tiled=True),
        lax.all_gather(cross_gain, "fsdp", axis=0, tiled=True),
    )
    cross_vector = cross_full[2].astype(jnp.float32)
    projected_rows = [
        three_ways(block_of_rows, cross_full[0], cross_vector) for block_of_rows in streams
    ]
    attended = (
        attend(projected_rows[0][0], projected_rows[1][1], projected_rows[1][2], item_count),
        attend(projected_rows[1][0], projected_rows[0][1], projected_rows[0][2], item_count),
    )
    first = []
    for stream in range(2):
        branch = (
            jnp.dot(attended[stream][0], cross_full[1], preferred_element_type=jnp.float32)
            + cross_vector[2]
        )
        first.append(
            layer_norm(
                streams[stream].astype(jnp.float32) + branch,
                cross_full[3].astype(jnp.float32),
                cross_vector[3],
            )
        )
    self_full = (
        lax.all_gather(self_project, "fsdp", axis=2, tiled=True),
        lax.all_gather(self_output, "fsdp", axis=1, tiled=True),
        lax.all_gather(self_biases, "fsdp", axis=2, tiled=True),
        lax.all_gather(self_gain, "fsdp", axis=1, tiled=True),
    )
    self_vector = self_full[2].astype(jnp.float32)
    second = []
    self_kept = []
    for stream in range(2):
        rows_in = first[stream][0].astype(jnp.bfloat16)
        query, keys, values = three_ways(rows_in, self_full[0][stream], self_vector[stream])
        context, log_total = attend(query, keys, values, item_count)
        branch = (
            jnp.dot(context, self_full[1][stream], preferred_element_type=jnp.float32)
            + self_vector[stream][2]
        )
        second.append(
            layer_norm(
                first[stream][0] + branch,
                self_full[3][stream].astype(jnp.float32),
                self_vector[stream][3],
            )
        )
        self_kept.append((rows_in, query, keys, values, context, log_total))
    feed_full = (
        lax.all_gather(feed_up, "fsdp", axis=1, tiled=True),
        lax.all_gather(feed_up_bias, "fsdp", axis=1, tiled=True),
        lax.all_gather(feed_down, "fsdp", axis=1, tiled=True),
        lax.all_gather(feed_biases, "fsdp", axis=2, tiled=True),
        lax.all_gather(feed_gain, "fsdp", axis=1, tiled=True),
    )
    feed_vector = feed_full[3].astype(jnp.float32)
    third = []
    feed_kept = []
    for stream in range(2):
        rows_in = second[stream][0].astype(jnp.bfloat16)
        prior_input = jnp.dot(
            rows_in, feed_full[0][stream], preferred_element_type=jnp.float32
        ) + feed_full[1][stream].astype(jnp.float32)
        active = gelu_of(prior_input).astype(jnp.bfloat16)
        branch = (
            jnp.dot(active, feed_full[2][stream], preferred_element_type=jnp.float32)
            + feed_vector[stream][0]
        )
        third.append(
            layer_norm(
                second[stream][0] + branch,
                feed_full[4][stream].astype(jnp.float32),
                feed_vector[stream][1],
            )
        )
        feed_kept.append((rows_in, prior_input, active))
    feed_again = (
        lax.all_gather(feed_up, "fsdp", axis=1, tiled=True),
        lax.all_gather(feed_up_bias, "fsdp", axis=1, tiled=True),
        lax.all_gather(feed_down, "fsdp", axis=1, tiled=True),
        lax.all_gather(feed_biases, "fsdp", axis=2, tiled=True),
        lax.all_gather(feed_gain, "fsdp", axis=1, tiled=True),
    )
    feed_terms = [[], [], [], [], []]
    into_second = []
    for stream in range(2):
        masking = task_flags[:, stream].astype(jnp.float32)[:, None, None]
        upstream = (cotangents[stream].astype(jnp.float32) * masking).reshape(-1, model_width)
        summed, gain_term, shift_term = norm_back(
            upstream, third[stream][1], third[stream][2], feed_again[4][stream].astype(jnp.float32)
        )
        branch_grad = summed.astype(jnp.bfloat16)
        rows_in, prior_input, active = feed_kept[stream]
        before_grad = (
            row_grad(branch_grad, feed_again[2][stream]) * gelu_slope(prior_input)
        ).astype(jnp.bfloat16)
        feed_terms[0].append(weight_grad(rows_in, before_grad))
        feed_terms[1].append(jnp.sum(before_grad.astype(jnp.float32), axis=0))
        feed_terms[2].append(weight_grad(active, branch_grad))
        feed_terms[3].append(
            jnp.stack([jnp.sum(branch_grad.astype(jnp.float32), axis=0), shift_term])
        )
        feed_terms[4].append(gain_term)
        into_second.append(summed + row_grad(before_grad, feed_again[0][stream]))
    feed_sums = to_front([jnp.stack(collected) for collected in feed_terms], feed_dims)
    feed_shards = to_place(
        (
            lax.psum_scatter(feed_sums[0], "fsdp", scatter_dimension=0, tiled=True),
            lax.psum_scatter(feed_sums[1], "fsdp", scatter_dimension=0, tiled=True),
            lax.psum_scatter(feed_sums[2], "fsdp", scatter_dimension=0, tiled=True),
            lax.psum_scatter(feed_sums[3], "fsdp", scatter_dimension=0, tiled=True),
            lax.psum_scatter(feed_sums[4], "fsdp", scatter_dimension=0, tiled=True),
        ),
        feed_dims,
    )
    self_again = (
        lax.all_gather(self_project, "fsdp", axis=2, tiled=True),
        lax.all_gather(self_output, "fsdp", axis=1, tiled=True),
        lax.all_gather(self_biases, "fsdp", axis=2, tiled=True),
        lax.all_gather(self_gain, "fsdp", axis=1, tiled=True),
    )
    self_terms = [[], [], [], []]
    into_first = []
    for stream in range(2):
        summed, gain_term, shift_term = norm_back(
            into_second[stream],
            second[stream][1],
            second[stream][2],
            self_again[3][stream].astype(jnp.float32),
        )
        branch_grad = summed.astype(jnp.bfloat16)
        rows_in, query, keys, values, context, log_total = self_kept[stream]
        context_grad = row_grad(branch_grad, self_again[1][stream]).astype(jnp.bfloat16)
        pieces = attend_back(context_grad, query, keys, values, log_total, item_count)
        gradient_rows, project_term, bias_term = project_back(
            rows_in, pieces, self_again[0][stream]
        )
        self_terms[0].append(project_term)
        self_terms[1].append(weight_grad(context, branch_grad))
        self_terms[2].append(
            jnp.stack(
                [
                    bias_term[0],
                    bias_term[1],
                    jnp.sum(branch_grad.astype(jnp.float32), axis=0),
                    shift_term,
                ]
            )
        )
        self_terms[3].append(gain_term)
        into_first.append(summed + gradient_rows)
    self_sums = to_front([jnp.stack(collected) for collected in self_terms], self_dims)
    self_shards = to_place(
        (
            lax.psum_scatter(self_sums[0], "fsdp", scatter_dimension=0, tiled=True),
            lax.psum_scatter(self_sums[1], "fsdp", scatter_dimension=0, tiled=True),
            lax.psum_scatter(self_sums[2], "fsdp", scatter_dimension=0, tiled=True),
            lax.psum_scatter(self_sums[3], "fsdp", scatter_dimension=0, tiled=True),
        ),
        self_dims,
    )
    cross_again = (
        lax.all_gather(cross_project, "fsdp", axis=1, tiled=True),
        lax.all_gather(cross_output, "fsdp", axis=0, tiled=True),
        lax.all_gather(cross_biases, "fsdp", axis=1, tiled=True),
        lax.all_gather(cross_gain, "fsdp", axis=0, tiled=True),
    )
    cross_scale = cross_again[3].astype(jnp.float32)
    normed_back = [
        norm_back(into_first[stream], first[stream][1], first[stream][2], cross_scale)
        for stream in range(2)
    ]
    branch_grads = [outcome[0].astype(jnp.bfloat16) for outcome in normed_back]
    context_grads = [
        row_grad(upstream, cross_again[1]).astype(jnp.bfloat16) for upstream in branch_grads
    ]
    language_pieces = attend_back(
        context_grads[0],
        projected_rows[0][0],
        projected_rows[1][1],
        projected_rows[1][2],
        attended[0][1],
        item_count,
    )
    vision_pieces = attend_back(
        context_grads[1],
        projected_rows[1][0],
        projected_rows[0][1],
        projected_rows[0][2],
        attended[1][1],
        item_count,
    )
    language_rows, language_project, language_bias = project_back(
        streams[0], (language_pieces[0], vision_pieces[1], vision_pieces[2]), cross_again[0]
    )
    vision_rows, vision_project, vision_bias = project_back(
        streams[1], (vision_pieces[0], language_pieces[1], language_pieces[2]), cross_again[0]
    )
    cross_sums = to_front(
        [
            language_project + vision_project,
            weight_grad(attended[0][0], branch_grads[0])
            + weight_grad(attended[1][0], branch_grads[1]),
            jnp.stack(
                [
                    language_bias[0] + vision_bias[0],
                    language_bias[1] + vision_bias[1],
                    jnp.sum(branch_grads[0].astype(jnp.float32), axis=0)
                    + jnp.sum(branch_grads[1].astype(jnp.float32), axis=0),
                    normed_back[0][2] + normed_back[1][2],
                ]
            ),
            normed_back[0][1] + normed_back[1][1],
        ],
        cross_dims,
    )
    language_grad = (normed_back[0][0] + language_rows).reshape(language.shape)
    vision_grad = (normed_back[1][0] + vision_rows).reshape(vision.shape)
    cross_shards = to_place(
        (
            lax.psum_scatter(cross_sums[0], "fsdp", scatter_dimension=0, tiled=True),
            lax.psum_scatter(cross_sums[1], "fsdp", scatter_dimension=0, tiled=True),
            lax.psum_scatter(cross_sums[2], "fsdp", scatter_dimension=0, tiled=True),
            lax.psum_scatter(cross_sums[3], "fsdp", scatter_dimension=0, tiled=True),
        ),
        cross_dims,
    )
    shards = tuple(cross_shards) + tuple(self_shards) + tuple(feed_shards)
    language_out = third[0][0].astype(jnp.bfloat16).reshape(language.shape)
    vision_out = third[1][0].astype(jnp.bfloat16).reshape(vision.shape)
    return (
        language_out,
        vision_out,
        language_grad,
        vision_grad,
        shards[0],
        shards[1],
        shards[2],
        shards[3],
        shards[4],
        shards[5],
        shards[6],
        shards[7],
        shards[8],
        shards[9],
        shards[10],
        shards[11],
        shards[12],
    )


def solution(mesh):
    placed = (
        P("fsdp", None, None),
        P("fsdp", None, None),
        P(None, "fsdp", None),
        P("fsdp", None),
        P(None, "fsdp"),
        P("fsdp"),
        P(None, None, "fsdp", None),
        P(None, "fsdp", None),
        P(None, None, "fsdp"),
        P(None, "fsdp"),
        P(None, "fsdp", None),
        P(None, "fsdp"),
        P(None, "fsdp", None),
        P(None, None, "fsdp"),
        P(None, "fsdp"),
        P("fsdp", None, None),
        P("fsdp", None, None),
        P("fsdp", None),
    )
    return jax.shard_map(
        per_device,
        mesh=mesh,
        in_specs=placed,
        out_specs=(
            P("fsdp", None, None),
            P("fsdp", None, None),
            P("fsdp", None, None),
            P("fsdp", None, None),
            P(None, "fsdp", None),
            P("fsdp", None),
            P(None, "fsdp"),
            P("fsdp"),
            P(None, None, "fsdp", None),
            P(None, "fsdp", None),
            P(None, None, "fsdp"),
            P(None, "fsdp"),
            P(None, "fsdp", None),
            P(None, "fsdp"),
            P(None, "fsdp", None),
            P(None, None, "fsdp"),
            P(None, "fsdp"),
        ),
        check_vma=False,
    )
```

profile of v0, /device:TPU:0, one launch (start us, length us, event | category | flops | bytes accessed | tf_op | source)
XLA Modules:
  0.0 1681.0 jit_solution(4094386509656926172)
XLA Ops:
  14.1 42.6 %all-reduce = bf16[768]{0:T(1024)(128)(2,1)S(1)} all-reduce(bf16[768]{0:T(1024)(128)(2,1)S(1)} %dynamic-update-slice), channel_id=1, replica_groups=mesh['fsdp'=32] {'fsdp'}, use_global_device_ids=true, to_apply=%add | all-reduce | flops 768 | bytes 3072
  57.5 39.9 %all-gather.1 = bf16[32,24,2]{1,2,0:T(2,128)(2,1)S(1)} all-gather(bf16[1,24,2]{1,2,0:T(2,128)(2,1)S(1)} %bitcast.330), channel_id=1, replica_groups=mesh['fsdp'=32] {'fsdp'}, dimensions={0}, use_global_device_ids=true | all-gather | bytes 3168 | tf_op jit(solution)/shard_map/all_gather | solution.py:207
  97.6 36.7 %all-gather.2 = bf16[32,96,2]{1,2,0:T(2,128)(2,1)S(1)} all-gather(bf16[1,96,2]{1,2,0:T(2,128)(2,1)S(1)} %bitcast.331), channel_id=1, replica_groups=mesh['fsdp'=32] {'fsdp'}, dimensions={0}, use_global_device_ids=true | all-gather | bytes 12672 | tf_op jit(solution)/shard_map/all_gather | solution.py:230
  134.4 38.1 %all-gather.3 = bf16[32,24,2]{1,2,0:T(2,128)(2,1)S(1)} all-gather(bf16[1,24,2]{1,2,0:T(2,128)(2,1)S(1)} %bitcast.332), channel_id=1, replica_groups=mesh['fsdp'=32] {'fsdp'}, dimensions={0}, use_global_device_ids=true | all-gather | bytes 3168 | tf_op jit(solution)/shard_map/all_gather | solution.py:233
  172.6 37.5 %all-gather = bf16[32,24,4]{1,2,0:T(4,128)(2,1)S(1)} all-gather(bf16[1,24,4]{1,2,0:T(4,128)(2,1)S(1)} %bitcast.328), channel_id=1, replica_groups=mesh['fsdp'=32] {'fsdp'}, dimensions={0}, use_global_device_ids=true | all-gather | bytes 6336 | tf_op jit(solution)/shard_map/all_gather | solution.py:179
  212.4 39.3 %all_gather.53 = bf16[2,4,768]{1,0,2:T(2,128)(2,1)S(1)} all-gather(bf16[2,4,24]{1,0,2:T(2,128)(2,1)S(1)} %copy.253), channel_id=1, replica_groups=mesh['fsdp'=32] {'fsdp'}, dimensions={2}, use_global_device_ids=true | all-gather | bytes 12672 | tf_op jit(solution)/shard_map/all_gather | solution.py:206
  252.0 20.4 %slice_reduce_fusion.2 = (f32[768]{0:T(1024)S(1)}, f32[768]{0:T(1024)}, f32[768]{0:T(1024)S(1)}, f32[768]{0:T(1024)S(1)}, f32[768]{0:T(1024)S(1)}, /*index=5*/f32[768]{0:T(1024)}, f32[768]{0:T(1024)S(1)}, f32[768]{0:T(1024)S(1)}) fusion(f32[2,4,768]{1,0,2:T(2,128)S(1)} %convert_element_type.533), kind=kLoop, calls=%fused_computation.272 | loop fusion | bytes 49152 | tf_op jit(solution)/shard_map/slice | solution.py:224
  275.0 39.9 %all_gather.59 = bf16[2,2,768]{1,0,2:T(2,128)(2,1)S(1)} all-gather(bf16[2,2,24]{1,0,2:T(2,128)(2,1)S(1)} %copy.261), channel_id=1, replica_groups=mesh['fsdp'=32] {'fsdp'}, dimensions={2}, use_global_device_ids=true | all-gather | bytes 6336 | tf_op jit(solution)/shard_map/all_gather | solution.py:232
  320.3 10.2 slice_reduce_fusion
  411.4 5.2 fusion.12
  416.6 13.4 all-gather.21.cloned.1.call-done
  429.9 4.6 fusion.164
  466.6 4.4 multiply_reduce_fusion.17
  486.0 3.9 fusion.9
  489.9 5.0 fusion.159
  523.8 4.3 multiply_reduce_fusion.7
  541.4 4.1 convolution_bitcast_fusion.5
  545.4 4.2 convolution_bitcast_fusion.4
  562.7 4.0 add_bitcast_fusion
  566.8 12.0 maximum_bitcast_fusion.2
  578.8 21.8 %copy.307 = f32[768,2,3,768]{3,1,2,0:T(2,128)} copy(f32[768,2,3,768]{0,3,2,1:T(8,128)} %maximum_bitcast_fusion.2) | data formatting | bytes 28311552 | tf_op jit(solution)/shard_map/transpose | solution.py:142
  600.6 11.0 copy.306
  626.3 6.7 maximum_bitcast_fusion.1
  638.5 7.1 maximum_bitcast_fusion
  674.3 3.5 fusion.52
  686.0 41.9 %all-reduce.9 = (f32[768,4]{0,1:T(4,128)}, f32[768]{0:T(1024)}, f32[768,2,4]{0,2,1:T(4,128)}, f32[768,2]{0,1:T(2,128)}, f32[768,2,2]{0,2,1:T(2,128)}, /*index=5*/f32[768,2]{0,1:T(2,128)}) all-reduce(f32[768,4]{0,1:T(4,128)} %maximum_bitcast_fusion.6, f32[768]{0:T(1024)S(1)} %add.548, ...), channel_id=4, replica_groups=mesh['fsdp'=32] {'fsdp'}, use_global_device_ids=true, to_apply=%region_46.0.clone | all-reduce | flops 16128 | bytes 129024
  735.9 3.5 fusion.57
  740.8 293.7 %all-reduce.13.cloned.1.call-done = (f32[768,3,768]{2,1,0:T(4,128)}, f32[768,2,3,768]{3,1,2,0:T(2,128)}) async-done(((f32[768,3,768]{2,1,0:T(4,128)}, f32[768,2,3,768]{3,1,2,0:T(2,128)}), (f32[768,3,768]{2,1,0:T(4,128)}, f32[768,2,3,768]{3,1,2,0:T(2,128)})) %all-reduce.13.cloned.1.call-update) | async-done | bytes 21233680
  1038.1 101.3 %reduce-scatter.13.cloned.1.call-done = f32[24,768]{1,0:T(8,128)} async-done(((f32[768,768]{1,0:T(8,128)}), f32[24,768]{1,0:T(8,128)}) %reduce-scatter.13.cloned.1.call-update) | async-done | bytes 73744 | tf_op jit(solution)/shard_map/reduce_scatter | solution.py:401
  1139.4 112.5 %reduce-scatter.15.cloned.1.call-done = f32[24,2,768]{2,0,1:T(8,128)} async-done(((f32[768,2,768]{2,0,1:T(8,128)}), f32[24,2,768]{2,0,1:T(8,128)}) %reduce-scatter.15.cloned.1.call-update) | async-done | bytes 147472 | tf_op jit(solution)/shard_map/reduce_scatter | solution.py:335
  1251.9 211.1 %reduce-scatter.19.cloned.1.call-done = f32[96,2,768]{2,0,1:T(8,128)} async-done(((f32[3072,2,768]{2,0,1:T(8,128)}), f32[96,2,768]{2,0,1:T(8,128)}) %reduce-scatter.19.cloned.1.call-update) | async-done | bytes 589840 | tf_op jit(solution)/shard_map/reduce_scatter | solution.py:289
  1463.0 211.0 %reduce-scatter.17.cloned.1.call-done = f32[24,2,3072]{2,0,1:T(8,128)} async-done(((f32[768,2,3072]{2,0,1:T(8,128)}), f32[24,2,3072]{2,0,1:T(8,128)}) %reduce-scatter.17.cloned.1.call-update) | async-done | bytes 589840 | tf_op jit(solution)/shard_map/reduce_scatter | solution.py:287
  (676 shorter events, 269.6 us)
Async XLA Ops:
  7.2 6.7 copy-start.187
  7.2 50.1 %copy-start.178 = (bf16[2,4,24]{2,1,0:T(4,128)(2,1)S(1)}, bf16[2,4,24]{2,1,0:T(4,128)(2,1)}, u32[]{:S(2)}) copy-start(bf16[2,4,24]{2,1,0:T(4,128)(2,1)} %param.26) | copy-start | bytes 1156
  7.2 50.2 %copy-start.181 = (bf16[2,2,24]{2,1,0:T(2,128)(2,1)S(1)}, bf16[2,2,24]{2,1,0:T(2,128)(2,1)}, u32[]{:S(2)}) copy-start(bf16[2,2,24]{2,1,0:T(2,128)(2,1)} %param.31) | copy-start | bytes 580
  7.2 50.3 %copy-start.182 = (bf16[2,24]{1,0:T(2,128)(2,1)S(1)}, bf16[2,24]{1,0:T(2,128)(2,1)}, u32[]{:S(2)}) copy-start(bf16[2,24]{1,0:T(2,128)(2,1)} %param.27) | copy-start | bytes 292
  7.2 90.3 %copy-start.183 = (bf16[2,96]{1,0:T(2,128)(2,1)S(1)}, bf16[2,96]{1,0:T(2,128)(2,1)}, u32[]{:S(2)}) copy-start(bf16[2,96]{1,0:T(2,128)(2,1)} %param.29) | copy-start | bytes 1156
  7.3 127.1 %copy-start.184 = (bf16[2,24]{1,0:T(2,128)(2,1)S(1)}, bf16[2,24]{1,0:T(2,128)(2,1)}, u32[]{:S(2)}) copy-start(bf16[2,24]{1,0:T(2,128)(2,1)} %param.32) | copy-start | bytes 292
  7.3 165.3 %copy-start.179 = (bf16[4,24]{1,0:T(4,128)(2,1)S(1)}, bf16[4,24]{1,0:T(4,128)(2,1)}, u32[]{:S(2)}) copy-start(bf16[4,24]{1,0:T(4,128)(2,1)} %param.22) | copy-start | bytes 580
  7.3 323.9 %all-gather.11.cloned.1.call-start = ((), (), s32[]{:S(2)}) async-start(), calls=%async_computation.5 | async-start | bytes 3649536 | tf_op jit(solution)/shard_map/all_gather | solution.py:177
  8.0 354.7 %all-gather.13.cloned.1.call-start = ((), (), s32[]{:S(2)}) async-start(), calls=%async_computation.6 | async-start | bytes 1216512 | tf_op jit(solution)/shard_map/all_gather | solution.py:178
  8.8 359.2 %all-gather.15.cloned.1.call-start = ((), (), s32[]{:S(2)}) async-start(), calls=%async_computation.7 | async-start | bytes 7299072 | tf_op jit(solution)/shard_map/all_gather | solution.py:204
  9.5 394.8 %all-gather.17.cloned.1.call-start = ((), (), s32[]{:S(2)}) async-start(), calls=%async_computation.8 | async-start | bytes 2433024 | tf_op jit(solution)/shard_map/all_gather | solution.py:205
  10.1 401.3 %all-gather.19.cloned.1.call-start = ((), (), s32[]{:S(2)}) async-start(), calls=%async_computation.9 | async-start | bytes 9732096 | tf_op jit(solution)/shard_map/all_gather | solution.py:229
  10.7 419.3 %all-gather.21.cloned.1.call-start = ((), (), s32[]{:S(2)}) async-start(), calls=%async_computation.10 | async-start | bytes 9732096 | tf_op jit(solution)/shard_map/all_gather | solution.py:231
  11.2 728.1 %reduce-scatter.21.cloned.1.call-start = ((), (), s32[]{:S(2)}) async-start(), calls=%async_computation.15 | async-start | bytes 1622016
  251.9 63.3 %copy-start.180 = (s32[12,2]{0,1:T(2,128)S(1)}, s32[12,2]{0,1:T(2,128)}, u32[]{:S(2)}) copy-start(s32[12,2]{0,1:T(2,128)} %param.35) | copy-start | bytes 292
  252.0 63.3 %copy-start.120 = (bf16[12,16,768]{2,1,0:T(8,128)(2,1)S(1)}, bf16[12,16,768]{2,1,0:T(8,128)(2,1)}, u32[]{:S(2)}) copy-start(bf16[12,16,768]{2,1,0:T(8,128)(2,1)} %param.34) | copy-start | bytes 884740
  272.3 44.5 %copy-start.113 = (bf16[12,20,768]{2,1,0:T(8,128)(2,1)S(1)}, bf16[12,20,768]{2,1,0:T(8,128)(2,1)}, u32[]{:S(2)}) copy-start(bf16[12,20,768]{2,1,0:T(8,128)(2,1)} %param.33) | copy-start | bytes 1105924
  319.3 11.8 copy-start.74
  365.8 17.0 %copy-start.9 = (f32[240,768]{1,0:T(8,128)}, f32[240,768]{1,0:T(8,128)S(1)}, u32[]{:S(2)}) copy-start(f32[240,768]{1,0:T(8,128)S(1)} %get-tuple-element.185) | copy-start | bytes 2211844
  429.9 7.6 copy-start.186
  485.9 11.7 slice-start.3
  485.9 11.7 slice-start.4
  489.8 7.8 copy-start.37
  489.9 7.8 slice-start.5
  560.2 474.3 %all-reduce.13.cloned.1.call-start = ((), (), s32[]{:S(2)}) async-start(), calls=%async_computation.16 | async-start | bytes 47185920
  611.7 527.8 %reduce-scatter.13.cloned.1.call-start = ((), (), s32[]{:S(2)}) async-start(), calls=%async_computation.11 | async-start | bytes 2433024 | tf_op jit(solution)/shard_map/reduce_scatter | solution.py:401
  615.4 636.5 %reduce-scatter.15.cloned.1.call-start = ((), (), s32[]{:S(2)}) async-start(), calls=%async_computation.12 | async-start | bytes 4866048 | tf_op jit(solution)/shard_map/reduce_scatter | solution.py:335
  620.1 842.8 %reduce-scatter.19.cloned.1.call-start = ((), (), s32[]{:S(2)}) async-start(), calls=%async_computation.14 | async-start | bytes 19464192 | tf_op jit(solution)/shard_map/reduce_scatter | solution.py:289
  633.1 1040.9 %reduce-scatter.17.cloned.1.call-start = ((), (), s32[]{:S(2)}) async-start(), calls=%async_computation.13 | async-start | bytes 19464192 | tf_op jit(solution)/shard_map/reduce_scatter | solution.py:287
  645.7 25.3 %copy-start.137 = (f32[12,64]{1,0:T(8,128)S(1)}, f32[12,64]{1,0:T(8,128)}, u32[]{:S(2)}) copy-start(f32[12,64]{1,0:T(8,128)} %get-tuple-element.214) | copy-start | bytes 9220
  645.7 25.3 %copy-start.138 = (f32[12,64]{1,0:T(8,128)S(1)}, f32[12,64]{1,0:T(8,128)}, u32[]{:S(2)}) copy-start(f32[12,64]{1,0:T(8,128)} %get-tuple-element.216) | copy-start | bytes 9220
  645.7 28.6 %copy-start.1 = (bf16[3,768,768]{2,1,0:T(8,128)(2,1)S(1)}, bf16[3,768,768]{2,1,0:T(8,128)(2,1)}, u32[]{:S(2)}) copy-start(bf16[3,768,768]{2,1,0:T(8,128)(2,1)} %all-gather.11.cloned.1.call-done) | copy-start | bytes 10616836
  (174 other events, 429.7 us)
Sparse Core Ops, SparseCore 0:
  11.0 62.8 all-gather.10
  76.8 52.7 all-gather.12
  132.5 71.0 all-gather.14
  206.4 55.9 all-gather.16
  265.2 81.7 all-gather.18
  349.8 80.0 all-gather.20
  560.4 96.3 reduce-scatter.20
  663.1 371.3 all-reduce.12
  1040.4 98.9 reduce-scatter.12
  1145.3 106.5 reduce-scatter.14
  1258.9 204.0 reduce-scatter.18
  1469.8 204.1 reduce-scatter.16
where the time goes:
time: 1690 us; the launch traced here: 1680 us
  waiting for transfers between devices  947 us (56%)
  blocking collectives  316 us (19%)
  local copies, waits for them, and re-layouts  211 us (12%)
  matrix products  126 us (7%)
  other arithmetic  63.4 us (4%)
    unnamed x14, waiting for transfers between devices  297 us
    reduce_scatter x1, waiting for transfers between devices, per_device(): lax.psum_scatter(feed_sums[2], 'fsdp', scatter_dimension=0, tiled=True)  211 us
    reduce_scatter x1, waiting for transfers between devices, per_device(): lax.psum_scatter(feed_sums[0], 'fsdp', scatter_dimension=0, tiled=True)  211 us
    reduce_scatter x1, waiting for transfers between devices, per_device(): lax.psum_scatter(self_sums[1], 'fsdp', scatter_dimension=0, tiled=True)  112 us
    reduce_scatter x1, waiting for transfers between devices, per_device(): lax.psum_scatter(cross_sums[1], 'fsdp', scatter_dimension=0, tiled=True)  101 us
    unnamed x2, blocking collectives  84.5 us
    all_gather x1, blocking collectives, per_device(): lax.all_gather(feed_biases, 'fsdp', axis=2, tiled=True)  39.9 us
    all_gather x1, blocking collectives, per_device(): lax.all_gather(self_gain, 'fsdp', axis=1, tiled=True)  39.9 us
  transfers between devices with their start and end apart: 12, of which 6 were waited for; matrix products, arithmetic and copies ran while one was open for 15% of the time, Pallas kernels for 0%

commit v1 on v0

v1 whole, which is shorter than its diff:
```python
import functools
import math

import jax
import jax.numpy as jnp
from jax import lax
from jax.experimental import pallas as pl
from jax.experimental.pallas import tpu as pltpu
from jax.sharding import PartitionSpec as P

HEAD = 64


BF, F32 = jnp.bfloat16, jnp.float32
MESH = pl.DeviceIdType.MESH


def axes_of(mesh):
    devices = list(mesh.devices.flat)
    first = devices[0]
    sizes, strides = {}, {}
    for name, where in (("x", 0), ("y", 1), ("z", 2), ("c", None)):
        def at(device):
            return device.core_on_chip if where is None else device.coords[where]
        def rest(device):
            return tuple(device.coords[i] for i in range(3) if i != where) + (
                () if where is None else (device.core_on_chip,))
        line = [i for i, d in enumerate(devices) if rest(d) == rest(first)]
        sizes[name] = len(line)
        strides[name] = line[1] - line[0] if len(line) > 1 else 1
    return {name: (sizes[name], strides[name]) for name in sizes}


class Place:
    def __init__(self, axes):
        self.axes = axes
        self.me = lax.axis_index("fsdp")
        self.at = {k: lax.rem(lax.div(self.me, t), s) for k, (s, t) in axes.items()}

    def index(self, **to):
        i = self.me
        for k, v in to.items():
            i = i + (v - self.at[k]) * self.axes[k][1]
        return i

    def peers(self, axis):
        size = self.axes[axis][0]
        return [lax.rem(self.at[axis] + d, size) for d in range(1, size)]

    def barrier(self):
        sem = pltpu.get_barrier_semaphore()
        count = 0
        for axis in "xyzc":
            for p in self.peers(axis):
                pl.semaphore_signal(sem, inc=1, device_id=(self.index(**{axis: p}),), device_id_type=MESH)
                count += 1
        pl.semaphore_wait(sem, count)


def free_shards(place, done, fixed, body):
    total = 1
    for k in done:
        total *= place.axes[k][0]

    def step(i, carry):
        to = dict(fixed)
        for k in done:
            s = place.axes[k][0]
            to[k] = lax.rem(i, s)
            i = lax.div(i, s)
        body(place.index(**to))
        return carry
    if total == 1:
        step(0, 0)
    else:
        lax.fori_loop(0, total, step, 0)
    return total


PARTS = (
    (6, (), "xzy"),
    (0, (0,), "zyx"), (0, (1,), "zxy"), (0, (2,), "yzx"), (1, (), "xzy"),
    (2, (0,), "zyx"), (2, (1,), "zxy"), (3, (0,), "yzx"), (3, (1,), "xzy"),
    (4, (0,), "zyx"), (4, (1,), "zxy"), (5, (0,), "yzx"), (5, (1,), "xzy"),
)


def gather_kernel(axes, parts, narrays, *refs):
    shards, fulls = refs[:narrays], refs[narrays:2 * narrays]
    send, recv, csend, crecv, local = refs[2 * narrays:]
    place = Place(axes)

    def own(p):
        a, lead, _ = parts[p]
        return shards[a].at[lead] if lead else shards[a]

    def full(p, i):
        a, lead, _ = parts[p]
        r = fulls[a].at[lead] if lead else fulls[a]
        nd = len(r.shape)
        return r.at[i] if nd == 3 else r.at[:, i]

    def many(p, m):
        a, lead, _ = parts[p]
        r = fulls[a].at[lead] if lead else fulls[a]
        nd = len(r.shape)
        return r.at[pl.ds(0, m)] if nd == 3 else r.at[:, pl.ds(0, m)]

    def remote(src, dst, ss, rs, to):
        return pltpu.make_async_remote_copy(src_ref=src, dst_ref=dst, send_sem=ss, recv_sem=rs,
                                            device_id=(to,), device_id_type=MESH)

    def sizes(p, stage):
        m = 1
        for k in parts[p][2][:stage]:
            m *= axes[k][0]
        return m

    place.barrier()
    other = place.index(c=1 - place.at["c"])
    P = range(len(parts))

    def start(p, stage):
        order = parts[p][2]
        axis = order[stage]
        for peer in place.peers(axis):
            to = place.index(**{axis: peer})
            def one(i):
                src = own(p) if stage == 0 else full(p, i)
                remote(src, full(p, i), send.at[p, stage, peer], recv.at[p, stage, place.at[axis]], to).start()
            free_shards(place, order[:stage], {}, one)

    def wait_recv(p, stage):
        order = parts[p][2]
        axis = order[stage]
        m = sizes(p, stage)
        for peer in place.peers(axis):
            ref = many(p, m)
            remote(ref, ref, send.at[p, stage, peer], recv.at[p, stage, peer], other).wait_recv()

    def wait_send(p, stage):
        order = parts[p][2]
        axis = order[stage]
        m = sizes(p, stage)
        for peer in place.peers(axis):
            ref = many(p, m)
            remote(ref, ref, send.at[p, stage, peer], recv.at[p, stage, peer], other).wait_send()

    def core_start(p, stage):
        order = parts[p][2]
        if stage == 0:
            remote(own(p), full(p, place.me), csend.at[p, 0], crecv.at[p, 0], other).start()
            return
        axis = order[stage - 1]
        for peer in place.peers(axis):
            def one(i):
                remote(full(p, i), full(p, i), csend.at[p, stage], crecv.at[p, stage], other).start()
            free_shards(place, order[:stage - 1], {axis: peer}, one)

    def core_wait(p, stage):
        order = parts[p][2]
        m = 1 if stage == 0 else sizes(p, stage) - sizes(p, stage - 1)
        ref = many(p, m)
        c = remote(ref, ref, csend.at[p, stage], crecv.at[p, stage], other)
        c.wait_send()
        c.wait_recv()

    for p in P:
        start(p, 0)
        pltpu.make_async_copy(own(p), full(p, place.me), local.at[p]).start()
        core_start(p, 0)
    for p in P:
        pltpu.make_async_copy(own(p), full(p, place.me), local.at[p]).wait()
    for p in P:
        wait_recv(p, 0)
        start(p, 1)
        core_start(p, 1)
    for p in P:
        wait_recv(p, 1)
        start(p, 2)
        core_start(p, 2)
    for p in P:
        wait_recv(p, 2)
        core_start(p, 3)
    for p in P:
        for stage in range(3):
            wait_send(p, stage)
        for stage in range(4):
            core_wait(p, stage)


def gather_call(axes, shards, parts=PARTS):
    n = 1
    for s, _ in axes.values():
        n *= s
    outs = [jax.ShapeDtypeStruct(s.shape[:-2] + (n,) + s.shape[-2:], s.dtype) for s in shards]
    most = max(s for s, _ in axes.values())
    P = len(parts)
    return pl.pallas_call(
        functools.partial(gather_kernel, axes, parts, len(shards)),
        out_shape=outs,
        in_specs=[pl.BlockSpec(memory_space=pltpu.VMEM)] * len(shards),
        out_specs=[pl.BlockSpec(memory_space=pltpu.HBM)] * len(shards),
        scratch_shapes=[
            pltpu.SemaphoreType.DMA((P, 3, most)),
            pltpu.SemaphoreType.DMA((P, 3, most)),
            pltpu.SemaphoreType.DMA((P, 4)),
            pltpu.SemaphoreType.DMA((P, 4)),
            pltpu.SemaphoreType.DMA((P,)),
        ],
        compiler_params=pltpu.CompilerParams(collective_id=0, has_side_effects=True),
    )(*shards)


def scatter_kernel(axes, parts, narrays, *refs):
    grads, outs = refs[:narrays], refs[narrays:2 * narrays]
    rest = refs[2 * narrays:]
    P = len(parts)
    held, landed = rest[:P], [rest[P * (1 + s):P * (2 + s)] for s in range(4)]
    send, recv, local = rest[5 * P:]
    place = Place(axes)
    chip_axes = "xyz"

    def chip_index(to):
        i = 0
        for k in "zyx":
            i = i * axes[k][0] + to.get(k, place.at[k])
        return i

    def grad(p, i):
        a, lead, _ = parts[p]
        r = grads[a].at[lead] if lead else grads[a]
        return r.at[i] if len(r.shape) == 3 else r.at[:, i]

    def at(ref, p, i):
        return ref.at[i]

    def loop(names, fixed, body):
        total = 1
        for k in names:
            total *= axes[k][0]

        def step(n, carry):
            to, i = dict(fixed), n
            for k in names:
                to[k] = lax.rem(i, axes[k][0])
                i = lax.div(i, axes[k][0])
            body(to, n)
            return carry
        if total == 1:
            step(0, 0)
        else:
            lax.fori_loop(0, total, step, 0)
        return total

    def remote(src, dst, ss, rs, to):
        return pltpu.make_async_remote_copy(src_ref=src, dst_ref=dst, send_sem=ss, recv_sem=rs,
                                            device_id=(to,), device_id_type=MESH)

    place.barrier()
    mine, theirs = place.at["c"], 1 - place.at["c"]
    other = place.index(c=theirs)

    def begin(p):
        def one(to, n):
            remote(grad(p, place.index(c=theirs, **to)), landed[0][p].at[chip_index(to)],
                   send.at[p, 0, 0], recv.at[p, 0, 0], other).start()
            pltpu.make_async_copy(grad(p, place.index(c=mine, **to)), held[p].at[chip_index(to)], local.at[p]).start()
        loop(chip_axes, {}, one)

    def first(p):
        whole = held[p]
        pltpu.make_async_copy(whole, whole, local.at[p]).wait()
        c = remote(whole, landed[0][p], send.at[p, 0, 0], recv.at[p, 0, 0], other)
        c.wait_recv()

        def one(n, carry):
            held[p][n] = held[p][n] + landed[0][p][n]
            return carry
        lax.fori_loop(0, held[p].shape[0], one, 0)

    def distance(frm, to, axis):
        m = axes[axis][0]
        return lax.rem(frm - to + m, m) - 1

    def pass_on(p, stage):
        order = parts[p][2]
        axis, free = order[3 - stage], order[:3 - stage]
        for peer in place.peers(axis):
            to_device = place.index(**{axis: peer})
            d = distance(place.at[axis], peer, axis)

            def one(to, n):
                remote(held[p].at[chip_index(to)], landed[stage][p].at[d, n],
                       send.at[p, stage, d], recv.at[p, stage, d], to_device).start()
            loop(free, {axis: peer}, one)

    def take(p, stage):
        order = parts[p][2]
        axis, free = order[3 - stage], order[:3 - stage]
        m = axes[axis][0]
        for d in range(m - 1):
            ref = landed[stage][p].at[d]
            remote(ref, ref, send.at[p, stage, d], recv.at[p, stage, d], other).wait_recv()

        def one(to, n):
            i = chip_index(to)
            total = held[p][i].astype(F32)
            for d in range(m - 1):
                total = total + landed[stage][p][d, n].astype(F32)
            if stage == 3:
                a, lead, _ = parts[p]
                if lead:
                    outs[a][lead] = total
                else:
                    outs[a][...] = total
            else:
                held[p][i] = total.astype(BF)
        loop(free, {}, one)

    def finish(p):
        whole = held[p]
        remote(whole, whole, send.at[p, 0, 0], recv.at[p, 0, 0], other).wait_send()
        for stage in range(1, 4):
            axis = parts[p][2][3 - stage]
            for d in range(axes[axis][0] - 1):
                ref = landed[stage][p].at[d]
                remote(ref, ref, send.at[p, stage, d], recv.at[p, stage, d], other).wait_send()

    for p in range(P):
        begin(p)
    for t in range(P + 3):
        if t < P:
            first(t)
            pass_on(t, 1)
        for stage in (1, 2):
            if 0 <= t - stage < P:
                take(t - stage, stage)
                pass_on(t - stage, stage + 1)
        if 0 <= t - 3 < P:
            take(t - 3, 3)
    for p in range(P):
        finish(p)


def scatter_call(axes, grads, parts):
    outs = [jax.ShapeDtypeStruct(g.shape[:-3] + g.shape[-2:], F32) for g in grads]
    most = max(max(s for s, _ in axes.values()) - 1, 1)
    P = len(parts)
    held, landed = [], [[], [], [], []]
    for a, lead, order in parts:
        g = grads[a].shape[len(lead):]
        shard = g[:-3] + g[-2:]
        chips = g[-3] // 2
        held.append(pltpu.VMEM((chips,) + shard, BF))
        landed[0].append(pltpu.VMEM((chips,) + shard, BF))
        for stage in range(1, 4):
            f = 1
            for k in order[:3 - stage]:
                f *= axes[k][0]
            landed[stage].append(pltpu.VMEM((max(axes[order[3 - stage]][0] - 1, 1), f) + shard, BF))
    return pl.pallas_call(
        functools.partial(scatter_kernel, axes, parts, len(grads)),
        out_shape=outs,
        in_specs=[pl.BlockSpec(memory_space=pltpu.HBM)] * len(grads),
        out_specs=[pl.BlockSpec(memory_space=pltpu.VMEM)] * len(grads),
        scratch_shapes=held + landed[0] + landed[1] + landed[2] + landed[3] + [
            pltpu.SemaphoreType.DMA((P, 4, most)),
            pltpu.SemaphoreType.DMA((P, 4, most)),
            pltpu.SemaphoreType.DMA((P,)),
        ],
        compiler_params=pltpu.CompilerParams(collective_id=1, has_side_effects=True, vmem_limit_bytes=64 * 1024 * 1024 - 70000),
        name="scatter",
    )(*grads)


epsilon = 1e-12
root_half = 0.7071067811865476
root_two_pi = 2.5066282746310002


def layer_norm(hidden, gain, shift):
    average = jnp.mean(hidden, axis=-1, keepdims=True)
    centred = hidden - average
    inverse = lax.rsqrt(jnp.mean(centred * centred, axis=-1, keepdims=True) + epsilon)
    normed = centred * inverse
    return (normed * gain + shift, normed, inverse)


def norm_back(upstream, normed, inverse, gain):
    scaled = upstream * gain
    centred = scaled - jnp.mean(scaled, axis=-1, keepdims=True)
    result = inverse * (centred - normed * jnp.mean(scaled * normed, axis=-1, keepdims=True))
    return (result, jnp.sum(upstream * normed, axis=0), jnp.sum(upstream, axis=0))


def weight_grad(left_rows, right_rows):
    return jnp.einsum("na,nb->ab", left_rows, right_rows, preferred_element_type=jnp.float32)


def row_grad(upstream, weight):
    return jnp.einsum("nb,ab->na", upstream, weight, preferred_element_type=jnp.float32)


def three_ways(block_of_rows, incoming_weight, biases):
    projected_rows = jnp.einsum(
        "vf,zfk->zvk", block_of_rows, incoming_weight, preferred_element_type=jnp.float32
    )
    query = (projected_rows[0] + biases[0]).astype(jnp.bfloat16)
    keys = projected_rows[1].astype(jnp.bfloat16)
    values = (projected_rows[2] + biases[1]).astype(jnp.bfloat16)
    return (query, keys, values)


def split_heads(block_of_rows, item_count):
    return block_of_rows.reshape(
        item_count, block_of_rows.shape[0] // item_count, block_of_rows.shape[1] // HEAD, HEAD
    )


def scores_of(query, keys, item_count):
    return jnp.einsum(
        "bqhd,bkhd->bhqk",
        split_heads(query, item_count),
        split_heads(keys, item_count),
        preferred_element_type=jnp.float32,
    ) * HEAD ** (-0.5)


def attend(query, keys, values, item_count):
    scores = scores_of(query, keys, item_count)
    highest = jnp.max(scores, axis=-1, keepdims=True)
    powers = jnp.exp(scores - highest)
    totals = jnp.sum(powers, axis=-1, keepdims=True)
    weights = (powers / totals).astype(jnp.bfloat16)
    context = jnp.einsum(
        "bhqk,bkhd->bqhd",
        weights,
        split_heads(values, item_count),
        preferred_element_type=jnp.float32,
    )
    return (context.reshape(query.shape).astype(jnp.bfloat16), highest + jnp.log(totals))


def attend_back(context_grad, query, keys, values, log_total, item_count):
    weights = jnp.exp(scores_of(query, keys, item_count) - log_total)
    upstream = split_heads(context_grad, item_count)
    gradient_weights = jnp.einsum(
        "bqhd,bkhd->bhqk",
        upstream,
        split_heads(values, item_count),
        preferred_element_type=jnp.float32,
    )
    values_grad = jnp.einsum(
        "bhqk,bqhd->bkhd",
        weights.astype(jnp.bfloat16),
        upstream,
        preferred_element_type=jnp.float32,
    )
    scores_grad = (
        weights * (gradient_weights - jnp.sum(weights * gradient_weights, axis=-1, keepdims=True))
    ).astype(jnp.bfloat16)
    query_grad = jnp.einsum(
        "bhqk,bkhd->bqhd",
        scores_grad,
        split_heads(keys, item_count),
        preferred_element_type=jnp.float32,
    ) * HEAD ** (-0.5)
    keys_grad = jnp.einsum(
        "bhqk,bqhd->bkhd",
        scores_grad,
        split_heads(query, item_count),
        preferred_element_type=jnp.float32,
    ) * HEAD ** (-0.5)
    return (
        query_grad.reshape(query.shape).astype(jnp.bfloat16),
        keys_grad.reshape(keys.shape).astype(jnp.bfloat16),
        values_grad.reshape(values.shape).astype(jnp.bfloat16),
    )


def project_back(block_of_rows, pieces, incoming_weight):
    stacked_pieces = jnp.stack(pieces)
    gradient_rows = jnp.einsum(
        "rzi,rti->zt", stacked_pieces, incoming_weight, preferred_element_type=jnp.float32
    )
    gradient_weights = jnp.einsum(
        "ti,gtx->gix", block_of_rows, stacked_pieces, preferred_element_type=jnp.float32
    )
    biases_grad = jnp.stack(
        [
            jnp.sum(pieces[0].astype(jnp.float32), axis=0),
            jnp.sum(pieces[2].astype(jnp.float32), axis=0),
        ]
    )
    return (gradient_rows, gradient_weights, biases_grad)


def gelu_of(prior_input):
    return prior_input * (lax.erf(prior_input * root_half) + 1.0) * 0.5


def gelu_slope(prior_input):
    return (lax.erf(prior_input * root_half) + 1.0) * 0.5 + prior_input * jnp.exp(
        -0.5 * prior_input * prior_input
    ) / root_two_pi


def bundle(pieces, lead, granule):
    flat = jnp.concatenate([p.reshape(lead + (-1,)) for p in pieces], axis=-1)
    size = flat.shape[-1]
    padded = -(-size // granule) * granule
    flat = jnp.pad(flat, [(0, 0)] * len(lead) + [(0, padded - size)])
    return flat.reshape(lead + (padded // 128, 128))


def unbundle(array, lead, shapes):
    flat = array.reshape(lead + (-1,))
    out, at = [], 0
    for s in shapes:
        size = math.prod(s)
        out.append(flat[..., at:at + size].reshape(lead + s))
        at += size
    return out


def gather_all(axes, kernels, shards):
    if kernels:
        return gather_call(axes, shards)
    return [lax.all_gather(s, "fsdp", axis=s.ndim - 2, tiled=False) for s in shards]


def scatter_all(axes, kernels, grads):
    if kernels:
        return scatter_call(axes, grads, PARTS)
    return [
        lax.psum_scatter(g.astype(F32), "fsdp", scatter_dimension=g.ndim - 3, tiled=False) for g in grads
    ]


def per_device(
    axes,
    language,
    vision,
    cross_project,
    cross_output,
    cross_biases,
    cross_gain,
    self_project,
    self_output,
    self_biases,
    self_gain,
    feed_up,
    feed_up_bias,
    feed_down,
    feed_biases,
    feed_gain,
    language_cotangent,
    vision_cotangent,
    task_flags,
):
    n = math.prod(s for s, _ in axes.values())
    kernels = (
        cross_output.shape[0] % 8 == 0
        and feed_down.shape[1] % 8 == 0
        and axes["c"][0] == 2
    )
    item_count = language.shape[0]
    width = language.shape[2]
    streams = (language.reshape(-1, width), vision.reshape(-1, width))
    cotangents = (language_cotangent, vision_cotangent)
    small = (cross_biases, cross_gain, self_biases, self_gain, feed_up_bias, feed_biases, feed_gain)
    small_shapes = [s.shape for s in small]
    granule = 1024 if kernels else 128
    big = [cross_project, cross_output, self_project, self_output, feed_up, feed_down]
    gathered = gather_all(axes, kernels, big + [bundle(small, (), granule)])
    merged = [
        g.reshape(g.shape[:-3] + (g.shape[-3] * g.shape[-2], g.shape[-1])) for g in gathered[:6]
    ]
    cross_project, cross_output, self_project, self_output, feed_up, feed_down = merged
    vectors = []
    for v in unbundle(gathered[6].astype(F32), (n,), small_shapes):
        v = jnp.moveaxis(v, 0, -2)
        vectors.append(v.reshape(v.shape[:-2] + (-1,)))
    cross_vector, cross_gain, self_vector, self_gain, feed_up_bias, feed_vector, feed_gain = vectors

    projected_rows = [three_ways(rows, cross_project, cross_vector) for rows in streams]
    attended = (
        attend(projected_rows[0][0], projected_rows[1][1], projected_rows[1][2], item_count),
        attend(projected_rows[1][0], projected_rows[0][1], projected_rows[0][2], item_count),
    )
    first, second, third, self_kept, feed_kept = [], [], [], [], []
    for stream in range(2):
        branch = jnp.dot(attended[stream][0], cross_output, preferred_element_type=F32) + cross_vector[2]
        first.append(layer_norm(streams[stream].astype(F32) + branch, cross_gain, cross_vector[3]))
    for stream in range(2):
        rows_in = first[stream][0].astype(BF)
        query, keys, values = three_ways(rows_in, self_project[stream], self_vector[stream])
        context, log_total = attend(query, keys, values, item_count)
        branch = jnp.dot(context, self_output[stream], preferred_element_type=F32) + self_vector[stream][2]
        second.append(layer_norm(first[stream][0] + branch, self_gain[stream], self_vector[stream][3]))
        self_kept.append((rows_in, query, keys, values, context, log_total))
    for stream in range(2):
        rows_in = second[stream][0].astype(BF)
        prior_input = jnp.dot(rows_in, feed_up[stream], preferred_element_type=F32) + feed_up_bias[stream]
        active = gelu_of(prior_input).astype(BF)
        branch = jnp.dot(active, feed_down[stream], preferred_element_type=F32) + feed_vector[stream][0]
        third.append(layer_norm(second[stream][0] + branch, feed_gain[stream], feed_vector[stream][1]))
        feed_kept.append((rows_in, prior_input, active))

    up_grads, up_bias_grads, down_grads, feed_bias_grads, feed_gain_grads = [], [], [], [], []
    into_second = []
    for stream in range(2):
        masking = task_flags[:, stream].astype(F32)[:, None, None]
        upstream = (cotangents[stream].astype(F32) * masking).reshape(-1, width)
        summed, gain_term, shift_term = norm_back(
            upstream, third[stream][1], third[stream][2], feed_gain[stream]
        )
        branch_grad = summed.astype(BF)
        rows_in, prior_input, active = feed_kept[stream]
        before_grad = (row_grad(branch_grad, feed_down[stream]) * gelu_slope(prior_input)).astype(BF)
        up_grads.append(weight_grad(rows_in, before_grad).astype(BF))
        up_bias_grads.append(jnp.sum(before_grad.astype(F32), axis=0))
        down_grads.append(weight_grad(active, branch_grad).astype(BF))
        feed_bias_grads.append(jnp.stack([jnp.sum(branch_grad.astype(F32), axis=0), shift_term]))
        feed_gain_grads.append(gain_term)
        into_second.append(summed + row_grad(before_grad, feed_up[stream]))
    project_grads, output_grads, self_bias_grads, self_gain_grads = [], [], [], []
    into_first = []
    for stream in range(2):
        summed, gain_term, shift_term = norm_back(
            into_second[stream], second[stream][1], second[stream][2], self_gain[stream]
        )
        branch_grad = summed.astype(BF)
        rows_in, query, keys, values, context, log_total = self_kept[stream]
        context_grad = row_grad(branch_grad, self_output[stream]).astype(BF)
        pieces = attend_back(context_grad, query, keys, values, log_total, item_count)
        gradient_rows, project_term, bias_term = project_back(rows_in, pieces, self_project[stream])
        project_grads.append(project_term.astype(BF))
        output_grads.append(weight_grad(context, branch_grad).astype(BF))
        self_bias_grads.append(
            jnp.stack([bias_term[0], bias_term[1], jnp.sum(branch_grad.astype(F32), axis=0), shift_term])
        )
        self_gain_grads.append(gain_term)
        into_first.append(summed + gradient_rows)
    normed_back = [
        norm_back(into_first[stream], first[stream][1], first[stream][2], cross_gain) for stream in range(2)
    ]
    branch_grads = [outcome[0].astype(BF) for outcome in normed_back]
    context_grads = [row_grad(upstream, cross_output).astype(BF) for upstream in branch_grads]
    language_pieces = attend_back(
        context_grads[0], projected_rows[0][0], projected_rows[1][1], projected_rows[1][2],
        attended[0][1], item_count,
    )
    vision_pieces = attend_back(
        context_grads[1], projected_rows[1][0], projected_rows[0][1], projected_rows[0][2],
        attended[1][1], item_count,
    )
    language_rows, language_project, language_bias = project_back(
        streams[0], (language_pieces[0], vision_pieces[1], vision_pieces[2]), cross_project
    )
    vision_rows, vision_project, vision_bias = project_back(
        streams[1], (vision_pieces[0], language_pieces[1], language_pieces[2]), cross_project
    )
    language_grad = (normed_back[0][0] + language_rows).reshape(language.shape)
    vision_grad = (normed_back[1][0] + vision_rows).reshape(vision.shape)
    small_grads = (
        jnp.stack(
            [
                language_bias[0] + vision_bias[0],
                language_bias[1] + vision_bias[1],
                jnp.sum(branch_grads[0].astype(F32), axis=0) + jnp.sum(branch_grads[1].astype(F32), axis=0),
                normed_back[0][2] + normed_back[1][2],
            ]
        ),
        normed_back[0][1] + normed_back[1][1],
        jnp.stack(self_bias_grads),
        jnp.stack(self_gain_grads),
        jnp.stack(up_bias_grads),
        jnp.stack(feed_bias_grads),
        jnp.stack(feed_gain_grads),
    )
    small_grads = [
        jnp.moveaxis(g.reshape(g.shape[:-1] + (n, g.shape[-1] // n)), -2, 0) for g in small_grads
    ]
    big_grads = [
        (language_project + vision_project).astype(BF),
        (
            weight_grad(attended[0][0], branch_grads[0]) + weight_grad(attended[1][0], branch_grads[1])
        ).astype(BF),
        jnp.stack(project_grads),
        jnp.stack(output_grads),
        jnp.stack(up_grads),
        jnp.stack(down_grads),
    ]
    big_grads = [g.reshape(g.shape[:-2] + (n, g.shape[-2] // n, g.shape[-1])) for g in big_grads]
    summed = scatter_all(axes, kernels, big_grads + [bundle(small_grads, (n,), granule).astype(BF)])
    cb, cg, sb, sg, ub, fb, fg = unbundle(summed[6], (), small_shapes)
    return (
        third[0][0].astype(BF).reshape(language.shape),
        third[1][0].astype(BF).reshape(vision.shape),
        language_grad,
        vision_grad,
        summed[0],
        summed[1],
        cb,
        cg,
        summed[2],
        summed[3],
        sb,
        sg,
        summed[4],
        ub,
        summed[5],
        fb,
        fg,
    )


def solution(mesh):
    placed = (
        P("fsdp", None, None),
        P("fsdp", None, None),
        P(None, "fsdp", None),
        P("fsdp", None),
        P(None, "fsdp"),
        P("fsdp"),
        P(None, None, "fsdp", None),
        P(None, "fsdp", None),
        P(None, None, "fsdp"),
        P(None, "fsdp"),
        P(None, "fsdp", None),
        P(None, "fsdp"),
        P(None, "fsdp", None),
        P(None, None, "fsdp"),
        P(None, "fsdp"),
        P("fsdp", None, None),
        P("fsdp", None, None),
        P("fsdp", None),
    )
    return jax.shard_map(
        functools.partial(per_device, axes_of(mesh)),
        mesh=mesh,
        in_specs=placed,
        out_specs=(
            P("fsdp", None, None),
            P("fsdp", None, None),
            P("fsdp", None, None),
            P("fsdp", None, None),
            P(None, "fsdp", None),
            P("fsdp", None),
            P(None, "fsdp"),
            P("fsdp"),
            P(None, None, "fsdp", None),
            P(None, "fsdp", None),
            P(None, None, "fsdp"),
            P(None, "fsdp"),
            P(None, "fsdp", None),
            P(None, "fsdp"),
            P(None, "fsdp", None),
            P(None, None, "fsdp"),
            P(None, "fsdp"),
        ),
        check_vma=False,
    )
```

time: 1690 us -> 807 us (0.48)
  waiting for transfers between devices: 947 us -> 0 us
  Pallas kernels: 0 us -> 391 us
  blocking collectives: 316 us -> 0 us
  local copies, waits for them, and re-layouts: 211 us -> 179 us
  other arithmetic: 63.4 us -> 81.6 us
    reduce_scatter x4 -> x0, waiting for transfers between devices: 636 us -> none  [the longest x1 211 us: per_device(): lax.psum_scatter(feed_sums[2], 'fsdp', scatter_dimension=0, tiled=True)]
    pallas_call x0 -> x2, Pallas kernels: none -> 391 us  [the longest x1 212 us: scatter_call(): pl.pallas_call(functools.partial(scatter_kernel, axes, parts, len(grads))...]
    unnamed x14 -> x0, waiting for transfers between devices: 297 us -> none
    all_gather x6 -> x0, blocking collectives: 231 us -> none  [the longest x1 39.9 us: per_device(): lax.all_gather(feed_biases, 'fsdp', axis=2, tiled=True)]
    unnamed x2 -> x0, blocking collectives: 84.5 us -> none
    transpose x9 -> x6, other arithmetic: 31.6 us -> 3.55 us  [per_device(): jnp.moveaxis(g.reshape(g.shape[:-1] + (n, g.shape[-1] // n)), -2, 0)]
    transpose x8 -> x6, local copies, waits for them, and re-layouts: 30.5 us -> 2.79 us  [per_device(): jnp.moveaxis(g.reshape(g.shape[:-1] + (n, g.shape[-1] // n)), -2, 0)]
    another operation x3 -> x9, other arithmetic: 2.16 us -> 23.9 us  [the longest x1 8.42 us: per_device(): jnp.stack(down_grads)]
  transfers between devices with their start and end apart: 12 -> 0, of which waited for: 6 -> 0; matrix products, arithmetic and copies ran while one was open for 15% -> 0% of each run, Pallas kernels for 0% -> 0%
where the time goes in v1:
time: 807 us; the launch traced here: 796 us
  Pallas kernels  391 us (48%)
  local copies, waits for them, and re-layouts  179 us (22%)
  matrix products  140 us (17%)
  other arithmetic  81.6 us (10%)
    pallas_call x1, Pallas kernels, scatter_call(): pl.pallas_call(functools.partial(scatter_kernel, axes, parts, len(grads))...  212 us
    pallas_call x1, Pallas kernels, gather_call(): pl.pallas_call(functools.partial(gather_kernel, axes, parts, len(shards))...  179 us
    dot_general x8, matrix products, row_grad(): jnp.einsum('nb,ab->na', upstream, weight, preferred_element_type=jnp.floa...  31.1 us
    unnamed x417, local copies, waits for them, and re-layouts  30.2 us
    dot_general x8, matrix products, weight_grad(): jnp.einsum('na,nb->ab', left_rows, right_rows, preferred_element_type=jnp...  19.3 us

profile of v1, /device:TPU:0, one launch (start us, length us, event | category | flops | bytes accessed | tf_op | source)
XLA Modules:
  0.0 795.6 jit_solution(6934539236464705007)
XLA Ops:
  6.6 178.8 %shard_map.305 = (bf16[3,32,24,768]{3,2,1,0:T(8,128)(2,1)}, bf16[32,24,768]{2,1,0:T(8,128)(2,1)}, bf16[2,3,32,24,768]{4,3,2,1,0:T(8,128)(2,1)}, bf16[2,32,24,768...) custom-call(bf16[3,24,768]{2,1,0:T(8,128)(2,1)} %refs_0_.1, ...), custom_call_target="tpu_custom_call" | custom-call | tf_op jit(solution)/shard_map/pallas_call | solution.py:199
  188.6 2.9 convolution_bitcast_fusion.3
  193.0 2.7 squeeze.81
  216.1 5.3 fusion.123
  244.2 2.9 fusion.124
  253.0 6.9 fusion.122
  259.9 3.8 multiply_convert_fusion.1
  264.5 6.6 fusion.121
  282.2 2.7 fusion.67
  291.2 2.8 squeeze.33
  293.9 2.7 add_convert_fusion.5
  312.4 3.1 convolution_bitcast_fusion
  337.0 6.4 multiply_convert_fusion
  343.5 4.4 fusion.141
  354.4 3.1 multiply_reduce_fusion.5
  360.0 3.1 convert_reduce_fusion.9
  370.0 7.5 fusion.151
  378.9 7.0 fusion.152
  390.1 6.0 multiply_reduce_fusion.16
  397.5 6.2 multiply_reduce_fusion.6
  451.5 4.1 multiply_reduce_fusion.17
  462.0 5.1 multiply_reduce_fusion.7
  502.7 4.9 convolution_convert_fusion.2
  507.6 3.6 convolution_convert_fusion
  511.2 8.4 %pad_maximum_fusion.1.refs_5_ = bf16[2,32,96,768]{3,2,1,0:T(8,128)(2,1)} fusion(bf16[1,32,96,768]{3,2,1,0:T(8,128)(2,1)} %bitcast.193, bf16[1,32,96,768]{3,2,1,0:T(8,128)(2,1)} %bitcast.200), kind=kLoop, calls=%fused_computation.1 | loop fusion | flops 4718592 | bytes 18874368 | tf_op jit(solution)/shard_map/stack | solution.py:694
  519.7 3.8 convolution_convert_fusion.1
  523.5 3.8 convolution_convert_fusion.3
  527.3 8.4 %pad_maximum_fusion.refs_4_ = bf16[2,32,24,3072]{3,2,1,0:T(8,128)(2,1)} fusion(bf16[1,32,24,3072]{3,2,1,0:T(8,128)(2,1)} %bitcast.201, bf16[1,32,24,3072]{3,2,1,0:T(8,128)(2,1)} %bitcast.202), kind=kLoop, calls=%fused_computation | loop fusion | flops 4718592 | bytes 18874368 | tf_op jit(solution)/shard_map/stack | solution.py:693
  542.1 3.5 pad_maximum_fusion.2.refs_2_
  559.6 3.3 add_convert_fusion
  562.9 212.4 %scatter.1 = (f32[3,24,768]{2,1,0:T(8,128)}, f32[24,768]{1,0:T(8,128)}, f32[2,3,24,768]{3,2,1,0:T(8,128)}, f32[2,24,768]{2,1,0:T(8,128)}, f32[2,24,3072]{2,1,0:T...) custom-call(bf16[3,32,24,768]{3,2,1,0:T(8,128)(2,1)} %bitcast.213, bf16[32,24,768]{2,1,0:T(8,128)(2,1)} %bitcast.216, ...), custom_call_target="tpu_custom_call" | custom-call | tf_op jit(solution)/shard_map/scatter/pallas_call | solution.py:362
  783.0 4.7 fusion.33
  (689 shorter events, 260.9 us)
Async XLA Ops:
  0.7 187.9 %copy-start.71 = (bf16[12,16,768]{2,1,0:T(8,128)(2,1)S(1)}, bf16[12,16,768]{2,1,0:T(8,128)(2,1)}, u32[]{:S(2)}) copy-start(bf16[12,16,768]{2,1,0:T(8,128)(2,1)} %param.19) | copy-start | bytes 884740
  188.5 7.2 copy-start.127
  193.0 7.1 copy-start.2
  214.4 7.0 copy-start.74
  214.5 6.9 copy-start.153
  215.6 31.6 %copy-start.8 = (f32[192,768]{1,0:T(8,128)}, f32[192,768]{1,0:T(8,128)S(1)}, u32[]{:S(2)}) copy-start(f32[192,768]{1,0:T(8,128)S(1)} %get-tuple-element.152) | copy-start | bytes 1769476
  215.6 31.5 %copy-start.145 = (f32[192]{0:T(256)}, f32[192]{0:T(256)S(1)}, u32[]{:S(2)}) copy-start(f32[192]{0:T(256)S(1)} %broadcast_multiply_fusion.9) | copy-start | bytes 2308
  215.8 31.3 %copy-start.155 = (f32[192]{0:T(256)}, f32[192]{0:T(256)S(1)}, u32[]{:S(2)}) copy-start(f32[192]{0:T(256)S(1)} %add_rsqrt_fusion.2) | copy-start | bytes 2308
  215.9 117.4 %copy-start.123 = (f32[768]{0:T(1024)}, f32[768]{0:T(1024)S(1)}, u32[]{:S(2)}) copy-start(f32[768]{0:T(1024)S(1)} %add.435) | copy-start | bytes 9220
  248.1 23.0 %copy-start.19 = (f32[192,768]{1,0:T(8,128)}, f32[192,768]{1,0:T(8,128)S(1)}, u32[]{:S(2)}) copy-start(f32[192,768]{1,0:T(8,128)S(1)} %get-tuple-element.156) | copy-start | bytes 1769476
  248.1 11.8 %copy-start.150 = (f32[192]{0:T(256)}, f32[192]{0:T(256)S(1)}, u32[]{:S(2)}) copy-start(f32[192]{0:T(256)S(1)} %broadcast_multiply_fusion.8) | copy-start | bytes 2308
  248.3 11.6 %copy-start.165 = (f32[192]{0:T(256)}, f32[192]{0:T(256)S(1)}, u32[]{:S(2)}) copy-start(f32[192]{0:T(256)S(1)} %add_rsqrt_fusion.1) | copy-start | bytes 2308
  312.2 21.2 %copy-start.168 = (f32[240]{0:T(256)}, f32[240]{0:T(256)S(1)}, u32[]{:S(2)}) copy-start(f32[240]{0:T(256)S(1)} %broadcast_multiply_fusion.17) | copy-start | bytes 2884
  312.4 20.9 %copy-start.177 = (f32[240]{0:T(256)}, f32[240]{0:T(256)S(1)}, u32[]{:S(2)}) copy-start(f32[240]{0:T(256)S(1)} %add_rsqrt_fusion.5) | copy-start | bytes 2884
  335.5 8.0 %copy-start.172 = (f32[240]{0:T(256)}, f32[240]{0:T(256)S(1)}, u32[]{:S(2)}) copy-start(f32[240]{0:T(256)S(1)} %broadcast_multiply_fusion.16) | copy-start | bytes 2884
  336.6 6.9 copy-start.183
  343.5 6.8 copy-start.149
  343.5 7.0 copy-start.114
  343.5 7.0 copy-start.192
  354.4 15.7 %copy-start.82 = (f32[192,768]{1,0:T(8,128)S(1)}, f32[192,768]{1,0:T(8,128)}, u32[]{:S(2)}) copy-start(f32[192,768]{1,0:T(8,128)} %get-tuple-element.90) | copy-start | bytes 1769476
  378.9 11.1 %copy-start.20 = (f32[192,768]{1,0:T(8,128)S(1)}, f32[192,768]{1,0:T(8,128)}, u32[]{:S(2)}) copy-start(f32[192,768]{1,0:T(8,128)} %copy-done.19) | copy-start | bytes 1769476
  443.7 7.7 copy-start.1
  469.7 76.4 %copy-start.24 = (f32[192,768]{1,0:T(8,128)}, f32[192,768]{1,0:T(8,128)S(1)}, u32[]{:S(2)}) copy-start(f32[192,768]{1,0:T(8,128)S(1)} %get-tuple-element.96) | copy-start | bytes 1769476
  494.8 7.9 copy-start.28
  511.2 8.4 %copy-start.31 = (f32[240,768]{1,0:T(8,128)S(1)}, f32[240,768]{1,0:T(8,128)}, u32[]{:S(2)}) copy-start(f32[240,768]{1,0:T(8,128)} %copy-done.29) | copy-start | bytes 2211844
  511.2 8.4 %copy-start.96 = (bf16[240,3072]{1,0:T(8,128)(2,1)S(1)}, bf16[240,3072]{1,0:T(8,128)(2,1)}, u32[]{:S(2)}) copy-start(bf16[240,3072]{1,0:T(8,128)(2,1)} %get-tuple-element.192) | copy-start | bytes 4423684
  511.2 8.4 %copy-start.126 = (f32[768]{0:T(1024)S(1)}, f32[768]{0:T(1024)}, u32[]{:S(2)}) copy-start(f32[768]{0:T(1024)} %copy-done.125) | copy-start | bytes 9220
  511.2 8.5 %copy-start.174 = (f32[240]{0:T(256)S(1)}, f32[240]{0:T(256)}, u32[]{:S(2)}) copy-start(f32[240]{0:T(256)} %copy-done.172) | copy-start | bytes 2884
  511.2 8.5 %copy-start.185 = (f32[240]{0:T(256)S(1)}, f32[240]{0:T(256)}, u32[]{:S(2)}) copy-start(f32[240]{0:T(256)} %copy-done.183) | copy-start | bytes 2884
  527.3 8.4 %copy-start.39 = (f32[240,768]{1,0:T(8,128)S(1)}, f32[240,768]{1,0:T(8,128)}, u32[]{:S(2)}) copy-start(f32[240,768]{1,0:T(8,128)} %copy-done.37) | copy-start | bytes 2211844
  527.3 8.4 %copy-start.95 = (bf16[240,768]{1,0:T(8,128)(2,1)S(1)}, bf16[240,768]{1,0:T(8,128)(2,1)}, u32[]{:S(2)}) copy-start(bf16[240,768]{1,0:T(8,128)(2,1)} %copy-done.94) | copy-start | bytes 1105924
  551.3 8.3 %copy-start.54 = (bf16[3,192,768]{2,1,0:T(8,128)(2,1)}, bf16[3,192,768]{2,1,0:T(8,128)(2,1)S(1)}, u32[]{:S(2)}) copy-start(bf16[3,192,768]{2,1,0:T(8,128)(2,1)S(1)} %constant_dynamic-update-slice_fusion.9) | copy-start | bytes 2654212
  (167 other events, 451.0 us)

commit v2 on v1

--- a/solution.py
+++ b/solution.py
@@ -9,6 +9,10 @@
 from jax.sharding import PartitionSpec as P
 
 HEAD = 64
+
+epsilon = 1e-12
+root_half = 0.7071067811865476
+root_two_pi = 2.5066282746310002
 
 
 BF, F32 = jnp.bfloat16, jnp.float32
@@ -374,136 +378,387 @@
     )(*grads)
 
 
-epsilon = 1e-12
-root_half = 0.7071067811865476
-root_two_pi = 2.5066282746310002
-
-
-def layer_norm(hidden, gain, shift):
-    average = jnp.mean(hidden, axis=-1, keepdims=True)
-    centred = hidden - average
+TILE = 256
+NN, NT, TN = (((1,), (0,)), ((), ())), (((1,), (1,)), ((), ())), (((0,), (0,)), ((), ()))
+
+
+def mm(a, b, dims):
+    return lax.dot_general(a, b, dims, preferred_element_type=F32)
+
+
+def tiles(total, body):
+    size = TILE if total % TILE == 0 else total
+
+    def step(j, carry):
+        body(pl.ds(pl.multiple_of(j * size, size), size))
+        return carry
+    lax.fori_loop(0, total // size, step, 0)
+
+
+def chunks(start, count, body):
+    size = next(s for s in (48, 40, 32, 16, count) if count % s == 0)
+
+    def step(j, carry):
+        body(pl.ds(pl.multiple_of(start + j * size, math.gcd(start, size) if start else size), size))
+        return carry
+    lax.fori_loop(0, count // size, step, 0)
+
+
+def item_mask(queries, keys, group):
+    row = lax.broadcasted_iota(jnp.int32, (group * queries, group * keys), 0)
+    col = lax.broadcasted_iota(jnp.int32, (group * queries, group * keys), 1)
+    same = None
+    for i in range(group):
+        here = (
+            (row >= i * queries) & (row < (i + 1) * queries) & (col >= i * keys) & (col < (i + 1) * keys)
+        )
+        same = here if same is None else same | here
+    return same
+
+
+def lower_half(rows):
+    return lax.broadcasted_iota(jnp.int32, (rows, 2 * HEAD), 1) < HEAD
+
+
+def attend_rows(qkv, context, weights, query_at, key_at, queries, keys, items, group):
+    width = qkv.shape[2]
+    rows, cols = group * queries, group * keys
+    mask = item_mask(queries, keys, group)
+    lower = lower_half(rows)
+
+    def pair(p, carry):
+        lanes = pl.ds(pl.multiple_of(p * 2 * HEAD, 2 * HEAD), 2 * HEAD)
+        for block in range(items // group):
+            r = pl.ds(query_at + block * rows, rows)
+            c = pl.ds(key_at + block * cols, cols)
+            q, k, v = qkv[0, r, lanes], qkv[1, c, lanes], qkv[2, c, lanes]
+            results = []
+            for half in range(2):
+                own = jnp.where(lower if half == 0 else ~lower, q, jnp.zeros_like(q))
+                scores = jnp.where(mask, mm(own, k, NT) * HEAD ** (-0.5), -jnp.inf)
+                powers = jnp.exp(scores - jnp.max(scores, axis=-1, keepdims=True))
+                w = powers / jnp.sum(powers, axis=-1, keepdims=True)
+                weights[p, half, block] = w
+                results.append(mm(w.astype(BF), v, NN))
+            context[r, lanes] = jnp.where(lower, results[0], results[1]).astype(BF)
+        return carry
+    lax.fori_loop(0, width // (2 * HEAD), pair, 0)
+
+
+def attend_rows_back(qkv, upstream, weights, grads, query_at, key_at, queries, keys, items, group):
+    width = qkv.shape[2]
+    rows, cols = group * queries, group * keys
+    lower, lower_keys = lower_half(rows), lower_half(cols)
+    scale = HEAD ** (-0.5)
+
+    def pair(p, carry):
+        lanes = pl.ds(pl.multiple_of(p * 2 * HEAD, 2 * HEAD), 2 * HEAD)
+        for block in range(items // group):
+            r = pl.ds(query_at + block * rows, rows)
+            c = pl.ds(key_at + block * cols, cols)
+            q, k, v, up = qkv[0, r, lanes], qkv[1, c, lanes], qkv[2, c, lanes], upstream[r, lanes]
+            dq, dk, dv = [], [], []
+            for half in range(2):
+                own = jnp.where(lower if half == 0 else ~lower, up, jnp.zeros_like(up))
+                w = weights[p, half, block]
+                product = w * mm(own, v, NT)
+                s = (product - w * jnp.sum(product, axis=-1, keepdims=True)).astype(BF)
+                dv.append(mm(w.astype(BF), up, TN))
+                dq.append(mm(s, k, NN))
+                dk.append(mm(s, q, TN))
+            grads[0, r, lanes] = (jnp.where(lower, dq[0], dq[1]) * scale).astype(BF)
+            grads[1, c, lanes] = (jnp.where(lower_keys, dk[0], dk[1]) * scale).astype(BF)
+            grads[2, c, lanes] = jnp.where(lower_keys, dv[0], dv[1]).astype(BF)
+        return carry
+    lax.fori_loop(0, width // (2 * HEAD), pair, 0)
+
+
+def normed_rows(hidden):
+    centred = hidden - jnp.mean(hidden, axis=-1, keepdims=True)
     inverse = lax.rsqrt(jnp.mean(centred * centred, axis=-1, keepdims=True) + epsilon)
-    normed = centred * inverse
-    return (normed * gain + shift, normed, inverse)
-
-
-def norm_back(upstream, normed, inverse, gain):
+    return centred * inverse, inverse
+
+
+def norm_rows_back(upstream, normed, inverse, gain):
     scaled = upstream * gain
     centred = scaled - jnp.mean(scaled, axis=-1, keepdims=True)
-    result = inverse * (centred - normed * jnp.mean(scaled * normed, axis=-1, keepdims=True))
-    return (result, jnp.sum(upstream * normed, axis=0), jnp.sum(upstream, axis=0))
-
-
-def weight_grad(left_rows, right_rows):
-    return jnp.einsum("na,nb->ab", left_rows, right_rows, preferred_element_type=jnp.float32)
-
-
-def row_grad(upstream, weight):
-    return jnp.einsum("nb,ab->na", upstream, weight, preferred_element_type=jnp.float32)
-
-
-def three_ways(block_of_rows, incoming_weight, biases):
-    projected_rows = jnp.einsum(
-        "vf,zfk->zvk", block_of_rows, incoming_weight, preferred_element_type=jnp.float32
-    )
-    query = (projected_rows[0] + biases[0]).astype(jnp.bfloat16)
-    keys = projected_rows[1].astype(jnp.bfloat16)
-    values = (projected_rows[2] + biases[1]).astype(jnp.bfloat16)
-    return (query, keys, values)
-
-
-def split_heads(block_of_rows, item_count):
-    return block_of_rows.reshape(
-        item_count, block_of_rows.shape[0] // item_count, block_of_rows.shape[1] // HEAD, HEAD
-    )
-
-
-def scores_of(query, keys, item_count):
-    return jnp.einsum(
-        "bqhd,bkhd->bhqk",
-        split_heads(query, item_count),
-        split_heads(keys, item_count),
-        preferred_element_type=jnp.float32,
-    ) * HEAD ** (-0.5)
-
-
-def attend(query, keys, values, item_count):
-    scores = scores_of(query, keys, item_count)
-    highest = jnp.max(scores, axis=-1, keepdims=True)
-    powers = jnp.exp(scores - highest)
-    totals = jnp.sum(powers, axis=-1, keepdims=True)
-    weights = (powers / totals).astype(jnp.bfloat16)
-    context = jnp.einsum(
-        "bhqk,bkhd->bqhd",
-        weights,
-        split_heads(values, item_count),
-        preferred_element_type=jnp.float32,
-    )
-    return (context.reshape(query.shape).astype(jnp.bfloat16), highest + jnp.log(totals))
-
-
-def attend_back(context_grad, query, keys, values, log_total, item_count):
-    weights = jnp.exp(scores_of(query, keys, item_count) - log_total)
-    upstream = split_heads(context_grad, item_count)
-    gradient_weights = jnp.einsum(
-        "bqhd,bkhd->bhqk",
-        upstream,
-        split_heads(values, item_count),
-        preferred_element_type=jnp.float32,
-    )
-    values_grad = jnp.einsum(
-        "bhqk,bqhd->bkhd",
-        weights.astype(jnp.bfloat16),
-        upstream,
-        preferred_element_type=jnp.float32,
-    )
-    scores_grad = (
-        weights * (gradient_weights - jnp.sum(weights * gradient_weights, axis=-1, keepdims=True))
-    ).astype(jnp.bfloat16)
-    query_grad = jnp.einsum(
-        "bhqk,bkhd->bqhd",
-        scores_grad,
-        split_heads(keys, item_count),
-        preferred_element_type=jnp.float32,
-    ) * HEAD ** (-0.5)
-    keys_grad = jnp.einsum(
-        "bhqk,bqhd->bkhd",
-        scores_grad,
-        split_heads(query, item_count),
-        preferred_element_type=jnp.float32,
-    ) * HEAD ** (-0.5)
-    return (
-        query_grad.reshape(query.shape).astype(jnp.bfloat16),
-        keys_grad.reshape(keys.shape).astype(jnp.bfloat16),
-        values_grad.reshape(values.shape).astype(jnp.bfloat16),
-    )
-
-
-def project_back(block_of_rows, pieces, incoming_weight):
-    stacked_pieces = jnp.stack(pieces)
-    gradient_rows = jnp.einsum(
-        "rzi,rti->zt", stacked_pieces, incoming_weight, preferred_element_type=jnp.float32
-    )
-    gradient_weights = jnp.einsum(
-        "ti,gtx->gix", block_of_rows, stacked_pieces, preferred_element_type=jnp.float32
-    )
-    biases_grad = jnp.stack(
-        [
-            jnp.sum(pieces[0].astype(jnp.float32), axis=0),
-            jnp.sum(pieces[2].astype(jnp.float32), axis=0),
-        ]
-    )
-    return (gradient_rows, gradient_weights, biases_grad)
-
-
-def gelu_of(prior_input):
-    return prior_input * (lax.erf(prior_input * root_half) + 1.0) * 0.5
-
-
-def gelu_slope(prior_input):
-    return (lax.erf(prior_input * root_half) + 1.0) * 0.5 + prior_input * jnp.exp(
-        -0.5 * prior_input * prior_input
-    ) / root_two_pi
+    return inverse * (centred - normed * jnp.mean(scaled * normed, axis=-1, keepdims=True))
+
+
+def total(rows):
+    return jnp.sum(rows, axis=0, keepdims=True)
+
+
+def load(pairs, sems):
+    copies = [pltpu.make_async_copy(src, dst, sems.at[i]) for i, (src, dst) in enumerate(pairs)]
+    for c in copies:
+        c.start()
+    return [c.wait for c in copies]
+
+
+def front_kernel(spans, items, group, x, cp_hbm, co_hbm, sp_hbm, so_hbm, cv, cg, sv, sg,
+                 qkv, ctx, n1, i1, rb, qkv2, e, n2, i2, p0, p1, p2, p3, cp, co, sp, so, hidden, sems):
+    waits = load([(cp_hbm, cp), (co_hbm, co), (sp_hbm, sp), (so_hbm, so)], sems)
+    width = x.shape[1]
+    (a0, m0, w0), (a1, m1, w1) = spans
+    waits[0]()
+    for z, bias in ((0, 0), (1, None), (2, 1)):
+        def project(c, z=z, bias=bias):
+            y = mm(x[...], cp[z, :, c], NN)
+            if bias is not None:
+                y = y + cv[bias:bias + 1, c]
+            qkv[z, :, c] = y.astype(BF)
+        tiles(width, project)
+    attend_rows(qkv, ctx, p0, a0, a1, w0, w1, items, group)
+    attend_rows(qkv, ctx, p1, a1, a0, w1, w0, items, group)
+    waits[1]()
+
+    def branch(c):
+        hidden[:, c] = x[:, c].astype(F32) + (mm(ctx[...], co[:, c], NN) + cv[2:3, c])
+    tiles(width, branch)
+
+    def norm(r):
+        n, i = normed_rows(hidden[r, :])
+        n1[r, :] = n
+        i1[r, :] = i
+        rb[r, :] = (n * cg[...] + cv[3:4, :]).astype(BF)
+    chunks(0, x.shape[0], norm)
+    waits[2]()
+    waits[3]()
+    for s, (at, m, w, p) in enumerate(((a0, m0, w0, p2), (a1, m1, w1, p3))):
+        rows = pl.ds(at, m)
+        for z, bias in ((0, 0), (1, None), (2, 1)):
+            def project(c, z=z, bias=bias, s=s, rows=rows):
+                y = mm(rb[rows, :], sp[s, z, :, c], NN)
+                if bias is not None:
+                    y = y + sv[s, bias:bias + 1, c]
+                qkv2[z, rows, c] = y.astype(BF)
+            tiles(width, project)
+        attend_rows(qkv2, e, p, at, at, w, w, items, group)
+
+        def branch(c, s=s, rows=rows):
+            first = n1[rows, c] * cg[:, c] + cv[3:4, c]
+            hidden[rows, c] = first + (mm(e[rows, :], so[s, :, c], NN) + sv[s, 2:3, c])
+        tiles(width, branch)
+
+        def norm(r):
+            n, i = normed_rows(hidden[r, :])
+            n2[r, :] = n
+            i2[r, :] = i
+        chunks(at, m, norm)
+
+
+def feed_kernel(spans, n2, cot, fu_hbm, fd_hbm, sv, sg, ub, fv, fg,
+                out, dy2, gu_hbm, gd_hbm, gub, gfv, gfg, fu, fd, gu, gd, yb, act, slope, du, dz, hidden, sems, osems):
+    streams = range(2)
+    waits = load([(fu_hbm.at[0], fu.at[0]), (fd_hbm.at[0], fd.at[0]), (fu_hbm.at[1], fu.at[1]), (fd_hbm.at[1], fd.at[1])], sems)
+    width, inner = fu.shape[1], fu.shape[2]
+    gfv[...] = jnp.zeros_like(gfv)
+    gfg[...] = jnp.zeros_like(gfg)
+    outgoing = []
+    for s in streams:
+        at, m, _ = spans[s]
+        mine = pl.ds(0, m)
+
+        def second(r, s=s):
+            return n2[r, :] * sg[s:s + 1, :] + sv[s, 3:4, :]
+
+        def lowered(j, carry, s=s, at=at):
+            yb[pl.ds(pl.multiple_of(j * 48, 16), 48), :] = second(pl.ds(pl.multiple_of(at + j * 48, 16), 48)).astype(BF)
+            return carry
+        lax.fori_loop(0, m // 48, lowered, 0)
+        waits[2 * s]()
+
+        def up(c, s=s, mine=mine):
+            u = mm(yb[mine, :], fu[s, :, c], NN) + ub[s:s + 1, c]
+            half = (lax.erf(u * root_half) + 1.0) * 0.5
+            act[mine, c] = (u * half).astype(BF)
+            slope[mine, c] = half + u * jnp.exp(-0.5 * u * u) / root_two_pi
+        tiles(inner, up)
+        waits[2 * s + 1]()
+
+        def down(c, s=s, mine=mine, at=at, m=m):
+            rows = pl.ds(at, m)
+            y = n2[rows, c] * sg[s:s + 1, c] + sv[s, 3:4, c]
+            hidden[mine, c] = y + (mm(act[mine, :], fd[s, :, c], NN) + fv[s, 0:1, c])
+        tiles(width, down)
+
+        def norms(j, carry, s=s, at=at):
+            r = pl.ds(pl.multiple_of(j * 48, 16), 48)
+            g = pl.ds(pl.multiple_of(at + j * 48, 16), 48)
+            n, inverse = normed_rows(hidden[r, :])
+            out[g, :] = (n * fg[s:s + 1, :] + fv[s, 1:2, :]).astype(BF)
+            upstream = cot[g, :].astype(F32)
+            dh = norm_rows_back(upstream, n, inverse, fg[s:s + 1, :])
+            hidden[r, :] = dh
+            z = dh.astype(BF)
+            dz[r, :] = z
+            gfg[s:s + 1, :] += total(upstream * n)
+            gfv[s, 0:1, :] += total(z.astype(F32))
+            gfv[s, 1:2, :] += total(upstream)
+            return carry
+        lax.fori_loop(0, m // 48, norms, 0)
+
+        def back(c, s=s, mine=mine):
+            d = (mm(dz[mine, :], fd[s, c, :], NT) * slope[mine, c]).astype(BF)
+            du[mine, c] = d
+            gub[s:s + 1, c] = total(d.astype(F32))
+            gd[s, c, :] = mm(act[mine, c], dz[mine, :], TN).astype(BF)
+            gu[s, :, c] = mm(yb[mine, :], d, TN).astype(BF)
+        tiles(inner, back)
+        for k, (src, dst) in enumerate(((gu, gu_hbm), (gd, gd_hbm))):
+            copy = pltpu.make_async_copy(src.at[s], dst.at[s], osems.at[2 * s + k])
+            copy.start()
+            outgoing.append(copy)
+
+        def rows_back(c, s=s, mine=mine, at=at, m=m):
+            dy2[pl.ds(at, m), c] = hidden[mine, c] + mm(du[mine, :], fu[s, c, :], NT)
+        tiles(width, rows_back)
+    for copy in outgoing:
+        copy.wait()
+
+
+def rear_kernel(spans, items, group, x, qkv, ctx, n1, i1, rb, qkv2, e, n2, i2, p0, p1, p2, p3, dy2,
+                cp_hbm, co_hbm, sp_hbm, so_hbm, cg, sg,
+                dx, gcp_hbm, gco_hbm, gsp_hbm, gso_hbm, gcv, gcg, gsv, gsg,
+                cp, co, sp, so, gcp, gco, gsp, gso, hidden, da, dctx, dqkv, sems, osems):
+    waits = load([(so_hbm, so), (sp_hbm, sp), (co_hbm, co), (cp_hbm, cp)], sems)
+    width = x.shape[1]
+    (a0, m0, w0), (a1, m1, w1) = spans
+    outgoing = []
+
+    def leave(src, dst):
+        copy = pltpu.make_async_copy(src, dst, osems.at[len(outgoing)])
+        copy.start()
+        outgoing.append(copy)
+
+    gsv[...] = jnp.zeros_like(gsv)
+    gsg[...] = jnp.zeros_like(gsg)
+    gcv[...] = jnp.zeros_like(gcv)
+    gcg[...] = jnp.zeros_like(gcg)
+    waits[0]()
+    waits[1]()
+    for s, (at, m, w, p) in enumerate(((a0, m0, w0, p2), (a1, m1, w1, p3))):
+        rows = pl.ds(at, m)
+
+        def norms(r, s=s):
+            upstream, n = dy2[r, :], n2[r, :]
+            dh = norm_rows_back(upstream, n, i2[r, :], sg[s:s + 1, :])
+            hidden[r, :] = dh
+            z = dh.astype(BF)
+            da[r, :] = z
+            gsg[s:s + 1, :] += total(upstream * n)
+            gsv[s, 2:3, :] += total(z.astype(F32))
+            gsv[s, 3:4, :] += total(upstream)
+        chunks(at, m, norms)
+
+        def output_back(c, s=s, rows=rows):
+            dctx[rows, c] = mm(da[rows, :], so[s, c, :], NT).astype(BF)
+            gso[s, c, :] = mm(e[rows, c], da[rows, :], TN).astype(BF)
+        tiles(width, output_back)
+        leave(gso.at[s], gso_hbm.at[s])
+        attend_rows_back(qkv2, dctx, p, dqkv, at, at, w, w, items, group)
+
+        def sums(c, s=s, rows=rows):
+            gsv[s, 0:1, c] = total(dqkv[0, rows, c].astype(F32))
+            gsv[s, 1:2, c] = total(dqkv[2, rows, c].astype(F32))
+        tiles(width, sums)
+        for z in range(3):
+            def project_back(c, s=s, z=z, rows=rows):
+                gsp[s, z, :, c] = mm(rb[rows, :], dqkv[z, rows, c], TN).astype(BF)
+                hidden[rows, c] = hidden[rows, c] + mm(dqkv[z, rows, :], sp[s, z, c, :], NT)
+            tiles(width, project_back)
+        leave(gsp.at[s], gsp_hbm.at[s])
+
+    def norms(r):
+        upstream, n = hidden[r, :], n1[r, :]
+        dh = norm_rows_back(upstream, n, i1[r, :], cg[...])
+        hidden[r, :] = dh
+        z = dh.astype(BF)
+        da[r, :] = z
+        gcg[...] += total(upstream * n)
+        gcv[2:3, :] += total(z.astype(F32))
+        gcv[3:4, :] += total(upstream)
+    chunks(0, x.shape[0], norms)
+    waits[2]()
+    waits[3]()
+
+    def output_back(c):
+        dctx[:, c] = mm(da[...], co[c, :], NT).astype(BF)
+        gco[c, :] = mm(ctx[:, c], da[...], TN).astype(BF)
+    tiles(width, output_back)
+    leave(gco, gco_hbm)
+    attend_rows_back(qkv, dctx, p0, dqkv, a0, a1, w0, w1, items, group)
+    attend_rows_back(qkv, dctx, p1, dqkv, a1, a0, w1, w0, items, group)
+
+    def sums(c):
+        gcv[0:1, c] = total(dqkv[0, :, c].astype(F32))
+        gcv[1:2, c] = total(dqkv[2, :, c].astype(F32))
+    tiles(width, sums)
+    for z in range(3):
+        def project_back(c, z=z):
+            gcp[z, :, c] = mm(x[...], dqkv[z, :, c], TN).astype(BF)
+            before = hidden[:, c] if z == 0 else dx[:, c]
+            dx[:, c] = before + mm(dqkv[z], cp[z, c, :], NT)
+        tiles(width, project_back)
+    leave(gcp, gcp_hbm)
+    for copy in outgoing:
+        copy.wait()
+
+
+VMEM_LIMIT = 64 * 1024 * 1024 - 70000
+
+
+def compute(x, cot, items, weights, vectors):
+    cp, co, sp, so, fu, fd = weights
+    cv, cg, sv, sg, ub, fv, fg = vectors
+    total_rows, width = x.shape
+    inner = fu.shape[2]
+    words, regions = items
+    count = words[0]
+    spans = ((0, count * words[1], words[1]), (count * words[1], count * regions[1], regions[1]))
+    group = next(g for g in (4, 2, 1, count) if count % g == 0 and g * words[1] % 16 == 0 and g * regions[1] % 16 == 0)
+    V, H = pl.BlockSpec(memory_space=pltpu.VMEM), pl.BlockSpec(memory_space=pltpu.HBM)
+    like = jax.ShapeDtypeStruct
+    params = pltpu.CompilerParams(vmem_limit_bytes=VMEM_LIMIT)
+
+    def kept(q, k):
+        return like((width // (2 * HEAD), 2, count // group, group * q, group * k), F32)
+    rows_bf, rows_f, one = like((total_rows, width), BF), like((total_rows, width), F32), like((total_rows, 1), F32)
+    three = like((3, total_rows, width), BF)
+    w0, w1 = words[1], regions[1]
+    state = pl.pallas_call(
+        functools.partial(front_kernel, spans, count, group),
+        out_shape=[three, rows_bf, rows_f, one, rows_bf, three, rows_bf, rows_f, one,
+                   kept(w0, w1), kept(w1, w0), kept(w0, w0), kept(w1, w1)],
+        in_specs=[V, H, H, H, H, V, V, V, V], out_specs=[V] * 13,
+        scratch_shapes=[pltpu.VMEM(a.shape, a.dtype) for a in (cp, co, sp, so)]
+        + [pltpu.VMEM((total_rows, width), F32), pltpu.SemaphoreType.DMA((4,))],
+        compiler_params=params, name="front",
+    )(x, cp, co, sp, so, cv, cg, sv, sg)
+    most = max(m for _, m, _ in spans)
+    n2 = state[7]
+    out, dy2, gu, gd, gub, gfv, gfg = pl.pallas_call(
+        functools.partial(feed_kernel, spans),
+        out_shape=[rows_bf, rows_f, like(fu.shape, BF), like(fd.shape, BF), like(ub.shape, F32),
+                   like(fv.shape, F32), like(fg.shape, F32)],
+        in_specs=[V, V, H, H, V, V, V, V, V], out_specs=[V, V, H, H, V, V, V],
+        scratch_shapes=[pltpu.VMEM(a.shape, BF) for a in (fu, fd, fu, fd)] + [
+            pltpu.VMEM((most, width), BF), pltpu.VMEM((most, inner), BF), pltpu.VMEM((most, inner), F32),
+            pltpu.VMEM((most, inner), BF), pltpu.VMEM((most, width), BF), pltpu.VMEM((most, width), F32),
+            pltpu.SemaphoreType.DMA((4,)), pltpu.SemaphoreType.DMA((4,))],
+        compiler_params=params, name="feed",
+    )(n2, cot, fu, fd, sv, sg, ub, fv, fg)
+    dx, gcp, gco, gsp, gso, gcv, gcg, gsv, gsg = pl.pallas_call(
+        functools.partial(rear_kernel, spans, count, group),
+        out_shape=[rows_f] + [like(a.shape, BF) for a in (cp, co, sp, so)] + [like(a.shape, F32) for a in (cv, cg, sv, sg)],
+        in_specs=[V] * 15 + [H] * 4 + [V] * 2, out_specs=[V] + [H] * 4 + [V] * 4,
+        scratch_shapes=[pltpu.VMEM(a.shape, BF) for a in (cp, co, sp, so) * 2] + [
+            pltpu.VMEM((total_rows, width), F32), pltpu.VMEM((total_rows, width), BF), pltpu.VMEM((total_rows, width), BF),
+            pltpu.VMEM((3, total_rows, width), BF), pltpu.SemaphoreType.DMA((4,)), pltpu.SemaphoreType.DMA((6,))],
+        compiler_params=params, name="rear",
+    )(x, *state, dy2, cp, co, sp, so, cg, sg)
+    return out, dx, (gcp, gco, gsp, gso, gu, gd), (gcv, gcg, gsv, gsg, gub, gfv, gfg)
 
 
 def bundle(pieces, lead, granule):
@@ -584,123 +839,30 @@
         vectors.append(v.reshape(v.shape[:-2] + (-1,)))
     cross_vector, cross_gain, self_vector, self_gain, feed_up_bias, feed_vector, feed_gain = vectors
 
-    projected_rows = [three_ways(rows, cross_project, cross_vector) for rows in streams]
-    attended = (
-        attend(projected_rows[0][0], projected_rows[1][1], projected_rows[1][2], item_count),
-        attend(projected_rows[1][0], projected_rows[0][1], projected_rows[0][2], item_count),
+    words, regions = language.shape[1], vision.shape[1]
+    masked = [
+        (c.astype(F32) * task_flags[:, s].astype(F32)[:, None, None]).astype(BF).reshape(-1, width)
+        for s, c in enumerate(cotangents)
+    ]
+    out, rows_grad, big_grads, small_grads = compute(
+        jnp.concatenate(streams),
+        jnp.concatenate(masked),
+        ((item_count, words), (item_count, regions)),
+        (cross_project, cross_output, self_project, self_output, feed_up, feed_down),
+        (cross_vector, cross_gain[None], self_vector, self_gain, feed_up_bias, feed_vector, feed_gain),
     )
-    first, second, third, self_kept, feed_kept = [], [], [], [], []
-    for stream in range(2):
-        branch = jnp.dot(attended[stream][0], cross_output, preferred_element_type=F32) + cross_vector[2]
-        first.append(layer_norm(streams[stream].astype(F32) + branch, cross_gain, cross_vector[3]))
-    for stream in range(2):
-        rows_in = first[stream][0].astype(BF)
-        query, keys, values = three_ways(rows_in, self_project[stream], self_vector[stream])
-        context, log_total = attend(query, keys, values, item_count)
-        branch = jnp.dot(context, self_output[stream], preferred_element_type=F32) + self_vector[stream][2]
-        second.append(layer_norm(first[stream][0] + branch, self_gain[stream], self_vector[stream][3]))
-        self_kept.append((rows_in, query, keys, values, context, log_total))
-    for stream in range(2):
-        rows_in = second[stream][0].astype(BF)
-        prior_input = jnp.dot(rows_in, feed_up[stream], preferred_element_type=F32) + feed_up_bias[stream]
-        active = gelu_of(prior_input).astype(BF)
-        branch = jnp.dot(active, feed_down[stream], preferred_element_type=F32) + feed_vector[stream][0]
-        third.append(layer_norm(second[stream][0] + branch, feed_gain[stream], feed_vector[stream][1]))
-        feed_kept.append((rows_in, prior_input, active))
-
-    up_grads, up_bias_grads, down_grads, feed_bias_grads, feed_gain_grads = [], [], [], [], []
-    into_second = []
-    for stream in range(2):
-        masking = task_flags[:, stream].astype(F32)[:, None, None]
-        upstream = (cotangents[stream].astype(F32) * masking).reshape(-1, width)
-        summed, gain_term, shift_term = norm_back(
-            upstream, third[stream][1], third[stream][2], feed_gain[stream]
-        )
-        branch_grad = summed.astype(BF)
-        rows_in, prior_input, active = feed_kept[stream]
-        before_grad = (row_grad(branch_grad, feed_down[stream]) * gelu_slope(prior_input)).astype(BF)
-        up_grads.append(weight_grad(rows_in, before_grad).astype(BF))
-        up_bias_grads.append(jnp.sum(before_grad.astype(F32), axis=0))
-        down_grads.append(weight_grad(active, branch_grad).astype(BF))
-        feed_bias_grads.append(jnp.stack([jnp.sum(branch_grad.astype(F32), axis=0), shift_term]))
-        feed_gain_grads.append(gain_term)
-        into_second.append(summed + row_grad(before_grad, feed_up[stream]))
-    project_grads, output_grads, self_bias_grads, self_gain_grads = [], [], [], []
-    into_first = []
-    for stream in range(2):
-        summed, gain_term, shift_term = norm_back(
-            into_second[stream], second[stream][1], second[stream][2], self_gain[stream]
-        )
-        branch_grad = summed.astype(BF)
-        rows_in, query, keys, values, context, log_total = self_kept[stream]
-        context_grad = row_grad(branch_grad, self_output[stream]).astype(BF)
-        pieces = attend_back(context_grad, query, keys, values, log_total, item_count)
-        gradient_rows, project_term, bias_term = project_back(rows_in, pieces, self_project[stream])
-        project_grads.append(project_term.astype(BF))
-        output_grads.append(weight_grad(context, branch_grad).astype(BF))
-        self_bias_grads.append(
-            jnp.stack([bias_term[0], bias_term[1], jnp.sum(branch_grad.astype(F32), axis=0), shift_term])
-        )
-        self_gain_grads.append(gain_term)
-        into_first.append(summed + gradient_rows)
-    normed_back = [
-        norm_back(into_first[stream], first[stream][1], first[stream][2], cross_gain) for stream in range(2)
-    ]
-    branch_grads = [outcome[0].astype(BF) for outcome in normed_back]
-    context_grads = [row_grad(upstream, cross_output).astype(BF) for upstream in branch_grads]
-    language_pieces = attend_back(
-        context_grads[0], projected_rows[0][0], projected_rows[1][1], projected_rows[1][2],
-        attended[0][1], item_count,
-    )
-    vision_pieces = attend_back(
-        context_grads[1], projected_rows[1][0], projected_rows[0][1], projected_rows[0][2],
-        attended[1][1], item_count,
-    )
-    language_rows, language_project, language_bias = project_back(
-        streams[0], (language_pieces[0], vision_pieces[1], vision_pieces[2]), cross_project
-    )
-    vision_rows, vision_project, vision_bias = project_back(
-        streams[1], (vision_pieces[0], language_pieces[1], language_pieces[2]), cross_project
-    )
-    language_grad = (normed_back[0][0] + language_rows).reshape(language.shape)
-    vision_grad = (normed_back[1][0] + vision_rows).reshape(vision.shape)
-    small_grads = (
-        jnp.stack(
-            [
-                language_bias[0] + vision_bias[0],
-                language_bias[1] + vision_bias[1],
-                jnp.sum(branch_grads[0].astype(F32), axis=0) + jnp.sum(branch_grads[1].astype(F32), axis=0),
-                normed_back[0][2] + normed_back[1][2],
-            ]
-        ),
-        normed_back[0][1] + normed_back[1][1],
-        jnp.stack(self_bias_grads),
-        jnp.stack(self_gain_grads),
-        jnp.stack(up_bias_grads),
-        jnp.stack(feed_bias_grads),
-        jnp.stack(feed_gain_grads),
-    )
+    small_grads = [g.reshape(v.shape) for g, v in zip(small_grads, vectors)]
     small_grads = [
         jnp.moveaxis(g.reshape(g.shape[:-1] + (n, g.shape[-1] // n)), -2, 0) for g in small_grads
-    ]
-    big_grads = [
-        (language_project + vision_project).astype(BF),
-        (
-            weight_grad(attended[0][0], branch_grads[0]) + weight_grad(attended[1][0], branch_grads[1])
-        ).astype(BF),
-        jnp.stack(project_grads),
-        jnp.stack(output_grads),
-        jnp.stack(up_grads),
-        jnp.stack(down_grads),
     ]
     big_grads = [g.reshape(g.shape[:-2] + (n, g.shape[-2] // n, g.shape[-1])) for g in big_grads]
     summed = scatter_all(axes, kernels, big_grads + [bundle(small_grads, (n,), granule).astype(BF)])
     cb, cg, sb, sg, ub, fb, fg = unbundle(summed[6], (), small_shapes)
     return (
-        third[0][0].astype(BF).reshape(language.shape),
-        third[1][0].astype(BF).reshape(vision.shape),
-        language_grad,
-        vision_grad,
+        out[:item_count * words].reshape(language.shape),
+        out[item_count * words:].reshape(vision.shape),
+        rows_grad[:item_count * words].reshape(language.shape),
+        rows_grad[item_count * words:].reshape(vision.shape),
         summed[0],
         summed[1],
         cb,

time: 807 us -> 605 us (0.75); the launches traced: 796 us -> 603 us
  Pallas kernels: 391 us -> 559 us
  local copies, waits for them, and re-layouts: 179 us -> 33.8 us
  matrix products: 140 us -> 0 us
  other arithmetic: 81.6 us -> 8.79 us
    pallas_call x0 -> x3, Pallas kernels: none -> 168 us  [the longest x1 71.9 us: compute(): pl.pallas_call(functools.partial(rear_kernel, spans, count, group), out_s...]
    dot_general x60 -> x0, matrix products: 140 us -> none  [the longest x8 31.1 us: row_grad(): jnp.einsum('nb,ab->na', upstream, weight, preferred_element_type=jnp.floa...]
    convert_element_type x36 -> x0, local copies, waits for them, and re-layouts: 30.8 us -> none  [the longest x8 8.76 us: attend_back(): query_grad.reshape(query.shape).astype(jnp.bfloat16)]
    slice x21 -> x4, local copies, waits for them, and re-layouts: 33 us -> 3.61 us  [the longest x1 1.69 us: per_device(): out[item_count * words:].reshape(vision.shape)]
    reduce_sum x20 -> x0, other arithmetic: 26.1 us -> none  [the longest x4 9.41 us: per_device(): jnp.sum(branch_grad.astype(F32), axis=0)]
    unnamed x417 -> x29, local copies, waits for them, and re-layouts: 30.2 us -> 6.06 us
    another operation x9 -> x7, other arithmetic: 23.9 us -> 5.01 us  [the longest x1 8.42 us: per_device(): jnp.stack(down_grads)]
    another operation x22 -> x2, local copies, waits for them, and re-layouts: 17.3 us -> 0.76 us  [the longest x1 0.67 us: per_device(): cross_gain[None]]
where the time goes in v2:
time: 605 us; the launch traced here: 603 us
  Pallas kernels  559 us (92%)
  local copies, waits for them, and re-layouts  33.8 us (6%)
  other arithmetic  8.79 us (1%)
    pallas_call x1, Pallas kernels, scatter_call(): pl.pallas_call(functools.partial(scatter_kernel, axes, parts, len(grads))...  212 us
    pallas_call x1, Pallas kernels, gather_call(): pl.pallas_call(functools.partial(gather_kernel, axes, parts, len(shards))...  179 us
    pallas_call x1, Pallas kernels, compute(): pl.pallas_call(functools.partial(rear_kernel, spans, count, group), out_s...  71.9 us
    pallas_call x1, Pallas kernels, compute(): pl.pallas_call(functools.partial(front_kernel, spans, count, group), out_...  55.8 us
    pallas_call x1, Pallas kernels, compute(): pl.pallas_call(functools.partial(feed_kernel, spans), out_shape=[rows_bf,...  40.2 us

profile of v2, /device:TPU:0, one launch (start us, length us, event | category | flops | bytes accessed | tf_op | source)
XLA Modules:
  0.0 602.7 jit_solution(13070380742541303482)
XLA Ops:
  0.7 0.8 reshape.242
  1.5 0.8 reshape.243
  2.3 0.7 reshape.244
  3.0 0.7 reshape.245
  3.8 0.8 reshape.246
  4.5 0.7 reshape.247
  5.3 0.7 concatenate.14
  6.6 0.8 convert_bitcast_fusion.1
  7.4 1.1 multiply_convert_fusion.1
  8.4 1.1 reshape.240
  9.5 0.9 pad_maximum_fusion.x
  10.7 0.9 pad_maximum_fusion.1.cot
  11.6 178.8 %shard_map.305 = (bf16[3,32,24,768]{3,2,1,0:T(8,128)(2,1)}, bf16[32,24,768]{2,1,0:T(8,128)(2,1)}, bf16[2,3,32,24,768]{4,3,2,1,0:T(8,128)(2,1)}, bf16[2,32,24,768...) custom-call(bf16[3,24,768]{2,1,0:T(8,128)(2,1)} %refs_0_.1, ...), custom_call_target="tpu_custom_call" | custom-call | tf_op jit(solution)/shard_map/pallas_call | solution.py:203
  190.4 0.9 copy.68
  197.3 55.8 %front.1 = (bf16[3,432,768]{2,1,0:T(8,128)(2,1)}, bf16[432,768]{1,0:T(8,128)(2,1)}, f32[432,768]{1,0:T(8,128)}, f32[432,1]{1,0:T(8,128)}, bf16[432,768]{1,0:T(8,...) custom-call(bf16[432,768]{1,0:T(8,128)(2,1)} %pad_maximum_fusion.x, ...), custom_call_target="tpu_custom_call" | custom-call | tf_op jit(solution)/shard_map/front/pallas_call | solution.py:730
  253.1 40.2 %feed.1 = (bf16[432,768]{1,0:T(8,128)(2,1)}, f32[432,768]{1,0:T(8,128)}, bf16[2,768,3072]{2,1,0:T(8,128)(2,1)}, bf16[2,3072,768]{2,1,0:T(8,128)(2,1)}, f32[2,307...) custom-call(f32[432,768]{1,0:T(8,128)} %get-tuple-element.65.n2, bf16[432,768]{1,0:T(8,128)(2,1)} %pad_maximum_fusion.1.cot, ...), custom_call_target="tpu_custom_call" | custom-call | tf_op jit(solution)/shard_map/feed/pallas_call | solution.py:741
  293.3 71.9 %rear.1 = (f32[432,768]{1,0:T(8,128)}, bf16[3,768,768]{2,1,0:T(8,128)(2,1)}, bf16[768,768]{1,0:T(8,128)(2,1)}, bf16[2,3,768,768]{3,2,1,0:T(8,128)(2,1)}, bf16[2,...) custom-call(bf16[432,768]{1,0:T(8,128)(2,1)} %pad_maximum_fusion.x, ...), custom_call_target="tpu_custom_call" | custom-call | tf_op jit(solution)/shard_map/rear/pallas_call | solution.py:752
  368.8 0.7 convert.45
  369.6 0.7 convert.47
  372.6 212.4 %scatter.1 = (f32[3,24,768]{2,1,0:T(8,128)}, f32[24,768]{1,0:T(8,128)}, f32[2,3,24,768]{3,2,1,0:T(8,128)}, f32[2,24,768]{2,1,0:T(8,128)}, f32[2,24,3072]{2,1,0:T...) custom-call(bf16[3,32,24,768]{3,2,1,0:T(8,128)(2,1)} %bitcast.68, bf16[32,24,768]{2,1,0:T(8,128)(2,1)} %bitcast.70, ...), custom_call_target="tpu_custom_call" | custom-call | tf_op jit(solution)/shard_map/scatter/pallas_call | solution.py:366
  585.1 1.4 slice.74
  586.4 0.8 fusion.3
  588.5 0.8 fusion.4
  589.4 0.8 fusion.5
  592.8 1.7 slice.70
  594.5 1.0 slice.69
  595.5 0.8 reshape.271
  596.4 0.9 slice.72
  597.3 1.0 reshape.273
  599.6 0.8 copy.78
  601.1 0.8 copy.80
  601.9 0.8 copy.81
  (81 shorter events, 18.6 us)
Async XLA Ops:
  0.7 9.8 %copy-start.3 = (bf16[12,20,768]{2,1,0:T(8,128)(2,1)S(1)}, bf16[12,20,768]{2,1,0:T(8,128)(2,1)}, u32[]{:S(2)}) copy-start(bf16[12,20,768]{2,1,0:T(8,128)(2,1)} %param.33) | copy-start | bytes 1105924
  0.7 8.9 %copy-start.5 = (bf16[12,16,768]{2,1,0:T(8,128)(2,1)S(1)}, bf16[12,16,768]{2,1,0:T(8,128)(2,1)}, u32[]{:S(2)}) copy-start(bf16[12,16,768]{2,1,0:T(8,128)(2,1)} %param.19) | copy-start | bytes 884740
  585.1 11.3 %copy-start = (f32[432,768]{1,0:T(8,128)S(1)}, f32[432,768]{1,0:T(8,128)}, u32[]{:S(2)}) copy-start(f32[432,768]{1,0:T(8,128)} %get-tuple-element.82) | copy-start | bytes 3981316
  597.2 1.1 copy-start.6
  597.2 1.8 copy-start.8
  597.3 2.3 copy-start.4
  597.3 3.1 copy-start.7
  597.3 3.8 copy-start.2
  598.3 3.6 copy-start.1

commit v3 on v2

--- a/solution.py
+++ b/solution.py
@@ -81,139 +81,160 @@
     return total
 
 
+LAG = 2
+
 PARTS = (
-    (6, (), "xzy"),
-    (0, (0,), "zyx"), (0, (1,), "zxy"), (0, (2,), "yzx"), (1, (), "xzy"),
-    (2, (0,), "zyx"), (2, (1,), "zxy"), (3, (0,), "yzx"), (3, (1,), "xzy"),
-    (4, (0,), "zyx"), (4, (1,), "zxy"), (5, (0,), "yzx"), (5, (1,), "xzy"),
+    (6, (), "xzy", None),
+    (0, (0,), "zyx", None), (0, (1,), "zxy", None), (0, (2,), "zyx", None), (1, (), "xzy", None),
+    (2, (0, 0), "zxy", None), (2, (0, 1), "zyx", None), (2, (0, 2), "zxy", None), (3, (0,), "yzx", None),
+    (2, (1, 0), "zyx", None), (2, (1, 1), "zxy", None), (2, (1, 2), "zyx", None), (3, (1,), "xzy", None),
+    (4, (0,), "zxy", (1, 0)), (4, (0,), "zyx", (1, 1)), (5, (0,), "zxy", (0, 0)), (5, (0,), "yzx", (0, 1)),
+    (4, (1,), "zyx", (1, 0)), (4, (1,), "zxy", (1, 1)), (5, (1,), "zyx", (0, 0)), (5, (1,), "xzy", (0, 1)),
 )
 
-
-def gather_kernel(axes, parts, narrays, *refs):
-    shards, fulls = refs[:narrays], refs[narrays:2 * narrays]
-    send, recv, csend, crecv, local = refs[2 * narrays:]
-    place = Place(axes)
-
-    def own(p):
-        a, lead, _ = parts[p]
-        return shards[a].at[lead] if lead else shards[a]
-
-    def full(p, i):
-        a, lead, _ = parts[p]
-        r = fulls[a].at[lead] if lead else fulls[a]
-        nd = len(r.shape)
-        return r.at[i] if nd == 3 else r.at[:, i]
-
-    def many(p, m):
-        a, lead, _ = parts[p]
-        r = fulls[a].at[lead] if lead else fulls[a]
-        nd = len(r.shape)
-        return r.at[pl.ds(0, m)] if nd == 3 else r.at[:, pl.ds(0, m)]
-
-    def remote(src, dst, ss, rs, to):
+def extent(shape, sub):
+    if sub is None:
+        return tuple(shape)
+    return tuple(s // 2 if d == sub[0] else s for d, s in enumerate(shape))
+
+
+class Gather:
+    def __init__(self, axes, shards, fulls, send, recv, csend, crecv, local):
+        self.axes, self.shards, self.fulls = axes, shards, fulls
+        self.send, self.recv, self.csend, self.crecv, self.local = send, recv, csend, crecv, local
+        self.place = Place(axes)
+        self.place.barrier()
+        self.other = self.place.index(c=1 - self.place.at["c"])
+
+    def cut(self, p):
+        a, lead, order, sub = PARTS[p]
+        shard = self.shards[a].at[lead] if lead else self.shards[a]
+        full = self.fulls[a].at[lead] if lead else self.fulls[a]
+        return shard, full, order, sub, shard.shape
+
+    def own(self, p):
+        shard, _, _, sub, shape = self.cut(p)
+        if sub is None:
+            return shard
+        size = shape[sub[0]] // 2
+        w = pl.ds(sub[1] * size, size)
+        return shard.at[w] if sub[0] == 0 else shard.at[:, w]
+
+    def rows(self, p, at, many=1):
+        _, full, _, sub, (r, c) = self.cut(p)
+        if sub is None:
+            return full.at[pl.ds(pl.multiple_of(at * r, 8), many * r)]
+        if sub[0] == 0:
+            size = r // 2
+            return full.at[pl.ds(pl.multiple_of(at * r + (sub[1] * size if many == 1 else 0), 8), many * size)]
+        size = c // 2
+        return full.at[pl.ds(pl.multiple_of(at * r, 8), many * r), pl.ds(sub[1] * size, size)]
+
+    def remote(self, src, dst, ss, rs, to):
         return pltpu.make_async_remote_copy(src_ref=src, dst_ref=dst, send_sem=ss, recv_sem=rs,
                                             device_id=(to,), device_id_type=MESH)
 
-    def sizes(p, stage):
+    def sizes(self, p, stage):
         m = 1
-        for k in parts[p][2][:stage]:
-            m *= axes[k][0]
+        for k in PARTS[p][2][:stage]:
+            m *= self.axes[k][0]
         return m
 
-    place.barrier()
-    other = place.index(c=1 - place.at["c"])
-    P = range(len(parts))
-
-    def start(p, stage):
-        order = parts[p][2]
+    def start(self, p, stage):
+        order, place = PARTS[p][2], self.place
         axis = order[stage]
         for peer in place.peers(axis):
             to = place.index(**{axis: peer})
+
             def one(i):
-                src = own(p) if stage == 0 else full(p, i)
-                remote(src, full(p, i), send.at[p, stage, peer], recv.at[p, stage, place.at[axis]], to).start()
+                src = self.own(p) if stage == 0 else self.rows(p, i)
+                self.remote(src, self.rows(p, i), self.send.at[p, stage],
+                            self.recv.at[p, stage, place.at[axis]], to).start()
             free_shards(place, order[:stage], {}, one)
 
-    def wait_recv(p, stage):
-        order = parts[p][2]
-        axis = order[stage]
-        m = sizes(p, stage)
-        for peer in place.peers(axis):
-            ref = many(p, m)
-            remote(ref, ref, send.at[p, stage, peer], recv.at[p, stage, peer], other).wait_recv()
-
-    def wait_send(p, stage):
-        order = parts[p][2]
-        axis = order[stage]
-        m = sizes(p, stage)
-        for peer in place.peers(axis):
-            ref = many(p, m)
-            remote(ref, ref, send.at[p, stage, peer], recv.at[p, stage, peer], other).wait_send()
-
-    def core_start(p, stage):
-        order = parts[p][2]
+    def arrive(self, p, stage):
+        axis = PARTS[p][2][stage]
+        ref = self.rows(p, 0, self.sizes(p, stage)) if stage else self.own(p)
+        for peer in self.place.peers(axis):
+            self.remote(ref, ref, self.send.at[p, stage], self.recv.at[p, stage, peer], self.other).wait_recv()
+
+    def share(self, p, stage):
+        order, place = PARTS[p][2], self.place
         if stage == 0:
-            remote(own(p), full(p, place.me), csend.at[p, 0], crecv.at[p, 0], other).start()
+            self.remote(self.own(p), self.rows(p, place.me), self.csend.at[p, 0], self.crecv.at[p, 0], self.other).start()
             return
         axis = order[stage - 1]
         for peer in place.peers(axis):
             def one(i):
-                remote(full(p, i), full(p, i), csend.at[p, stage], crecv.at[p, stage], other).start()
+                self.remote(self.rows(p, i), self.rows(p, i), self.csend.at[p, stage], self.crecv.at[p, stage], self.other).start()
             free_shards(place, order[:stage - 1], {axis: peer}, one)
 
-    def core_wait(p, stage):
-        order = parts[p][2]
-        m = 1 if stage == 0 else sizes(p, stage) - sizes(p, stage - 1)
-        ref = many(p, m)
-        c = remote(ref, ref, csend.at[p, stage], crecv.at[p, stage], other)
-        c.wait_send()
-        c.wait_recv()
-
-    for p in P:
-        start(p, 0)
-        pltpu.make_async_copy(own(p), full(p, place.me), local.at[p]).start()
-        core_start(p, 0)
-    for p in P:
-        pltpu.make_async_copy(own(p), full(p, place.me), local.at[p]).wait()
-    for p in P:
-        wait_recv(p, 0)
-        start(p, 1)
-        core_start(p, 1)
-    for p in P:
-        wait_recv(p, 1)
-        start(p, 2)
-        core_start(p, 2)
-    for p in P:
-        wait_recv(p, 2)
-        core_start(p, 3)
-    for p in P:
+    def shared(self, p, stage):
+        count = 1 if stage == 0 else self.sizes(p, stage) - self.sizes(p, stage - 1)
+        ref = self.rows(p, 0, count) if count > 1 else self.own(p)
+        return self.remote(ref, ref, self.csend.at[p, stage], self.crecv.at[p, stage], self.other)
+
+    def begin(self, p):
+        self.start(p, 0)
+        pltpu.make_async_copy(self.own(p), self.rows(p, self.place.me), self.local.at[p]).start()
+        self.share(p, 0)
+
+    def forward(self, p, stage):
+        if stage == 1:
+            pltpu.make_async_copy(self.own(p), self.rows(p, self.place.me), self.local.at[p]).wait()
+        self.arrive(p, stage - 1)
+        if stage < 3:
+            self.start(p, stage)
+        self.share(p, stage)
+
+    def complete(self, p):
+        for stage in range(4):
+            self.shared(p, stage).wait_recv()
+
+    def finish(self, p):
         for stage in range(3):
-            wait_send(p, stage)
+            count = self.sizes(p, stage) * (self.axes[PARTS[p][2][stage]][0] - 1)
+            ref = self.rows(p, 0, count) if count > 1 else self.own(p)
+            self.remote(ref, ref, self.send.at[p, stage], self.recv.at[p, stage, 0], self.other).wait_send()
         for stage in range(4):
-            core_wait(p, stage)
-
-
-def gather_call(axes, shards, parts=PARTS):
-    n = 1
-    for s, _ in axes.values():
-        n *= s
-    outs = [jax.ShapeDtypeStruct(s.shape[:-2] + (n,) + s.shape[-2:], s.dtype) for s in shards]
+            self.shared(p, stage).wait_send()
+
+    def steps(self):
+        count, ahead = len(PARTS), 5
+        out = [(functools.partial(self.begin, p), None) for p in range(ahead)]
+        for t in range(count + 2 * LAG + 2):
+            if t + ahead < count:
+                out.append((functools.partial(self.begin, t + ahead), None))
+            for stage in (1, 2, 3):
+                p = t - (stage - 1) * LAG
+                if 0 <= p < count:
+                    out.append((functools.partial(self.forward, p, stage), None))
+            p = t - 2 * LAG - 1
+            if 0 <= p < count:
+                out.append((functools.partial(self.complete, p), p))
+        return out
+
+
+def gather_scratch(axes):
     most = max(s for s, _ in axes.values())
-    P = len(parts)
-    return pl.pallas_call(
-        functools.partial(gather_kernel, axes, parts, len(shards)),
-        out_shape=outs,
-        in_specs=[pl.BlockSpec(memory_space=pltpu.VMEM)] * len(shards),
-        out_specs=[pl.BlockSpec(memory_space=pltpu.HBM)] * len(shards),
-        scratch_shapes=[
-            pltpu.SemaphoreType.DMA((P, 3, most)),
-            pltpu.SemaphoreType.DMA((P, 3, most)),
-            pltpu.SemaphoreType.DMA((P, 4)),
-            pltpu.SemaphoreType.DMA((P, 4)),
-            pltpu.SemaphoreType.DMA((P,)),
-        ],
-        compiler_params=pltpu.CompilerParams(collective_id=0, has_side_effects=True),
-    )(*shards)
+    parts = len(PARTS)
+    return [
+        pltpu.SemaphoreType.DMA((parts, 3)), pltpu.SemaphoreType.DMA((parts, 3, most)),
+        pltpu.SemaphoreType.DMA((parts, 4)), pltpu.SemaphoreType.DMA((parts, 4)), pltpu.SemaphoreType.DMA((parts,)),
+    ]
+
+
+def full_shapes(axes, shards):
+    n = math.prod(s for s, _ in axes.values())
+    return [jax.ShapeDtypeStruct(s.shape[:-2] + (n * s.shape[-2], s.shape[-1]), s.dtype) for s in shards]
+
+
+def window(sub, shape):
+    if sub is None:
+        return (slice(None), slice(None))
+    size = shape[sub[0]] // 2
+    w = pl.ds(sub[1] * size, size)
+    return (w, slice(None)) if sub[0] == 0 else (slice(None), w)
 
 
 def scatter_kernel(axes, parts, narrays, *refs):
@@ -232,12 +253,8 @@
         return i
 
     def grad(p, i):
-        a, lead, _ = parts[p]
-        r = grads[a].at[lead] if lead else grads[a]
-        return r.at[i] if len(r.shape) == 3 else r.at[:, i]
-
-    def at(ref, p, i):
-        return ref.at[i]
+        a, lead, _, sub = parts[p]
+        return grads[a].at[lead + (i,) + window(sub, grads[a].shape[-2:])]
 
     def loop(names, fixed, body):
         total = 1
@@ -313,11 +330,8 @@
             for d in range(m - 1):
                 total = total + landed[stage][p][d, n].astype(F32)
             if stage == 3:
-                a, lead, _ = parts[p]
-                if lead:
-                    outs[a][lead] = total
-                else:
-                    outs[a][...] = total
+                a, lead, _, sub = parts[p]
+                outs[a][lead + window(sub, grads[a].shape[-2:])] = total
             else:
                 held[p][i] = total.astype(BF)
         loop(free, {}, one)
@@ -333,16 +347,16 @@
 
     for p in range(P):
         begin(p)
-    for t in range(P + 3):
+    for t in range(P + 3 * LAG):
         if t < P:
             first(t)
             pass_on(t, 1)
-        for stage in (1, 2):
-            if 0 <= t - stage < P:
-                take(t - stage, stage)
-                pass_on(t - stage, stage + 1)
-        if 0 <= t - 3 < P:
-            take(t - 3, 3)
+        for stage in (1, 2, 3):
+            p = t - stage * LAG
+            if 0 <= p < P:
+                take(p, stage)
+                if stage < 3:
+                    pass_on(p, stage + 1)
     for p in range(P):
         finish(p)
 
@@ -352,10 +366,9 @@
     most = max(max(s for s, _ in axes.values()) - 1, 1)
     P = len(parts)
     held, landed = [], [[], [], [], []]
-    for a, lead, order in parts:
-        g = grads[a].shape[len(lead):]
-        shard = g[:-3] + g[-2:]
-        chips = g[-3] // 2
+    for a, lead, order, sub in parts:
+        shard = extent(grads[a].shape[-2:], sub)
+        chips = grads[a].shape[-3] // 2
         held.append(pltpu.VMEM((chips,) + shard, BF))
         landed[0].append(pltpu.VMEM((chips,) + shard, BF))
         for stage in range(1, 4):
@@ -420,8 +433,7 @@
     return lax.broadcasted_iota(jnp.int32, (rows, 2 * HEAD), 1) < HEAD
 
 
-def attend_rows(qkv, context, weights, query_at, key_at, queries, keys, items, group):
-    width = qkv.shape[2]
+def attend_rows(qkv, context, weights, query_at, key_at, queries, keys, items, group, pairs):
     rows, cols = group * queries, group * keys
     mask = item_mask(queries, keys, group)
     lower = lower_half(rows)
@@ -442,7 +454,7 @@
                 results.append(mm(w.astype(BF), v, NN))
             context[r, lanes] = jnp.where(lower, results[0], results[1]).astype(BF)
         return carry
-    lax.fori_loop(0, width // (2 * HEAD), pair, 0)
+    lax.fori_loop(pairs[0], pairs[1], pair, 0)
 
 
 def attend_rows_back(qkv, upstream, weights, grads, query_at, key_at, queries, keys, items, group):
@@ -496,63 +508,158 @@
     return [c.wait for c in copies]
 
 
-def front_kernel(spans, items, group, x, cp_hbm, co_hbm, sp_hbm, so_hbm, cv, cg, sv, sg,
-                 qkv, ctx, n1, i1, rb, qkv2, e, n2, i2, p0, p1, p2, p3, cp, co, sp, so, hidden, sems):
-    waits = load([(cp_hbm, cp), (co_hbm, co), (sp_hbm, sp), (so_hbm, so)], sems)
+CV, CG, SV, SG, UB = 0, 4, 5, 13, 15
+
+
+def vector_rows(width, inner):
+    fv = UB + 2 * (inner // width)
+    return fv, fv + 4, -(-(fv + 6) // 16) * 16
+
+
+def front_sections(spans, items, group, x, vec, sources, weights, state, hidden, sems):
+    qkv, ctx, n1, i1, rb, qkv2, e, n2, i2, p0, p1, p2, p3 = state
+    cp, co, sp, so = weights
     width = x.shape[1]
     (a0, m0, w0), (a1, m1, w1) = spans
-    waits[0]()
-    for z, bias in ((0, 0), (1, None), (2, 1)):
-        def project(c, z=z, bias=bias):
+    out = []
+
+    def add(needs, call, *args):
+        out.append((frozenset(needs), functools.partial(call, *args)))
+
+    def fetch(k, src, dst):
+        pltpu.make_async_copy(src, dst, sems.at[k]).start()
+
+    def fetched(k, src, dst):
+        pltpu.make_async_copy(src, dst, sems.at[k]).wait()
+    moves = [(sources[0], cp), (sources[1], co), (sources[2].at[0], sp.at[0]), (sources[3].at[0], so.at[0]),
+             (sources[2].at[1], sp.at[1]), (sources[3].at[1], so.at[1])]
+
+    def project(z, bias):
+        def one(c):
             y = mm(x[...], cp[z, :, c], NN)
             if bias is not None:
-                y = y + cv[bias:bias + 1, c]
+                y = y + vec[CV + bias:CV + bias + 1, c]
             qkv[z, :, c] = y.astype(BF)
-        tiles(width, project)
-    attend_rows(qkv, ctx, p0, a0, a1, w0, w1, items, group)
-    attend_rows(qkv, ctx, p1, a1, a0, w1, w0, items, group)
-    waits[1]()
-
-    def branch(c):
-        hidden[:, c] = x[:, c].astype(F32) + (mm(ctx[...], co[:, c], NN) + cv[2:3, c])
-    tiles(width, branch)
-
-    def norm(r):
-        n, i = normed_rows(hidden[r, :])
-        n1[r, :] = n
-        i1[r, :] = i
-        rb[r, :] = (n * cg[...] + cv[3:4, :]).astype(BF)
-    chunks(0, x.shape[0], norm)
-    waits[2]()
-    waits[3]()
-    for s, (at, m, w, p) in enumerate(((a0, m0, w0, p2), (a1, m1, w1, p3))):
+        if z == 0:
+            fetched(0, *moves[0])
+        tiles(width, one)
+
+    def branch():
+        def one(c):
+            hidden[:, c] = x[:, c].astype(F32) + (mm(ctx[...], co[:, c], NN) + vec[CV + 2:CV + 3, c])
+
+        def norm(r):
+            n, i = normed_rows(hidden[r, :])
+            n1[r, :] = n
+            i1[r, :] = i
+            rb[r, :] = (n * vec[CG:CG + 1, :] + vec[CV + 3:CV + 4, :]).astype(BF)
+        fetched(1, *moves[1])
+        tiles(width, one)
+        chunks(0, x.shape[0], norm)
+
+    def self_project(s, z, bias):
+        rows = pl.ds(spans[s][0], spans[s][1])
+
+        def one(c):
+            y = mm(rb[rows, :], sp[s, z, :, c], NN)
+            if bias is not None:
+                y = y + vec[SV + 4 * s + bias:SV + 4 * s + bias + 1, c]
+            qkv2[z, rows, c] = y.astype(BF)
+        if z == 0:
+            fetched(2 + 2 * s, *moves[2 + 2 * s])
+        tiles(width, one)
+
+    def self_branch(s):
+        at, m, _ = spans[s]
         rows = pl.ds(at, m)
-        for z, bias in ((0, 0), (1, None), (2, 1)):
-            def project(c, z=z, bias=bias, s=s, rows=rows):
-                y = mm(rb[rows, :], sp[s, z, :, c], NN)
-                if bias is not None:
-                    y = y + sv[s, bias:bias + 1, c]
-                qkv2[z, rows, c] = y.astype(BF)
-            tiles(width, project)
-        attend_rows(qkv2, e, p, at, at, w, w, items, group)
-
-        def branch(c, s=s, rows=rows):
-            first = n1[rows, c] * cg[:, c] + cv[3:4, c]
-            hidden[rows, c] = first + (mm(e[rows, :], so[s, :, c], NN) + sv[s, 2:3, c])
-        tiles(width, branch)
+
+        def one(c):
+            first = n1[rows, c] * vec[CG:CG + 1, c] + vec[CV + 3:CV + 4, c]
+            hidden[rows, c] = first + (mm(e[rows, :], so[s, :, c], NN) + vec[SV + 4 * s + 2:SV + 4 * s + 3, c])
 
         def norm(r):
             n, i = normed_rows(hidden[r, :])
             n2[r, :] = n
             i2[r, :] = i
+        fetched(3 + 2 * s, *moves[3 + 2 * s])
+        tiles(width, one)
         chunks(at, m, norm)
 
-
-def feed_kernel(spans, n2, cot, fu_hbm, fd_hbm, sv, sg, ub, fv, fg,
+    heads = width // (2 * HEAD)
+    halves = ((0, heads // 2), (heads // 2, heads))
+    ways = ((0, 0), (1, None), (2, 1))
+    add({1, 2, 3}, fetch, 0, *moves[0])
+    for z, bias in ways:
+        add((), project, z, bias)
+    for pairs in halves:
+        add((), attend_rows, qkv, ctx, p0, a0, a1, w0, w1, items, group, pairs)
+    add({4}, fetch, 1, *moves[1])
+    for pairs in halves:
+        add((), attend_rows, qkv, ctx, p1, a1, a0, w1, w0, items, group, pairs)
+    add((), branch)
+    for s, p in ((0, p2), (1, p3)):
+        at, _, w = spans[s]
+        base = 5 + 4 * s
+        add({base, base + 1, base + 2}, fetch, 2 + 2 * s, *moves[2 + 2 * s])
+        for z, bias in ways:
+            add((), self_project, s, z, bias)
+        add({base + 3}, fetch, 3 + 2 * s, *moves[3 + 2 * s])
+        for pairs in halves:
+            add((), attend_rows, qkv2, e, p, at, at, w, w, items, group, pairs)
+        add((), self_branch, s)
+    return out
+
+
+def interleave(steps, sections, pace):
+    at, done = 0, set()
+    for needs, call in sections:
+        began = at
+        while at < len(steps) and (at < began + pace or not needs <= done):
+            step, part = steps[at]
+            step()
+            done.add(part)
+            at += 1
+        call()
+    for step, _ in steps[at:]:
+        step()
+
+
+PACE = 3
+
+
+def gather_front_kernel(axes, spans, items, group, x, *refs):
+    shards, fulls, vec, state = refs[:7], refs[7:14], refs[14], refs[15:28]
+    weights, hidden, small, sems = refs[28:32], refs[32], refs[33], refs[34]
+    gather = Gather(axes, shards, fulls, *refs[35:])
+    n = math.prod(s for s, _ in axes.values())
+
+    def vectors():
+        copy = pltpu.make_async_copy(fulls[6], small, sems.at[6])
+        copy.start()
+        copy.wait()
+        count = vec.shape[0]
+
+        def one(i, carry):
+            return carry + small[pl.ds(pl.multiple_of(i * count, count), count), :].astype(F32)
+        vec[...] = lax.fori_loop(0, n, one, jnp.zeros(vec.shape, F32))
+    sections = [(frozenset({0}), vectors)]
+    sections += front_sections(spans, items, group, x, vec, fulls, weights, state, hidden, sems)
+    interleave(gather.steps(), sections, PACE)
+    for p in range(len(PARTS)):
+        gather.finish(p)
+
+
+def plain_front_kernel(spans, items, group, x, vec, *refs):
+    sources, state, weights, hidden, sems = refs[:4], refs[4:17], refs[17:21], refs[21], refs[22]
+    interleave([], front_sections(spans, items, group, x, vec, sources, weights, state, hidden, sems), 0)
+
+
+def feed_kernel(spans, n2, cot, fu_hbm, fd_hbm, vec, ub,
                 out, dy2, gu_hbm, gd_hbm, gub, gfv, gfg, fu, fd, gu, gd, yb, act, slope, du, dz, hidden, sems, osems):
     streams = range(2)
     waits = load([(fu_hbm.at[0], fu.at[0]), (fd_hbm.at[0], fd.at[0]), (fu_hbm.at[1], fu.at[1]), (fd_hbm.at[1], fd.at[1])], sems)
     width, inner = fu.shape[1], fu.shape[2]
+    FV, FG, _ = vector_rows(width, inner)
     gfv[...] = jnp.zeros_like(gfv)
     gfg[...] = jnp.zeros_like(gfg)
     outgoing = []
@@ -561,7 +668,7 @@
         mine = pl.ds(0, m)
 
         def second(r, s=s):
-            return n2[r, :] * sg[s:s + 1, :] + sv[s, 3:4, :]
+            return n2[r, :] * vec[SG + s:SG + s + 1, :] + vec[SV + 4 * s + 3:SV + 4 * s + 4, :]
 
         def lowered(j, carry, s=s, at=at):
             yb[pl.ds(pl.multiple_of(j * 48, 16), 48), :] = second(pl.ds(pl.multiple_of(at + j * 48, 16), 48)).astype(BF)
@@ -579,17 +686,17 @@
 
         def down(c, s=s, mine=mine, at=at, m=m):
             rows = pl.ds(at, m)
-            y = n2[rows, c] * sg[s:s + 1, c] + sv[s, 3:4, c]
-            hidden[mine, c] = y + (mm(act[mine, :], fd[s, :, c], NN) + fv[s, 0:1, c])
+            y = n2[rows, c] * vec[SG + s:SG + s + 1, c] + vec[SV + 4 * s + 3:SV + 4 * s + 4, c]
+            hidden[mine, c] = y + (mm(act[mine, :], fd[s, :, c], NN) + vec[FV + 2 * s:FV + 2 * s + 1, c])
         tiles(width, down)
 
         def norms(j, carry, s=s, at=at):
             r = pl.ds(pl.multiple_of(j * 48, 16), 48)
             g = pl.ds(pl.multiple_of(at + j * 48, 16), 48)
             n, inverse = normed_rows(hidden[r, :])
-            out[g, :] = (n * fg[s:s + 1, :] + fv[s, 1:2, :]).astype(BF)
+            out[g, :] = (n * vec[FG + s:FG + s + 1, :] + vec[FV + 2 * s + 1:FV + 2 * s + 2, :]).astype(BF)
             upstream = cot[g, :].astype(F32)
-            dh = norm_rows_back(upstream, n, inverse, fg[s:s + 1, :])
+            dh = norm_rows_back(upstream, n, inverse, vec[FG + s:FG + s + 1, :])
             hidden[r, :] = dh
             z = dh.astype(BF)
             dz[r, :] = z
@@ -619,7 +726,7 @@
 
 
 def rear_kernel(spans, items, group, x, qkv, ctx, n1, i1, rb, qkv2, e, n2, i2, p0, p1, p2, p3, dy2,
-                cp_hbm, co_hbm, sp_hbm, so_hbm, cg, sg,
+                cp_hbm, co_hbm, sp_hbm, so_hbm, vec,
                 dx, gcp_hbm, gco_hbm, gsp_hbm, gso_hbm, gcv, gcg, gsv, gsg,
                 cp, co, sp, so, gcp, gco, gsp, gso, hidden, da, dctx, dqkv, sems, osems):
     waits = load([(so_hbm, so), (sp_hbm, sp), (co_hbm, co), (cp_hbm, cp)], sems)
@@ -643,7 +750,7 @@
 
         def norms(r, s=s):
             upstream, n = dy2[r, :], n2[r, :]
-            dh = norm_rows_back(upstream, n, i2[r, :], sg[s:s + 1, :])
+            dh = norm_rows_back(upstream, n, i2[r, :], vec[SG + s:SG + s + 1, :])
             hidden[r, :] = dh
             z = dh.astype(BF)
             da[r, :] = z
@@ -672,7 +779,7 @@
 
     def norms(r):
         upstream, n = hidden[r, :], n1[r, :]
-        dh = norm_rows_back(upstream, n, i1[r, :], cg[...])
+        dh = norm_rows_back(upstream, n, i1[r, :], vec[CG:CG + 1, :])
         hidden[r, :] = dh
         z = dh.astype(BF)
         da[r, :] = z
@@ -709,11 +816,8 @@
 VMEM_LIMIT = 64 * 1024 * 1024 - 70000
 
 
-def compute(x, cot, items, weights, vectors):
-    cp, co, sp, so, fu, fd = weights
-    cv, cg, sv, sg, ub, fv, fg = vectors
+def compute(axes, kernels, x, cot, items, shards, small):
     total_rows, width = x.shape
-    inner = fu.shape[2]
     words, regions = items
     count = words[0]
     spans = ((0, count * words[1], words[1]), (count * words[1], count * regions[1], regions[1]))
@@ -727,37 +831,56 @@
     rows_bf, rows_f, one = like((total_rows, width), BF), like((total_rows, width), F32), like((total_rows, 1), F32)
     three = like((3, total_rows, width), BF)
     w0, w1 = words[1], regions[1]
-    state = pl.pallas_call(
-        functools.partial(front_kernel, spans, count, group),
-        out_shape=[three, rows_bf, rows_f, one, rows_bf, three, rows_bf, rows_f, one,
-                   kept(w0, w1), kept(w1, w0), kept(w0, w0), kept(w1, w1)],
-        in_specs=[V, H, H, H, H, V, V, V, V], out_specs=[V] * 13,
-        scratch_shapes=[pltpu.VMEM(a.shape, a.dtype) for a in (cp, co, sp, so)]
-        + [pltpu.VMEM((total_rows, width), F32), pltpu.SemaphoreType.DMA((4,))],
-        compiler_params=params, name="front",
-    )(x, cp, co, sp, so, cv, cg, sv, sg)
+    state_shapes = [three, rows_bf, rows_f, one, rows_bf, three, rows_bf, rows_f, one,
+                    kept(w0, w1), kept(w1, w0), kept(w0, w0), kept(w1, w1)]
+    vec_shape = like(small.shape, F32)
+    weights = full_shapes(axes, shards)
+    held = [pltpu.VMEM(a.shape, a.dtype) for a in weights[:4]] + [pltpu.VMEM((total_rows, width), F32)]
+    if kernels:
+        fulls = full_shapes(axes, shards + [small])
+        results = pl.pallas_call(
+            functools.partial(gather_front_kernel, axes, spans, count, group),
+            out_shape=fulls + [vec_shape] + state_shapes,
+            in_specs=[V] * 8, out_specs=[H] * 7 + [V] * 14,
+            scratch_shapes=held + [pltpu.VMEM(fulls[6].shape, BF), pltpu.SemaphoreType.DMA((7,))] + gather_scratch(axes),
+            compiler_params=pltpu.CompilerParams(collective_id=0, has_side_effects=True, vmem_limit_bytes=VMEM_LIMIT),
+            name="gather_front",
+        )(x, *shards, small)
+        cp, co, sp, so, fu, fd = results[:6]
+        vec, state = results[7], results[8:]
+    else:
+        cp, co, sp, so, fu, fd = [lax.all_gather(a, "fsdp", axis=a.ndim - 2, tiled=True) for a in shards]
+        vec = lax.psum(small.astype(F32), "fsdp")
+        state = pl.pallas_call(
+            functools.partial(plain_front_kernel, spans, count, group),
+            out_shape=state_shapes, in_specs=[V, V] + [H] * 4, out_specs=[V] * 13,
+            scratch_shapes=held + [pltpu.SemaphoreType.DMA((7,))], compiler_params=params, name="front",
+        )(x, vec, cp, co, sp, so)
+    inner = fu.shape[2]
     most = max(m for _, m, _ in spans)
     n2 = state[7]
+    ub = vec[UB:UB + 2 * (inner // width)].reshape(2, inner)
     out, dy2, gu, gd, gub, gfv, gfg = pl.pallas_call(
         functools.partial(feed_kernel, spans),
         out_shape=[rows_bf, rows_f, like(fu.shape, BF), like(fd.shape, BF), like(ub.shape, F32),
-                   like(fv.shape, F32), like(fg.shape, F32)],
-        in_specs=[V, V, H, H, V, V, V, V, V], out_specs=[V, V, H, H, V, V, V],
+                   like((2, 2, width), F32), like((2, width), F32)],
+        in_specs=[V, V, H, H, V, V], out_specs=[V, V, H, H, V, V, V],
         scratch_shapes=[pltpu.VMEM(a.shape, BF) for a in (fu, fd, fu, fd)] + [
             pltpu.VMEM((most, width), BF), pltpu.VMEM((most, inner), BF), pltpu.VMEM((most, inner), F32),
             pltpu.VMEM((most, inner), BF), pltpu.VMEM((most, width), BF), pltpu.VMEM((most, width), F32),
             pltpu.SemaphoreType.DMA((4,)), pltpu.SemaphoreType.DMA((4,))],
         compiler_params=params, name="feed",
-    )(n2, cot, fu, fd, sv, sg, ub, fv, fg)
+    )(n2, cot, fu, fd, vec, ub)
     dx, gcp, gco, gsp, gso, gcv, gcg, gsv, gsg = pl.pallas_call(
         functools.partial(rear_kernel, spans, count, group),
-        out_shape=[rows_f] + [like(a.shape, BF) for a in (cp, co, sp, so)] + [like(a.shape, F32) for a in (cv, cg, sv, sg)],
-        in_specs=[V] * 15 + [H] * 4 + [V] * 2, out_specs=[V] + [H] * 4 + [V] * 4,
+        out_shape=[rows_f] + [like(a.shape, BF) for a in (cp, co, sp, so)]
+        + [like(s, F32) for s in ((4, width), (1, width), (2, 4, width), (2, width))],
+        in_specs=[V] * 15 + [H] * 4 + [V], out_specs=[V] + [H] * 4 + [V] * 4,
         scratch_shapes=[pltpu.VMEM(a.shape, BF) for a in (cp, co, sp, so) * 2] + [
             pltpu.VMEM((total_rows, width), F32), pltpu.VMEM((total_rows, width), BF), pltpu.VMEM((total_rows, width), BF),
             pltpu.VMEM((3, total_rows, width), BF), pltpu.SemaphoreType.DMA((4,)), pltpu.SemaphoreType.DMA((6,))],
         compiler_params=params, name="rear",
-    )(x, *state, dy2, cp, co, sp, so, cg, sg)
+    )(x, *state, dy2, cp, co, sp, so, vec)
     return out, dx, (gcp, gco, gsp, gso, gu, gd), (gcv, gcg, gsv, gsg, gub, gfv, gfg)
 
 
@@ -779,10 +902,15 @@
     return out
 
 
-def gather_all(axes, kernels, shards):
-    if kernels:
-        return gather_call(axes, shards)
-    return [lax.all_gather(s, "fsdp", axis=s.ndim - 2, tiled=False) for s in shards]
+def spread(small, n, rows):
+    me = lax.axis_index("fsdp")
+    placed = []
+    for v in small:
+        whole = jnp.zeros(v.shape[:-1] + (n * v.shape[-1],), v.dtype)
+        placed.append(lax.dynamic_update_slice_in_dim(whole, v, me * v.shape[-1], axis=v.ndim - 1))
+    width = placed[1].shape[-1]
+    flat = jnp.concatenate([p.reshape(-1, width) for p in placed])
+    return jnp.pad(flat, [(0, rows - flat.shape[0]), (0, 0)])
 
 
 def scatter_all(axes, kernels, grads):
@@ -828,30 +956,21 @@
     small_shapes = [s.shape for s in small]
     granule = 1024 if kernels else 128
     big = [cross_project, cross_output, self_project, self_output, feed_up, feed_down]
-    gathered = gather_all(axes, kernels, big + [bundle(small, (), granule)])
-    merged = [
-        g.reshape(g.shape[:-3] + (g.shape[-3] * g.shape[-2], g.shape[-1])) for g in gathered[:6]
-    ]
-    cross_project, cross_output, self_project, self_output, feed_up, feed_down = merged
-    vectors = []
-    for v in unbundle(gathered[6].astype(F32), (n,), small_shapes):
-        v = jnp.moveaxis(v, 0, -2)
-        vectors.append(v.reshape(v.shape[:-2] + (-1,)))
-    cross_vector, cross_gain, self_vector, self_gain, feed_up_bias, feed_vector, feed_gain = vectors
-
     words, regions = language.shape[1], vision.shape[1]
     masked = [
         (c.astype(F32) * task_flags[:, s].astype(F32)[:, None, None]).astype(BF).reshape(-1, width)
         for s, c in enumerate(cotangents)
     ]
     out, rows_grad, big_grads, small_grads = compute(
+        axes,
+        kernels,
         jnp.concatenate(streams),
         jnp.concatenate(masked),
         ((item_count, words), (item_count, regions)),
-        (cross_project, cross_output, self_project, self_output, feed_up, feed_down),
-        (cross_vector, cross_gain[None], self_vector, self_gain, feed_up_bias, feed_vector, feed_gain),
+        big,
+        spread(small, n, vector_rows(width, feed_up.shape[-1])[2]),
     )
-    small_grads = [g.reshape(v.shape) for g, v in zip(small_grads, vectors)]
+    small_grads = [g.reshape(v.shape[:-1] + (-1,)) for g, v in zip(small_grads, small)]
     small_grads = [
         jnp.moveaxis(g.reshape(g.shape[:-1] + (n, g.shape[-1] // n)), -2, 0) for g in small_grads
     ]

time: 605 us -> 519 us (0.86)
  Pallas kernels: 559 us -> 479 us
    pallas_call x2 -> x1, Pallas kernels: 235 us -> 192 us  [compute(): pl.pallas_call(functools.partial(gather_front_kernel, axes, spans, count,...]
    pallas_call x1, Pallas kernels: 212 us -> 175 us  [scatter_call(): pl.pallas_call(functools.partial(scatter_kernel, axes, parts, len(grads))...]
where the time goes in v3:
time: 519 us; the launch traced here: 518 us
  Pallas kernels  479 us (92%)
  local copies, waits for them, and re-layouts  29.2 us (6%)
  other arithmetic  8.77 us (2%)
    pallas_call x1, Pallas kernels, compute(): pl.pallas_call(functools.partial(gather_front_kernel, axes, spans, count,...  192 us
    pallas_call x1, Pallas kernels, scatter_call(): pl.pallas_call(functools.partial(scatter_kernel, axes, parts, len(grads))...  175 us
    pallas_call x1, Pallas kernels, compute(): pl.pallas_call(functools.partial(rear_kernel, spans, count, group), out_s...  71.7 us
    pallas_call x1, Pallas kernels, compute(): pl.pallas_call(functools.partial(feed_kernel, spans), out_shape=[rows_bf,...  40.3 us

profile of v3, /device:TPU:0, one launch (start us, length us, event | category | flops | bytes accessed | tf_op | source)
XLA Modules:
  0.0 518.1 jit_solution(692353004600759868)
XLA Ops:
  0.7 0.8 convert_bitcast_fusion.1
  1.4 0.8 dynamic_update_slice.25
  2.2 0.8 dynamic_update_slice.28
  3.0 0.8 dynamic_update_slice.23
  3.8 0.8 dynamic_update_slice.27
  4.7 0.8 dynamic_update_slice.22
  5.5 0.8 dynamic_update_slice.26
  6.4 0.8 dynamic_update_slice.24
  8.3 1.1 multiply_convert_fusion.1
  9.3 1.1 reshape.176
  10.4 0.9 pad_maximum_fusion.x
  11.6 0.9 pad_maximum_fusion.1.cot
  12.4 192.2 %gather_front.1 = (bf16[3,768,768]{2,1,0:T(8,128)(2,1)}, bf16[768,768]{1,0:T(8,128)(2,1)}, bf16[2,3,768,768]{3,2,1,0:T(8,128)(2,1)}, bf16[2,768,768]{2,1,0:T(8,1...) custom-call(bf16[432,768]{1,0:T(8,128)(2,1)} %pad_maximum_fusion.x, ...), custom_call_target="tpu_custom_call" | custom-call | tf_op jit(solution)/shard_map/gather_front/pallas_call | solution.py:841
  204.7 0.8 slice.44
  206.1 40.3 %feed.1 = (bf16[432,768]{1,0:T(8,128)(2,1)}, f32[432,768]{1,0:T(8,128)}, bf16[2,768,3072]{2,1,0:T(8,128)(2,1)}, bf16[2,3072,768]{2,1,0:T(8,128)(2,1)}, f32[2,307...) custom-call(f32[432,768]{1,0:T(8,128)} %get-tuple-element.60.n2, bf16[432,768]{1,0:T(8,128)(2,1)} %pad_maximum_fusion.1.cot, ...), custom_call_target="tpu_custom_call" | custom-call | tf_op jit(solution)/shard_map/feed/pallas_call | solution.py:863
  246.4 71.7 %rear.1 = (f32[432,768]{1,0:T(8,128)}, bf16[3,768,768]{2,1,0:T(8,128)(2,1)}, bf16[768,768]{1,0:T(8,128)(2,1)}, bf16[2,3,768,768]{3,2,1,0:T(8,128)(2,1)}, bf16[2,...) custom-call(bf16[432,768]{1,0:T(8,128)(2,1)} %pad_maximum_fusion.x, ...), custom_call_target="tpu_custom_call" | custom-call | tf_op jit(solution)/shard_map/rear/pallas_call | solution.py:874
  320.3 0.7 convert.42
  321.8 0.7 convert.44
  322.5 0.7 convert.46
  325.5 174.9 %scatter.1 = (f32[3,24,768]{2,1,0:T(8,128)}, f32[24,768]{1,0:T(8,128)}, f32[2,3,24,768]{3,2,1,0:T(8,128)}, f32[2,24,768]{2,1,0:T(8,128)}, f32[2,24,3072]{2,1,0:T...) custom-call(bf16[3,32,24,768]{3,2,1,0:T(8,128)(2,1)} %bitcast.30, bf16[32,24,768]{2,1,0:T(8,128)(2,1)} %bitcast.32, ...), custom_call_target="tpu_custom_call" | custom-call | tf_op jit(solution)/shard_map/scatter/pallas_call | solution.py:379
  500.4 1.4 slice.50
  501.8 0.8 fusion
  503.9 0.8 fusion.1
  504.7 0.8 fusion.2
  508.2 1.7 slice.46
  509.9 1.0 slice.45
  510.9 0.8 reshape.185
  511.7 0.9 slice.48
  512.7 1.0 reshape.187
  515.0 0.8 copy.66
  516.4 0.8 copy.68
  517.2 0.8 copy.69
  (69 shorter events, 13.1 us)
Async XLA Ops:
  0.7 9.8 %copy-start.5 = (bf16[12,16,768]{2,1,0:T(8,128)(2,1)S(1)}, bf16[12,16,768]{2,1,0:T(8,128)(2,1)}, u32[]{:S(2)}) copy-start(bf16[12,16,768]{2,1,0:T(8,128)(2,1)} %param.19) | copy-start | bytes 884740
  7.2 4.1 copy-start.3
  500.4 11.3 %copy-start = (f32[432,768]{1,0:T(8,128)S(1)}, f32[432,768]{1,0:T(8,128)}, u32[]{:S(2)}) copy-start(f32[432,768]{1,0:T(8,128)} %get-tuple-element.82) | copy-start | bytes 3981316
  512.6 1.1 copy-start.6
  512.6 1.8 copy-start.8
  512.6 2.3 copy-start.4
  512.7 3.1 copy-start.7
  512.7 3.8 copy-start.2
  513.7 3.6 copy-start.1

commit v4 on v3

--- a/solution.py
+++ b/solution.py
@@ -81,21 +81,35 @@
     return total
 
 
-LAG = 2
+LAG = 3
 
 PARTS = (
     (6, (), "xzy", None),
     (0, (0,), "zyx", None), (0, (1,), "zxy", None), (0, (2,), "zyx", None), (1, (), "xzy", None),
     (2, (0, 0), "zxy", None), (2, (0, 1), "zyx", None), (2, (0, 2), "zxy", None), (3, (0,), "yzx", None),
     (2, (1, 0), "zyx", None), (2, (1, 1), "zxy", None), (2, (1, 2), "zyx", None), (3, (1,), "xzy", None),
-    (4, (0,), "zxy", (1, 0)), (4, (0,), "zyx", (1, 1)), (5, (0,), "zxy", (0, 0)), (5, (0,), "yzx", (0, 1)),
-    (4, (1,), "zyx", (1, 0)), (4, (1,), "zxy", (1, 1)), (5, (1,), "zyx", (0, 0)), (5, (1,), "xzy", (0, 1)),
+    (4, (0,), "zxy", (1, 0, 4)),
+    (5, (0,), "zyx", (0, 0, 4)),
+    (4, (0,), "yzx", (1, 1, 4)),
+    (5, (0,), "zxy", (0, 1, 4)),
+    (4, (0,), "zyx", (1, 2, 4)),
+    (5, (0,), "zxy", (0, 2, 4)),
+    (4, (0,), "xzy", (1, 3, 4)),
+    (5, (0,), "zyx", (0, 3, 4)),
+    (4, (1,), "zxy", (1, 0, 4)),
+    (5, (1,), "zyx", (0, 0, 4)),
+    (4, (1,), "yzx", (1, 1, 4)),
+    (5, (1,), "zxy", (0, 1, 4)),
+    (4, (1,), "zyx", (1, 2, 4)),
+    (5, (1,), "zxy", (0, 2, 4)),
+    (4, (1,), "xzy", (1, 3, 4)),
+    (5, (1,), "zyx", (0, 3, 4)),
 )
 
 def extent(shape, sub):
     if sub is None:
         return tuple(shape)
-    return tuple(s // 2 if d == sub[0] else s for d, s in enumerate(shape))
+    return tuple(s // sub[2] if d == sub[0] else s for d, s in enumerate(shape))
 
 
 class Gather:
@@ -116,7 +130,7 @@
         shard, _, _, sub, shape = self.cut(p)
         if sub is None:
             return shard
-        size = shape[sub[0]] // 2
+        size = shape[sub[0]] // sub[2]
         w = pl.ds(sub[1] * size, size)
         return shard.at[w] if sub[0] == 0 else shard.at[:, w]
 
@@ -125,9 +139,9 @@
         if sub is None:
             return full.at[pl.ds(pl.multiple_of(at * r, 8), many * r)]
         if sub[0] == 0:
-            size = r // 2
+            size = r // sub[2]
             return full.at[pl.ds(pl.multiple_of(at * r + (sub[1] * size if many == 1 else 0), 8), many * size)]
-        size = c // 2
+        size = c // sub[2]
         return full.at[pl.ds(pl.multiple_of(at * r, 8), many * r), pl.ds(sub[1] * size, size)]
 
     def remote(self, src, dst, ss, rs, to):
@@ -232,163 +246,189 @@
 def window(sub, shape):
     if sub is None:
         return (slice(None), slice(None))
-    size = shape[sub[0]] // 2
+    size = shape[sub[0]] // sub[2]
     w = pl.ds(sub[1] * size, size)
     return (w, slice(None)) if sub[0] == 0 else (slice(None), w)
 
 
-def scatter_kernel(axes, parts, narrays, *refs):
-    grads, outs = refs[:narrays], refs[narrays:2 * narrays]
-    rest = refs[2 * narrays:]
-    P = len(parts)
-    held, landed = rest[:P], [rest[P * (1 + s):P * (2 + s)] for s in range(4)]
-    send, recv, local = rest[5 * P:]
-    place = Place(axes)
-    chip_axes = "xyz"
-
-    def chip_index(to):
+class Scatter:
+    def __init__(self, place, parts, grads, outs, refs):
+        self.place, self.axes, self.parts, self.grads, self.outs = place, place.axes, parts, grads, outs
+        count = len(parts)
+        self.held = refs[:count]
+        self.landed = [refs[count * (1 + s):count * (2 + s)] for s in range(4)]
+        self.send, self.recv, self.local = refs[5 * count:]
+        self.mine, self.theirs = place.at["c"], 1 - place.at["c"]
+        self.other = place.index(c=self.theirs)
+        self.n = math.prod(s for s, _ in self.axes.values())
+
+    def chip_index(self, to):
         i = 0
         for k in "zyx":
-            i = i * axes[k][0] + to.get(k, place.at[k])
+            i = i * self.axes[k][0] + to.get(k, self.place.at[k])
         return i
 
-    def grad(p, i):
-        a, lead, _, sub = parts[p]
-        return grads[a].at[lead + (i,) + window(sub, grads[a].shape[-2:])]
-
-    def loop(names, fixed, body):
-        total = 1
+    def shard_shape(self, p):
+        rows, columns = self.grads[self.parts[p][0]].shape[-2:]
+        return rows // self.n, columns
+
+    def grad(self, p, i):
+        a, lead, _, sub = self.parts[p]
+        r, c = self.shard_shape(p)
+        full = self.grads[a].at[lead] if lead else self.grads[a]
+        if sub is None:
+            return full.at[pl.ds(pl.multiple_of(i * r, 8), r)]
+        if sub[0] == 0:
+            return full.at[pl.ds(pl.multiple_of(i * r + sub[1] * (r // sub[2]), 8), r // sub[2])]
+        return full.at[pl.ds(pl.multiple_of(i * r, 8), r), pl.ds(sub[1] * (c // sub[2]), c // sub[2])]
+
+    def loop(self, names, fixed, body):
+        count = 1
         for k in names:
-            total *= axes[k][0]
+            count *= self.axes[k][0]
 
         def step(n, carry):
             to, i = dict(fixed), n
             for k in names:
-                to[k] = lax.rem(i, axes[k][0])
-                i = lax.div(i, axes[k][0])
+                to[k] = lax.rem(i, self.axes[k][0])
+                i = lax.div(i, self.axes[k][0])
             body(to, n)
             return carry
-        if total == 1:
+        if count == 1:
             step(0, 0)
         else:
-            lax.fori_loop(0, total, step, 0)
-        return total
-
-    def remote(src, dst, ss, rs, to):
-        return pltpu.make_async_remote_copy(src_ref=src, dst_ref=dst, send_sem=ss, recv_sem=rs,
-                                            device_id=(to,), device_id_type=MESH)
-
-    place.barrier()
-    mine, theirs = place.at["c"], 1 - place.at["c"]
-    other = place.index(c=theirs)
-
-    def begin(p):
+            lax.fori_loop(0, count, step, 0)
+
+    def remote(self, src, dst, p, stage, d, to):
+        return pltpu.make_async_remote_copy(src_ref=src, dst_ref=dst, send_sem=self.send.at[p, stage, d],
+                                            recv_sem=self.recv.at[p, stage, d], device_id=(to,), device_id_type=MESH)
+
+    def begin(self, p):
+        place = self.place
+
         def one(to, n):
-            remote(grad(p, place.index(c=theirs, **to)), landed[0][p].at[chip_index(to)],
-                   send.at[p, 0, 0], recv.at[p, 0, 0], other).start()
-            pltpu.make_async_copy(grad(p, place.index(c=mine, **to)), held[p].at[chip_index(to)], local.at[p]).start()
-        loop(chip_axes, {}, one)
-
-    def first(p):
-        whole = held[p]
-        pltpu.make_async_copy(whole, whole, local.at[p]).wait()
-        c = remote(whole, landed[0][p], send.at[p, 0, 0], recv.at[p, 0, 0], other)
-        c.wait_recv()
+            i = self.chip_index(to)
+            self.remote(self.grad(p, place.index(c=self.theirs, **to)), self.landed[0][p].at[i], p, 0, 0, self.other).start()
+            pltpu.make_async_copy(self.grad(p, place.index(c=self.mine, **to)), self.held[p].at[i], self.local.at[p]).start()
+        self.loop("xyz", {}, one)
+
+    def first(self, p):
+        held, landed = self.held[p], self.landed[0][p]
+        pltpu.make_async_copy(held, held, self.local.at[p]).wait()
+        self.remote(held, landed, p, 0, 0, self.other).wait_recv()
 
         def one(n, carry):
-            held[p][n] = held[p][n] + landed[0][p][n]
+            held[n] = held[n] + landed[n]
             return carry
-        lax.fori_loop(0, held[p].shape[0], one, 0)
-
-    def distance(frm, to, axis):
-        m = axes[axis][0]
-        return lax.rem(frm - to + m, m) - 1
-
-    def pass_on(p, stage):
-        order = parts[p][2]
+        lax.fori_loop(0, held.shape[0], one, 0)
+        self.pass_on(p, 1)
+
+    def pass_on(self, p, stage):
+        order, place = self.parts[p][2], self.place
         axis, free = order[3 - stage], order[:3 - stage]
+        m = self.axes[axis][0]
         for peer in place.peers(axis):
             to_device = place.index(**{axis: peer})
-            d = distance(place.at[axis], peer, axis)
+            d = lax.rem(place.at[axis] - peer + m, m) - 1
 
             def one(to, n):
-                remote(held[p].at[chip_index(to)], landed[stage][p].at[d, n],
-                       send.at[p, stage, d], recv.at[p, stage, d], to_device).start()
-            loop(free, {axis: peer}, one)
-
-    def take(p, stage):
-        order = parts[p][2]
+                self.remote(self.held[p].at[self.chip_index(to)], self.landed[stage][p].at[d, n], p, stage, d, to_device).start()
+            self.loop(free, {axis: peer}, one)
+
+    def take(self, p, stage):
+        a, lead, order, sub = self.parts[p]
         axis, free = order[3 - stage], order[:3 - stage]
-        m = axes[axis][0]
+        landed = self.landed[stage][p]
+        m = self.axes[axis][0]
         for d in range(m - 1):
-            ref = landed[stage][p].at[d]
-            remote(ref, ref, send.at[p, stage, d], recv.at[p, stage, d], other).wait_recv()
+            self.remote(landed.at[d], landed.at[d], p, stage, d, self.other).wait_recv()
 
         def one(to, n):
-            i = chip_index(to)
-            total = held[p][i].astype(F32)
+            i = self.chip_index(to)
+            result = self.held[p][i].astype(F32)
             for d in range(m - 1):
-                total = total + landed[stage][p][d, n].astype(F32)
+                result = result + landed[d, n].astype(F32)
             if stage == 3:
-                a, lead, _, sub = parts[p]
-                outs[a][lead + window(sub, grads[a].shape[-2:])] = total
+                self.outs[a][lead + window(sub, self.shard_shape(p))] = result
             else:
-                held[p][i] = total.astype(BF)
-        loop(free, {}, one)
-
-    def finish(p):
-        whole = held[p]
-        remote(whole, whole, send.at[p, 0, 0], recv.at[p, 0, 0], other).wait_send()
+                self.held[p][i] = result.astype(BF)
+        self.loop(free, {}, one)
+        if stage < 3:
+            self.pass_on(p, stage + 1)
+
+    def finish(self, p):
+        self.remote(self.held[p], self.held[p], p, 0, 0, self.other).wait_send()
         for stage in range(1, 4):
-            axis = parts[p][2][3 - stage]
-            for d in range(axes[axis][0] - 1):
-                ref = landed[stage][p].at[d]
-                remote(ref, ref, send.at[p, stage, d], recv.at[p, stage, d], other).wait_send()
-
-    for p in range(P):
-        begin(p)
-    for t in range(P + 3 * LAG):
-        if t < P:
-            first(t)
-            pass_on(t, 1)
-        for stage in (1, 2, 3):
-            p = t - stage * LAG
-            if 0 <= p < P:
-                take(p, stage)
-                if stage < 3:
-                    pass_on(p, stage + 1)
-    for p in range(P):
-        finish(p)
-
-
-def scatter_call(axes, grads, parts):
-    outs = [jax.ShapeDtypeStruct(g.shape[:-3] + g.shape[-2:], F32) for g in grads]
+            for d in range(self.axes[self.parts[p][2][3 - stage]][0] - 1):
+                ref = self.landed[stage][p].at[d]
+                self.remote(ref, ref, p, stage, d, self.other).wait_send()
+
+    def steps(self, which):
+        count, ahead, out = len(which), 3, []
+        for t in range(-ahead, count + 3 * LAG):
+            if 0 <= t + ahead < count:
+                out.append((functools.partial(self.begin, which[t + ahead]), None))
+            if 0 <= t < count:
+                out.append((functools.partial(self.first, which[t]), None))
+            for stage in (1, 2, 3):
+                at = t - stage * LAG
+                if 0 <= at < count:
+                    out.append((functools.partial(self.take, which[at], stage), None))
+        return out
+
+
+def scatter_scratch(axes, parts, shapes):
     most = max(max(s for s, _ in axes.values()) - 1, 1)
-    P = len(parts)
+    chips = math.prod(axes[k][0] for k in "xyz")
     held, landed = [], [[], [], [], []]
     for a, lead, order, sub in parts:
-        shard = extent(grads[a].shape[-2:], sub)
-        chips = grads[a].shape[-3] // 2
+        shard = extent(shapes[a], sub)
         held.append(pltpu.VMEM((chips,) + shard, BF))
         landed[0].append(pltpu.VMEM((chips,) + shard, BF))
         for stage in range(1, 4):
-            f = 1
-            for k in order[:3 - stage]:
-                f *= axes[k][0]
+            f = math.prod(axes[k][0] for k in order[:3 - stage])
             landed[stage].append(pltpu.VMEM((max(axes[order[3 - stage]][0] - 1, 1), f) + shard, BF))
-    return pl.pallas_call(
-        functools.partial(scatter_kernel, axes, parts, len(grads)),
-        out_shape=outs,
-        in_specs=[pl.BlockSpec(memory_space=pltpu.HBM)] * len(grads),
-        out_specs=[pl.BlockSpec(memory_space=pltpu.VMEM)] * len(grads),
-        scratch_shapes=held + landed[0] + landed[1] + landed[2] + landed[3] + [
-            pltpu.SemaphoreType.DMA((P, 4, most)),
-            pltpu.SemaphoreType.DMA((P, 4, most)),
-            pltpu.SemaphoreType.DMA((P,)),
-        ],
-        compiler_params=pltpu.CompilerParams(collective_id=1, has_side_effects=True, vmem_limit_bytes=64 * 1024 * 1024 - 70000),
-        name="scatter",
-    )(*grads)
+    count = len(parts)
+    return held + sum(landed, []) + [
+        pltpu.SemaphoreType.DMA((count, 4, most)), pltpu.SemaphoreType.DMA((count, 4, most)), pltpu.SemaphoreType.DMA((count,)),
+    ]
+
+
+class Total:
+    ORDER = "cxyz"
+
+    def __init__(self, place, sums, landed, send, recv):
+        self.place, self.sums, self.landed, self.send, self.recv = place, sums, landed, send, recv
+
+    def copy(self, k, d, to):
+        return pltpu.make_async_remote_copy(src_ref=self.sums.at[k], dst_ref=self.landed.at[k, d], send_sem=self.send.at[k, d],
+                                            recv_sem=self.recv.at[k, d], device_id=(to,), device_id_type=MESH)
+
+    def pass_on(self, k):
+        axis = self.ORDER[k]
+        m = self.place.axes[axis][0]
+        for peer in self.place.peers(axis):
+            d = lax.rem(self.place.at[axis] - peer + m, m) - 1
+            self.copy(k, d, self.place.index(**{axis: peer})).start()
+
+    def take(self, k):
+        m = self.place.axes[self.ORDER[k]][0]
+        for d in range(m - 1):
+            c = self.copy(k, d, self.place.index(c=1 - self.place.at["c"]))
+            c.wait_recv()
+            c.wait_send()
+        result = self.sums[k]
+        for d in range(m - 1):
+            result = result + self.landed[k, d]
+        self.sums[k + 1] = result
+        if k < 3:
+            self.pass_on(k + 1)
+
+
+def total_scratch(axes, shape):
+    most = max(max(s for s, _ in axes.values()) - 1, 1)
+    return [pltpu.VMEM((5,) + shape, F32), pltpu.VMEM((4, most) + shape, F32),
+            pltpu.SemaphoreType.DMA((4, most)), pltpu.SemaphoreType.DMA((4, most))]
 
 
 TILE = 256
@@ -457,8 +497,7 @@
     lax.fori_loop(pairs[0], pairs[1], pair, 0)
 
 
-def attend_rows_back(qkv, upstream, weights, grads, query_at, key_at, queries, keys, items, group):
-    width = qkv.shape[2]
+def attend_rows_back(qkv, upstream, weights, grads, query_at, key_at, queries, keys, items, group, pairs):
     rows, cols = group * queries, group * keys
     lower, lower_keys = lower_half(rows), lower_half(cols)
     scale = HEAD ** (-0.5)
@@ -482,7 +521,7 @@
             grads[1, c, lanes] = (jnp.where(lower_keys, dk[0], dk[1]) * scale).astype(BF)
             grads[2, c, lanes] = jnp.where(lower_keys, dv[0], dv[1]).astype(BF)
         return carry
-    lax.fori_loop(0, width // (2 * HEAD), pair, 0)
+    lax.fori_loop(pairs[0], pairs[1], pair, 0)
 
 
 def normed_rows(hidden):
@@ -725,92 +764,208 @@
         copy.wait()
 
 
-def rear_kernel(spans, items, group, x, qkv, ctx, n1, i1, rb, qkv2, e, n2, i2, p0, p1, p2, p3, dy2,
-                cp_hbm, co_hbm, sp_hbm, so_hbm, vec,
-                dx, gcp_hbm, gco_hbm, gsp_hbm, gso_hbm, gcv, gcg, gsv, gsg,
-                cp, co, sp, so, gcp, gco, gsp, gso, hidden, da, dctx, dqkv, sems, osems):
-    waits = load([(so_hbm, so), (sp_hbm, sp), (co_hbm, co), (cp_hbm, cp)], sems)
-    width = x.shape[1]
-    (a0, m0, w0), (a1, m1, w1) = spans
-    outgoing = []
-
-    def leave(src, dst):
-        copy = pltpu.make_async_copy(src, dst, osems.at[len(outgoing)])
-        copy.start()
-        outgoing.append(copy)
-
-    gsv[...] = jnp.zeros_like(gsv)
-    gsg[...] = jnp.zeros_like(gsg)
-    gcv[...] = jnp.zeros_like(gcv)
-    gcg[...] = jnp.zeros_like(gcg)
-    waits[0]()
-    waits[1]()
-    for s, (at, m, w, p) in enumerate(((a0, m0, w0, p2), (a1, m1, w1, p3))):
-        rows = pl.ds(at, m)
-
-        def norms(r, s=s):
+def halves_of(heads):
+    return ((0, heads // 2), (heads // 2, heads))
+
+
+def self_back_sections(spans, items, group, rb, qkv2, e, n2, i2, p2, p3, dy2, vec, sp_hbm, so_hbm,
+                       dy1, gsp_hbm, gso_hbm, gsv, gsg, sp, so, gsp, gso, da, dctx, dqkv, sems, osems):
+    width = rb.shape[1]
+    moves = [(so_hbm, so), (sp_hbm, sp)]
+    leaving = [(gso, gso_hbm, s) for s in range(2)] + [(gsp, gsp_hbm, s) for s in range(2)]
+    out = []
+
+    def leave(k):
+        src, dst, s = leaving[k]
+        return pltpu.make_async_copy(src.at[s], dst.at[s], osems.at[k])
+
+    def begin():
+        for k, (src, dst) in enumerate(moves):
+            pltpu.make_async_copy(src, dst, sems.at[k]).start()
+        gsv[...] = jnp.zeros_like(gsv)
+        gsg[...] = jnp.zeros_like(gsg)
+
+    def norms(s):
+        def one(r):
             upstream, n = dy2[r, :], n2[r, :]
             dh = norm_rows_back(upstream, n, i2[r, :], vec[SG + s:SG + s + 1, :])
-            hidden[r, :] = dh
+            dy1[r, :] = dh
             z = dh.astype(BF)
             da[r, :] = z
             gsg[s:s + 1, :] += total(upstream * n)
             gsv[s, 2:3, :] += total(z.astype(F32))
             gsv[s, 3:4, :] += total(upstream)
-        chunks(at, m, norms)
-
-        def output_back(c, s=s, rows=rows):
+        if s == 0:
+            begin()
+        chunks(spans[s][0], spans[s][1], one)
+
+    def output_back(s):
+        rows = pl.ds(spans[s][0], spans[s][1])
+
+        def one(c):
             dctx[rows, c] = mm(da[rows, :], so[s, c, :], NT).astype(BF)
             gso[s, c, :] = mm(e[rows, c], da[rows, :], TN).astype(BF)
-        tiles(width, output_back)
-        leave(gso.at[s], gso_hbm.at[s])
-        attend_rows_back(qkv2, dctx, p, dqkv, at, at, w, w, items, group)
-
-        def sums(c, s=s, rows=rows):
-            gsv[s, 0:1, c] = total(dqkv[0, rows, c].astype(F32))
-            gsv[s, 1:2, c] = total(dqkv[2, rows, c].astype(F32))
-        tiles(width, sums)
+        if s == 0:
+            for k, (src, dst) in enumerate(moves):
+                pltpu.make_async_copy(src, dst, sems.at[k]).wait()
+        tiles(width, one)
+        leave(s).start()
+
+    def project_back(s, z):
+        rows = pl.ds(spans[s][0], spans[s][1])
+
+        def one(c):
+            gsp[s, z, :, c] = mm(rb[rows, :], dqkv[z, rows, c], TN).astype(BF)
+            dy1[rows, c] = dy1[rows, c] + mm(dqkv[z, rows, :], sp[s, z, c, :], NT)
+            if z != 1:
+                gsv[s, z // 2:z // 2 + 1, c] = total(dqkv[z, rows, c].astype(F32))
+        tiles(width, one)
+        if z == 2:
+            leave(2 + s).start()
+    for s, p in ((0, p2), (1, p3)):
+        at, _, w = spans[s]
+        out.append(functools.partial(norms, s))
+        out.append(functools.partial(output_back, s))
+        for pairs in halves_of(width // (2 * HEAD)):
+            out.append(functools.partial(attend_rows_back, qkv2, dctx, p, dqkv, at, at, w, w, items, group, pairs))
         for z in range(3):
-            def project_back(c, s=s, z=z, rows=rows):
-                gsp[s, z, :, c] = mm(rb[rows, :], dqkv[z, rows, c], TN).astype(BF)
-                hidden[rows, c] = hidden[rows, c] + mm(dqkv[z, rows, :], sp[s, z, c, :], NT)
-            tiles(width, project_back)
-        leave(gsp.at[s], gsp_hbm.at[s])
-
-    def norms(r):
-        upstream, n = hidden[r, :], n1[r, :]
-        dh = norm_rows_back(upstream, n, i1[r, :], vec[CG:CG + 1, :])
-        hidden[r, :] = dh
-        z = dh.astype(BF)
-        da[r, :] = z
-        gcg[...] += total(upstream * n)
-        gcv[2:3, :] += total(z.astype(F32))
-        gcv[3:4, :] += total(upstream)
-    chunks(0, x.shape[0], norms)
-    waits[2]()
-    waits[3]()
-
-    def output_back(c):
-        dctx[:, c] = mm(da[...], co[c, :], NT).astype(BF)
-        gco[c, :] = mm(ctx[:, c], da[...], TN).astype(BF)
-    tiles(width, output_back)
-    leave(gco, gco_hbm)
-    attend_rows_back(qkv, dctx, p0, dqkv, a0, a1, w0, w1, items, group)
-    attend_rows_back(qkv, dctx, p1, dqkv, a1, a0, w1, w0, items, group)
-
-    def sums(c):
-        gcv[0:1, c] = total(dqkv[0, :, c].astype(F32))
-        gcv[1:2, c] = total(dqkv[2, :, c].astype(F32))
-    tiles(width, sums)
+            out.append(functools.partial(project_back, s, z))
+
+    def end():
+        for k in range(4):
+            leave(k).wait()
+    return out, end
+
+
+def cross_back_sections(spans, items, group, x, qkv, ctx, n1, i1, p0, p1, dy1, vec, cp_hbm, co_hbm,
+                        dx, gcp_hbm, gco_hbm, gcv, cp, co, gcp, gco, da, dctx, dqkv, sems, osems):
+    width = x.shape[1]
+    (a0, m0, w0), (a1, m1, w1) = spans
+    moves = [(co_hbm, co), (cp_hbm, cp)]
+    leaving = [(gco, gco_hbm), (gcp, gcp_hbm)]
+    out = []
+
+    def leave(k):
+        return pltpu.make_async_copy(*leaving[k], osems.at[k])
+
+    def norms():
+        for k, (src, dst) in enumerate(moves):
+            pltpu.make_async_copy(src, dst, sems.at[k]).start()
+        gcv[...] = jnp.zeros_like(gcv)
+
+        def one(r):
+            upstream, n = dy1[r, :], n1[r, :]
+            dh = norm_rows_back(upstream, n, i1[r, :], vec[CG:CG + 1, :])
+            dx[r, :] = dh
+            z = dh.astype(BF)
+            da[r, :] = z
+            gcv[4:5, :] += total(upstream * n)
+            gcv[2:3, :] += total(z.astype(F32))
+            gcv[3:4, :] += total(upstream)
+        chunks(0, x.shape[0], one)
+
+    def output_back():
+        def one(c):
+            dctx[:, c] = mm(da[...], co[c, :], NT).astype(BF)
+            gco[c, :] = mm(ctx[:, c], da[...], TN).astype(BF)
+        for k, (src, dst) in enumerate(moves):
+            pltpu.make_async_copy(src, dst, sems.at[k]).wait()
+        tiles(width, one)
+        leave(0).start()
+
+    def project_back(z):
+        def one(c):
+            gcp[z, :, c] = mm(x[...], dqkv[z, :, c], TN).astype(BF)
+            dx[:, c] = dx[:, c] + mm(dqkv[z], cp[z, c, :], NT)
+            if z != 1:
+                gcv[z // 2:z // 2 + 1, c] = total(dqkv[z, :, c].astype(F32))
+        tiles(width, one)
+        if z == 2:
+            leave(1).start()
+    out.append(norms)
+    out.append(output_back)
+    for pairs in halves_of(width // (2 * HEAD)):
+        out.append(functools.partial(attend_rows_back, qkv, dctx, p0, dqkv, a0, a1, w0, w1, items, group, pairs))
+    for pairs in halves_of(width // (2 * HEAD)):
+        out.append(functools.partial(attend_rows_back, qkv, dctx, p1, dqkv, a1, a0, w1, w0, items, group, pairs))
     for z in range(3):
-        def project_back(c, z=z):
-            gcp[z, :, c] = mm(x[...], dqkv[z, :, c], TN).astype(BF)
-            before = hidden[:, c] if z == 0 else dx[:, c]
-            dx[:, c] = before + mm(dqkv[z], cp[z, c, :], NT)
-        tiles(width, project_back)
-    leave(gcp, gcp_hbm)
-    for copy in outgoing:
-        copy.wait()
+        out.append(functools.partial(project_back, z))
+
+    def end():
+        for k in range(2):
+            leave(k).wait()
+    return out, end
+
+
+def open_ended(calls):
+    return [(frozenset(), call) for call in calls]
+
+
+SELF_PACE, CROSS_PACE = 3, 4
+CROSS_PARTS = tuple(p for p in PARTS if p[0] in (0, 1))
+SELF_PARTS = tuple(p for p in PARTS if p[0] in (2, 3))
+FEED_PARTS = tuple(p for p in PARTS if p[0] in (4, 5))
+
+
+def scatter_self_kernel(axes, spans, items, group, *refs):
+    ins, refs = refs[:11], refs[11:]
+    feed, refs = (refs[:2], refs[2:]) if axes else (None, refs)
+    outs, refs = refs[:5], refs[5:]
+    sums, refs = (refs[:2], refs[2:]) if axes else (None, refs)
+    calls, end = self_back_sections(spans, items, group, *ins, *outs, *refs[:9])
+    steps = []
+    if axes:
+        place = Place(axes)
+        place.barrier()
+        scatter = Scatter(place, FEED_PARTS, {4: feed[0], 5: feed[1]}, {4: sums[0], 5: sums[1]}, refs[9:])
+        steps = scatter.steps(range(len(FEED_PARTS)))
+    interleave(steps, open_ended(calls), SELF_PACE)
+    end()
+    if axes:
+        for p in range(len(FEED_PARTS)):
+            scatter.finish(p)
+
+
+def scatter_cross_kernel(axes, spans, items, group, *refs):
+    ins, refs = refs[:11], refs[11:]
+    if axes:
+        (gsp, gso, late), refs = refs[:3], refs[3:]
+    outs, refs = refs[:3], refs[3:]
+    if axes:
+        (scp, sco, ssp, sso, vectors), refs = refs[:5], refs[5:]
+    else:
+        gcv, refs = refs[0], refs[1:]
+    work, refs = refs[:9], refs[9:]
+    if axes:
+        (sums, landed, tsend, trecv), refs = refs[:4], refs[4:]
+        gcv, refs = refs[0], refs[1:]
+    calls, end = cross_back_sections(spans, items, group, *ins, *outs, gcv, *work)
+    if not axes:
+        interleave([], open_ended(calls), 0)
+        end()
+        return
+    place = Place(axes)
+    place.barrier()
+    parts = SELF_PARTS + CROSS_PARTS
+    scatter = Scatter(place, parts, {0: outs[1], 1: outs[2], 2: gsp, 3: gso}, {0: scp, 1: sco, 2: ssp, 3: sso}, refs)
+    count = len(SELF_PARTS)
+    interleave(scatter.steps(range(count)), open_ended(calls), CROSS_PACE)
+    end()
+    whole = Total(place, sums, landed, tsend, trecv)
+    rows = late.shape[0]
+    sums[0] = late[...]
+    sums[0, 0:5, :] = gcv[0:5, :]
+    more = scatter.steps(range(count, len(parts)))
+    whole.pass_on(0)
+    for k in range(4):
+        for step, _ in more[4 * k:4 * k + 4]:
+            step()
+        whole.take(k)
+    for step, _ in more[16:]:
+        step()
+    vectors[...] = sums[4]
+    for p in range(len(parts)):
+        scatter.finish(p)
 
 
 VMEM_LIMIT = 64 * 1024 * 1024 - 70000
@@ -871,35 +1026,53 @@
             pltpu.SemaphoreType.DMA((4,)), pltpu.SemaphoreType.DMA((4,))],
         compiler_params=params, name="feed",
     )(n2, cot, fu, fd, vec, ub)
-    dx, gcp, gco, gsp, gso, gcv, gcg, gsv, gsg = pl.pallas_call(
-        functools.partial(rear_kernel, spans, count, group),
-        out_shape=[rows_f] + [like(a.shape, BF) for a in (cp, co, sp, so)]
-        + [like(s, F32) for s in ((4, width), (1, width), (2, 4, width), (2, width))],
-        in_specs=[V] * 15 + [H] * 4 + [V], out_specs=[V] + [H] * 4 + [V] * 4,
-        scratch_shapes=[pltpu.VMEM(a.shape, BF) for a in (cp, co, sp, so) * 2] + [
-            pltpu.VMEM((total_rows, width), F32), pltpu.VMEM((total_rows, width), BF), pltpu.VMEM((total_rows, width), BF),
-            pltpu.VMEM((3, total_rows, width), BF), pltpu.SemaphoreType.DMA((4,)), pltpu.SemaphoreType.DMA((6,))],
-        compiler_params=params, name="rear",
-    )(x, *state, dy2, cp, co, sp, so, vec)
-    return out, dx, (gcp, gco, gsp, gso, gu, gd), (gcv, gcg, gsv, gsg, gub, gfv, gfg)
-
-
-def bundle(pieces, lead, granule):
-    flat = jnp.concatenate([p.reshape(lead + (-1,)) for p in pieces], axis=-1)
-    size = flat.shape[-1]
-    padded = -(-size // granule) * granule
-    flat = jnp.pad(flat, [(0, 0)] * len(lead) + [(0, padded - size)])
-    return flat.reshape(lead + (padded // 128, 128))
-
-
-def unbundle(array, lead, shapes):
-    flat = array.reshape(lead + (-1,))
-    out, at = [], 0
-    for s in shapes:
-        size = math.prod(s)
-        out.append(flat[..., at:at + size].reshape(lead + s))
-        at += size
-    return out
+    qkv, ctx, n1, i1, rb, qkv2, e, n2, i2, p0, p1, p2, p3 = state
+    comm = axes if kernels else None
+
+    def communicating(number):
+        if not kernels:
+            return params
+        return pltpu.CompilerParams(collective_id=number, has_side_effects=True, vmem_limit_bytes=VMEM_LIMIT)
+
+    def work(*weights):
+        return [pltpu.VMEM(a.shape, BF) for a in weights * 2] + [
+            pltpu.VMEM((total_rows, width), BF), pltpu.VMEM((total_rows, width), BF), pltpu.VMEM((3, total_rows, width), BF),
+            pltpu.SemaphoreType.DMA((2,)), pltpu.SemaphoreType.DMA((4,))]
+    shard_rows = {a: s.shape[-2:] for a, s in enumerate(shards)}
+    summed = [like(s.shape, F32) for s in shards]
+    results = pl.pallas_call(
+        functools.partial(scatter_self_kernel, comm, spans, count, group),
+        out_shape=[rows_f, like(sp.shape, BF), like(so.shape, BF), like((2, 4, width), F32), like((2, width), F32)]
+        + (summed[4:] if kernels else []),
+        in_specs=[V] * 9 + [H] * 2 + [H] * (2 if kernels else 0), out_specs=[V, H, H, V, V] + [V] * (2 if kernels else 0),
+        scratch_shapes=work(sp, so) + (scatter_scratch(axes, FEED_PARTS, shard_rows) if kernels else []),
+        compiler_params=communicating(1), name="scatter_self",
+    )(rb, qkv2, e, n2, i2, p2, p3, dy2, vec, sp, so, *((gu, gd) if kernels else ()))
+    dy1, gsp, gso, gsv, gsg = results[:5]
+    late = jnp.concatenate([jnp.zeros((SV, width), F32)] + [g.reshape(-1, width) for g in (gsv, gsg, gub, gfv, gfg)])
+    late = jnp.pad(late, [(0, small.shape[0] - late.shape[0]), (0, 0)])
+    if kernels:
+        feed_sums = results[5:]
+        parts = SELF_PARTS + CROSS_PARTS
+        results = pl.pallas_call(
+            functools.partial(scatter_cross_kernel, axes, spans, count, group),
+            out_shape=[rows_f, like(cp.shape, BF), like(co.shape, BF)] + summed[:4] + [like(late.shape, F32)],
+            in_specs=[V] * 9 + [H] * 2 + [H, H, V], out_specs=[V, H, H] + [V] * 5,
+            scratch_shapes=work(cp, co) + total_scratch(axes, late.shape) + [pltpu.VMEM((8, width), F32)]
+            + scatter_scratch(axes, parts, shard_rows),
+            compiler_params=communicating(2), name="scatter_cross",
+        )(x, qkv, ctx, n1, i1, p0, p1, dy1, vec, cp, co, gsp, gso, late)
+        return out, results[0], list(results[3:7]) + list(feed_sums), results[7]
+    dx, gcp, gco, gcv = pl.pallas_call(
+        functools.partial(scatter_cross_kernel, None, spans, count, group),
+        out_shape=[rows_f, like(cp.shape, BF), like(co.shape, BF), like((8, width), F32)],
+        in_specs=[V] * 9 + [H] * 2, out_specs=[V, H, H, V],
+        scratch_shapes=work(cp, co), compiler_params=params, name="cross_back",
+    )(x, qkv, ctx, n1, i1, p0, p1, dy1, vec, cp, co)
+    sums = [
+        lax.psum_scatter(g.astype(F32), "fsdp", scatter_dimension=g.ndim - 2, tiled=True) for g in (gcp, gco, gsp, gso, gu, gd)
+    ]
+    return out, dx, sums, lax.psum(late.at[:5].set(gcv[:5]), "fsdp")
 
 
 def spread(small, n, rows):
@@ -911,14 +1084,6 @@
     width = placed[1].shape[-1]
     flat = jnp.concatenate([p.reshape(-1, width) for p in placed])
     return jnp.pad(flat, [(0, rows - flat.shape[0]), (0, 0)])
-
-
-def scatter_all(axes, kernels, grads):
-    if kernels:
-        return scatter_call(axes, grads, PARTS)
-    return [
-        lax.psum_scatter(g.astype(F32), "fsdp", scatter_dimension=g.ndim - 3, tiled=False) for g in grads
-    ]
 
 
 def per_device(
@@ -953,15 +1118,13 @@
     streams = (language.reshape(-1, width), vision.reshape(-1, width))
     cotangents = (language_cotangent, vision_cotangent)
     small = (cross_biases, cross_gain, self_biases, self_gain, feed_up_bias, feed_biases, feed_gain)
-    small_shapes = [s.shape for s in small]
-    granule = 1024 if kernels else 128
     big = [cross_project, cross_output, self_project, self_output, feed_up, feed_down]
     words, regions = language.shape[1], vision.shape[1]
     masked = [
         (c.astype(F32) * task_flags[:, s].astype(F32)[:, None, None]).astype(BF).reshape(-1, width)
         for s, c in enumerate(cotangents)
     ]
-    out, rows_grad, big_grads, small_grads = compute(
+    out, rows_grad, summed, vectors = compute(
         axes,
         kernels,
         jnp.concatenate(streams),
@@ -970,13 +1133,15 @@
         big,
         spread(small, n, vector_rows(width, feed_up.shape[-1])[2]),
     )
-    small_grads = [g.reshape(v.shape[:-1] + (-1,)) for g, v in zip(small_grads, small)]
-    small_grads = [
-        jnp.moveaxis(g.reshape(g.shape[:-1] + (n, g.shape[-1] // n)), -2, 0) for g in small_grads
-    ]
-    big_grads = [g.reshape(g.shape[:-2] + (n, g.shape[-2] // n, g.shape[-1])) for g in big_grads]
-    summed = scatter_all(axes, kernels, big_grads + [bundle(small_grads, (n,), granule).astype(BF)])
-    cb, cg, sb, sg, ub, fb, fg = unbundle(summed[6], (), small_shapes)
+    me = lax.axis_index("fsdp")
+    pieces, at = [], 0
+    for v in small:
+        whole = v.shape[:-1] + (n * v.shape[-1],)
+        rows = math.prod(whole) // width
+        whole = vectors[at:at + rows].reshape(whole)
+        pieces.append(lax.dynamic_slice_in_dim(whole, me * v.shape[-1], v.shape[-1], axis=v.ndim - 1))
+        at += rows
+    cb, cg, sb, sg, ub, fb, fg = pieces
     return (
         out[:item_count * words].reshape(language.shape),
         out[item_count * words:].reshape(vision.shape),

time: 519 us -> 464 us (0.89)
  Pallas kernels: 479 us -> 430 us
    pallas_call x2, Pallas kernels: 247 us -> 214 us  [the longest x1 109 us: compute(): pl.pallas_call(functools.partial(scatter_cross_kernel, axes, spans, count...]
    pallas_call x1, Pallas kernels: 192 us -> 175 us  [compute(): pl.pallas_call(functools.partial(gather_front_kernel, axes, spans, count,...]
where the time goes in v4:
time: 464 us; the launch traced here: 463 us
  Pallas kernels  430 us (93%)
  local copies, waits for them, and re-layouts  28.7 us (6%)
    pallas_call x1, Pallas kernels, compute(): pl.pallas_call(functools.partial(gather_front_kernel, axes, spans, count,...  175 us
    pallas_call x1, Pallas kernels, compute(): pl.pallas_call(functools.partial(scatter_cross_kernel, axes, spans, count...  109 us
    pallas_call x1, Pallas kernels, compute(): pl.pallas_call(functools.partial(scatter_self_kernel, comm, spans, count,...  105 us
    pallas_call x1, Pallas kernels, compute(): pl.pallas_call(functools.partial(feed_kernel, spans), out_shape=[rows_bf,...  40.3 us

profile of v4, /device:TPU:0, one launch (start us, length us, event | category | flops | bytes accessed | tf_op | source)
XLA Modules:
  0.0 463.5 jit_solution(9475951283687824167)
XLA Ops:
  0.7 0.8 dynamic_update_slice.24
  1.5 0.8 dynamic_update_slice.27
  2.4 0.8 dynamic_update_slice.22
  3.2 0.8 dynamic_update_slice.23
  4.0 0.8 dynamic_update_slice.25
  4.8 0.8 dynamic_update_slice.28
  5.6 0.8 dynamic_update_slice.26
  7.5 1.1 reshape.107
  8.6 1.8 pad_maximum_fusion.x.refs_0_
  10.4 175.4 %gather_front.1 = (bf16[3,768,768]{2,1,0:T(8,128)(2,1)}, bf16[768,768]{1,0:T(8,128)(2,1)}, bf16[2,3,768,768]{3,2,1,0:T(8,128)(2,1)}, bf16[2,768,768]{2,1,0:T(8,1...) custom-call(bf16[432,768]{1,0:T(8,128)(2,1)} %pad_maximum_fusion.x.r, ...), custom_call_target="tpu_custom_call" | custom-call | tf_op jit(solution)/shard_map/gather_front/pallas_call | solution.py:996
  185.8 0.8 slice.44
  187.3 1.2 multiply_convert_fusion
  188.7 0.9 pad_maximum_fusion.1.cot
  189.6 40.3 %feed.1 = (bf16[432,768]{1,0:T(8,128)(2,1)}, f32[432,768]{1,0:T(8,128)}, bf16[2,768,3072]{2,1,0:T(8,128)(2,1)}, bf16[2,3072,768]{2,1,0:T(8,128)(2,1)}, f32[2,307...) custom-call(f32[432,768]{1,0:T(8,128)} %get-tuple-element.57.n2.refs_3_, ...), custom_call_target="tpu_custom_call" | custom-call | tf_op jit(solution)/shard_map/feed/pallas_call | solution.py:1018
  230.0 105.1 %scatter_self.1 = (f32[432,768]{1,0:T(8,128)}, bf16[2,3,768,768]{3,2,1,0:T(8,128)(2,1)}, bf16[2,768,768]{2,1,0:T(8,128)(2,1)}, f32[2,4,768]{2,1,0:T(4,128)}, f32...) custom-call(bf16[432,768]{1,0:T(8,128)(2,1)} %get-tuple-element.68.refs_0_, ...), custom_call_target="tpu_custom_call" | custom-call | tf_op jit(solution)/shard_map/scatter_self/pallas_call | solution.py:1043
  335.0 0.8 reshape.118
  335.8 0.8 reshape.119
  336.5 0.7 reshape.120
  337.3 1.7 concatenate.15
  339.7 109.0 %scatter_cross.1 = (f32[432,768]{1,0:T(8,128)}, bf16[3,768,768]{2,1,0:T(8,128)(2,1)}, bf16[768,768]{1,0:T(8,128)(2,1)}, f32[3,24,768]{2,1,0:T(8,128)}, f32[24,76...) custom-call(bf16[432,768]{1,0:T(8,128)(2,1)} %pad_maximum_fusion.x.refs_0_, ...), custom_call_target="tpu_custom_call" | custom-call | tf_op jit(solution)/shard_map/scatter_cross/pallas_call | solution.py:1057
  448.7 0.8 fusion.1
  450.1 1.2 slice.47
  451.3 1.0 reshape.121
  452.2 1.9 slice.48
  454.2 0.7 constant_dynamic-slice_fusion.4
  457.5 0.8 reshape.116
  458.3 0.7 slice.46
  459.1 0.7 copy.49
  460.4 0.8 copy.51
  461.2 0.7 copy.52
  461.8 0.8 copy.53
  462.7 0.8 copy.54
  (51 shorter events, 6.5 us)
Async XLA Ops:
  8.6 178.7 %copy-start.9 = (s32[12,2]{0,1:T(2,128)S(1)}, s32[12,2]{0,1:T(2,128)}, u32[]{:S(2)}) copy-start(s32[12,2]{0,1:T(2,128)} %param.35) | copy-start | bytes 292
  185.8 2.7 copy-start.4
  451.2 2.9 copy-start.7
  451.2 6.2 %copy-start = (bf16[432,768]{1,0:T(8,128)(2,1)S(1)}, bf16[432,768]{1,0:T(8,128)(2,1)}, u32[]{:S(2)}) copy-start(bf16[432,768]{1,0:T(8,128)(2,1)} %get-tuple-element.61) | copy-start | bytes 1990660
  454.2 4.9 %copy-start.5 = (f32[3,24,768]{2,1,0:T(8,128)S(1)}, f32[3,24,768]{2,1,0:T(8,128)}, u32[]{:S(2)}) copy-start(f32[3,24,768]{2,1,0:T(8,128)} %get-tuple-element.128) | copy-start | bytes 663556
  454.2 5.6 %copy-start.8 = (f32[24,768]{1,0:T(8,128)S(1)}, f32[24,768]{1,0:T(8,128)}, u32[]{:S(2)}) copy-start(f32[24,768]{1,0:T(8,128)} %get-tuple-element.129) | copy-start | bytes 221188
  454.2 6.2 %copy-start.3 = (f32[2,3,24,768]{3,2,1,0:T(8,128)S(1)}, f32[2,3,24,768]{3,2,1,0:T(8,128)}, u32[]{:S(2)}) copy-start(f32[2,3,24,768]{3,2,1,0:T(8,128)} %get-tuple-element.132) | copy-start | bytes 1327108
  457.5 3.7 copy-start.6
  457.5 4.3 copy-start.2
  459.1 3.6 copy-start.1

commit v5 on v4

--- a/solution.py
+++ b/solution.py
@@ -214,7 +214,7 @@
             self.shared(p, stage).wait_send()
 
     def steps(self):
-        count, ahead = len(PARTS), 5
+        count, ahead = len(PARTS), 3
         out = [(functools.partial(self.begin, p), None) for p in range(ahead)]
         for t in range(count + 2 * LAG + 2):
             if t + ahead < count:
@@ -694,7 +694,7 @@
 
 
 def feed_kernel(spans, n2, cot, fu_hbm, fd_hbm, vec, ub,
-                out, dy2, gu_hbm, gd_hbm, gub, gfv, gfg, fu, fd, gu, gd, yb, act, slope, du, dz, hidden, sems, osems):
+                out0, out1, dy2, gu_hbm, gd_hbm, gub, gfv, gfg, fu, fd, gu, gd, yb, act, slope, du, dz, hidden, sems, osems):
     streams = range(2)
     waits = load([(fu_hbm.at[0], fu.at[0]), (fd_hbm.at[0], fd.at[0]), (fu_hbm.at[1], fu.at[1]), (fd_hbm.at[1], fd.at[1])], sems)
     width, inner = fu.shape[1], fu.shape[2]
@@ -733,7 +733,7 @@
             r = pl.ds(pl.multiple_of(j * 48, 16), 48)
             g = pl.ds(pl.multiple_of(at + j * 48, 16), 48)
             n, inverse = normed_rows(hidden[r, :])
-            out[g, :] = (n * vec[FG + s:FG + s + 1, :] + vec[FV + 2 * s + 1:FV + 2 * s + 2, :]).astype(BF)
+            (out0, out1)[s][r, :] = (n * vec[FG + s:FG + s + 1, :] + vec[FV + 2 * s + 1:FV + 2 * s + 2, :]).astype(BF)
             upstream = cot[g, :].astype(F32)
             dh = norm_rows_back(upstream, n, inverse, vec[FG + s:FG + s + 1, :])
             hidden[r, :] = dh
@@ -1015,11 +1015,11 @@
     most = max(m for _, m, _ in spans)
     n2 = state[7]
     ub = vec[UB:UB + 2 * (inner // width)].reshape(2, inner)
-    out, dy2, gu, gd, gub, gfv, gfg = pl.pallas_call(
+    out0, out1, dy2, gu, gd, gub, gfv, gfg = pl.pallas_call(
         functools.partial(feed_kernel, spans),
-        out_shape=[rows_bf, rows_f, like(fu.shape, BF), like(fd.shape, BF), like(ub.shape, F32),
+        out_shape=[like((spans[0][1], width), BF), like((spans[1][1], width), BF), rows_f, like(fu.shape, BF), like(fd.shape, BF), like(ub.shape, F32),
                    like((2, 2, width), F32), like((2, width), F32)],
-        in_specs=[V, V, H, H, V, V], out_specs=[V, V, H, H, V, V, V],
+        in_specs=[V, V, H, H, V, V], out_specs=[V, V, V, H, H, V, V, V],
         scratch_shapes=[pltpu.VMEM(a.shape, BF) for a in (fu, fd, fu, fd)] + [
             pltpu.VMEM((most, width), BF), pltpu.VMEM((most, inner), BF), pltpu.VMEM((most, inner), F32),
             pltpu.VMEM((most, inner), BF), pltpu.VMEM((most, width), BF), pltpu.VMEM((most, width), F32),
@@ -1062,7 +1062,7 @@
             + scatter_scratch(axes, parts, shard_rows),
             compiler_params=communicating(2), name="scatter_cross",
         )(x, qkv, ctx, n1, i1, p0, p1, dy1, vec, cp, co, gsp, gso, late)
-        return out, results[0], list(results[3:7]) + list(feed_sums), results[7]
+        return (out0, out1), results[0], list(results[3:7]) + list(feed_sums), results[7]
     dx, gcp, gco, gcv = pl.pallas_call(
         functools.partial(scatter_cross_kernel, None, spans, count, group),
         out_shape=[rows_f, like(cp.shape, BF), like(co.shape, BF), like((8, width), F32)],
@@ -1072,7 +1072,7 @@
     sums = [
         lax.psum_scatter(g.astype(F32), "fsdp", scatter_dimension=g.ndim - 2, tiled=True) for g in (gcp, gco, gsp, gso, gu, gd)
     ]
-    return out, dx, sums, lax.psum(late.at[:5].set(gcv[:5]), "fsdp")
+    return (out0, out1), dx, sums, lax.psum(late.at[:5].set(gcv[:5]), "fsdp")
 
 
 def spread(small, n, rows):
@@ -1143,8 +1143,8 @@
         at += rows
     cb, cg, sb, sg, ub, fb, fg = pieces
     return (
-        out[:item_count * words].reshape(language.shape),
-        out[item_count * words:].reshape(vision.shape),
+        out[0].reshape(language.shape),
+        out[1].reshape(vision.shape),
         rows_grad[:item_count * words].reshape(language.shape),
         rows_grad[item_count * words:].reshape(vision.shape),
         summed[0],

time: 464 us -> 463 us (level)
  no operation moved by 1% of the time
where the time goes in v5:
time: 463 us; the launch traced here: 462 us
  Pallas kernels  429 us (93%)
  local copies, waits for them, and re-layouts  28 us (6%)
    pallas_call x1, Pallas kernels, compute(): pl.pallas_call(functools.partial(gather_front_kernel, axes, spans, count,...  172 us
    pallas_call x1, Pallas kernels, compute(): pl.pallas_call(functools.partial(scatter_cross_kernel, axes, spans, count...  110 us
    pallas_call x1, Pallas kernels, compute(): pl.pallas_call(functools.partial(scatter_self_kernel, comm, spans, count,...  107 us
    pallas_call x1, Pallas kernels, compute(): pl.pallas_call(functools.partial(feed_kernel, spans), out_shape=[like((sp...  40.3 us

profile of v5, /device:TPU:0, one launch (start us, length us, event | category | flops | bytes accessed | tf_op | source)
XLA Modules:
  0.0 461.6 jit_solution(11106446144539715605)
XLA Ops:
  0.7 0.8 dynamic_update_slice.24
  1.5 0.8 dynamic_update_slice.27
  2.4 0.8 dynamic_update_slice.22
  3.2 0.8 dynamic_update_slice.23
  4.0 0.8 dynamic_update_slice.25
  4.8 0.8 dynamic_update_slice.28
  5.6 0.8 dynamic_update_slice.26
  7.5 1.1 reshape.107
  8.6 1.8 pad_maximum_fusion.x.refs_0_
  10.4 171.8 %gather_front.1 = (bf16[3,768,768]{2,1,0:T(8,128)(2,1)}, bf16[768,768]{1,0:T(8,128)(2,1)}, bf16[2,3,768,768]{3,2,1,0:T(8,128)(2,1)}, bf16[2,768,768]{2,1,0:T(8,1...) custom-call(bf16[432,768]{1,0:T(8,128)(2,1)} %pad_maximum_fusion.x.r, ...), custom_call_target="tpu_custom_call" | custom-call | tf_op jit(solution)/shard_map/gather_front/pallas_call | solution.py:996
  182.3 0.8 slice.38
  183.8 1.2 multiply_convert_fusion
  185.2 0.9 pad_maximum_fusion.1.cot
  186.0 40.3 %feed.1 = (bf16[240,768]{1,0:T(8,128)(2,1)}, bf16[192,768]{1,0:T(8,128)(2,1)}, f32[432,768]{1,0:T(8,128)}, bf16[2,768,3072]{2,1,0:T(8,128)(2,1)}, bf16[2,3072,76...) custom-call(f32[432,768]{1,0:T(8,128)} %get-tuple-element.58.n2.refs_3_, ...), custom_call_target="tpu_custom_call" | custom-call | tf_op jit(solution)/shard_map/feed/pallas_call | solution.py:1018
  226.4 106.8 %scatter_self.1 = (f32[432,768]{1,0:T(8,128)}, bf16[2,3,768,768]{3,2,1,0:T(8,128)(2,1)}, bf16[2,768,768]{2,1,0:T(8,128)(2,1)}, f32[2,4,768]{2,1,0:T(4,128)}, f32...) custom-call(bf16[432,768]{1,0:T(8,128)(2,1)} %get-tuple-element.70.refs_0_, ...), custom_call_target="tpu_custom_call" | custom-call | tf_op jit(solution)/shard_map/scatter_self/pallas_call | solution.py:1043
  333.1 0.8 reshape.118
  333.9 0.8 reshape.119
  334.6 0.7 reshape.120
  335.4 1.7 concatenate.15
  337.8 109.8 %scatter_cross.1 = (f32[432,768]{1,0:T(8,128)}, bf16[3,768,768]{2,1,0:T(8,128)(2,1)}, bf16[768,768]{1,0:T(8,128)(2,1)}, f32[3,24,768]{2,1,0:T(8,128)}, f32[24,76...) custom-call(bf16[432,768]{1,0:T(8,128)(2,1)} %pad_maximum_fusion.x.refs_0_, ...), custom_call_target="tpu_custom_call" | custom-call | tf_op jit(solution)/shard_map/scatter_cross/pallas_call | solution.py:1057
  447.5 0.8 fusion.1
  448.9 1.2 slice.39
  450.1 1.0 reshape.121
  451.1 2.0 slice.40
  453.1 0.7 constant_dynamic-slice_fusion.4
  454.5 0.7 constant_dynamic-slice_fusion.1
  456.4 0.8 reshape.116
  457.2 0.7 copy.49
  458.6 0.8 copy.51
  459.3 0.7 copy.52
  460.0 0.8 copy.53
  460.8 0.8 copy.54
  (49 shorter events, 5.9 us)
Async XLA Ops:
  8.6 175.2 %copy-start.9 = (s32[12,2]{0,1:T(2,128)S(1)}, s32[12,2]{0,1:T(2,128)}, u32[]{:S(2)}) copy-start(s32[12,2]{0,1:T(2,128)} %param.35) | copy-start | bytes 292
  182.3 2.7 copy-start.4
  450.1 3.0 copy-start.7
  450.1 6.3 %copy-start.3 = (bf16[240,768]{1,0:T(8,128)(2,1)S(1)}, bf16[240,768]{1,0:T(8,128)(2,1)}, u32[]{:S(2)}) copy-start(bf16[240,768]{1,0:T(8,128)(2,1)} %get-tuple-element.62) | copy-start | bytes 1105924
  451.1 6.1 %copy-start.5 = (f32[3,24,768]{2,1,0:T(8,128)S(1)}, f32[3,24,768]{2,1,0:T(8,128)}, u32[]{:S(2)}) copy-start(f32[3,24,768]{2,1,0:T(8,128)} %get-tuple-element.130) | copy-start | bytes 663556
  451.1 6.8 %copy-start.8 = (f32[24,768]{1,0:T(8,128)S(1)}, f32[24,768]{1,0:T(8,128)}, u32[]{:S(2)}) copy-start(f32[24,768]{1,0:T(8,128)} %get-tuple-element.131) | copy-start | bytes 221188
  451.1 7.5 %copy-start.2 = (f32[2,3,24,768]{3,2,1,0:T(8,128)S(1)}, f32[2,3,24,768]{3,2,1,0:T(8,128)}, u32[]{:S(2)}) copy-start(f32[2,3,24,768]{3,2,1,0:T(8,128)} %get-tuple-element.134) | copy-start | bytes 1327108
  453.1 6.2 %copy-start.6 = (f32[2,24,768]{2,1,0:T(8,128)S(1)}, f32[2,24,768]{2,1,0:T(8,128)}, u32[]{:S(2)}) copy-start(f32[2,24,768]{2,1,0:T(8,128)} %get-tuple-element.135) | copy-start | bytes 442372
  453.1 6.9 %copy-start.1 = (f32[2,24,3072]{2,1,0:T(8,128)S(1)}, f32[2,24,3072]{2,1,0:T(8,128)}, u32[]{:S(2)}) copy-start(f32[2,24,3072]{2,1,0:T(8,128)} %get-tuple-element.138) | copy-start | bytes 1769476
  457.2 3.6 copy-start
